TPU v7x, 32 devices: a whole 2x2x4 slice. The times are simulated.
32 devices in a mesh: mem: 8 (over z, x), head: 4 (over y, core).
Axes of the slice: x: 2, y: 2, z: 4, core: 2. Of those that a mesh axis runs over, the one named last changes fastest.
Arguments:
- queries: bfloat16 [128, 32, 128], P('mem', 'head'), may hold values from -170 to 170
- cache_blocks: bfloat16 [256, 2, 8, 64, 128], P('mem', None, 'head'), may hold values from -9 to 9
- selected: int32 [128, 32], P('mem'), may hold values from 0 to 255, as said below
- counts: int32 [16, 256], P(None, 'mem'), may hold values from 0 to 8
- output_weight: bfloat16 [4096, 4096], P('head'), may hold values from -0.09375 to 0.09375
Outputs:
- layer_out: bfloat16 [128, 4096], P('mem', 'head')
- block_heat: float32 [256], P('mem')
Inputs may be any that keep to these rules, and one draw needn't show every extreme that they name: `selected`: each request names 32 different blocks; at most 8 of a request's blocks b share the same b // 32.
All inputs are finite; a program needn't handle non-finite values.
Results may differ from a plain program's by a relative error of at most 0.012.
Values may be sent and summed in bfloat16 or wider, within the bound.
No kernel may reach another device: no remote copies, remote signals or barrier semaphores. Data moves between devices by JAX's collectives and lax.ppermute only.
A program may use at most 128 MiB of HBM per device.

v0:
```python
import functools
import math

import jax
import jax.numpy as jnp
from jax import lax
from jax.experimental import pallas as pl
from jax.experimental.pallas import tpu as pltpu
from jax.sharding import PartitionSpec as P


MASKED = -1e30
LANES = 128


def exchange(value, axis, step):
    count = lax.axis_size(axis)
    return lax.ppermute(value, axis, [(i, i ^ step) for i in range(count)])


def payload_kernel(queries_hbm, selected_hbm, out_ref, queries_ref, selected_ref, sems):
    copies = [
        pltpu.make_async_copy(selected_hbm, selected_ref, sems.at[0]),
        pltpu.make_async_copy(queries_hbm, queries_ref, sems.at[1]),
    ]
    for copy in copies:
        copy.start()
    rows, heads, depth = queries_ref.shape
    width = heads * depth
    block = lax.broadcasted_iota(jnp.int32, (rows, out_ref.shape[1] - width), 1)
    marks = jnp.zeros(block.shape, jnp.float32)
    copies[0].wait()
    chosen = selected_ref[...]
    for i in range(chosen.shape[1]):
        marks = jnp.where(block == chosen[:, i : i + 1], 1.0, marks)
    out_ref[:, width:] = marks.astype(jnp.bfloat16)
    copies[1].wait()
    for h in range(heads):
        out_ref[:, h * depth : (h + 1) * depth] = queries_ref[:, h, :]


def stage_kernel(source_hbm, _, out_ref, sem):
    copy = pltpu.make_async_copy(source_hbm, out_ref, sem)
    copy.start()
    copy.wait()


def attend_kernel(own_ref, near_ref, straight_ref, forwarded_ref, cache_ref, *refs, heads):
    messages = refs[:-1]
    hits_ref = refs[-1]
    blocks, _, heads_kv, tokens, depth = cache_ref.shape
    width = heads * depth
    rows_each = own_ref.shape[0]
    all_blocks = own_ref.shape[1] - width
    group_q = heads // heads_kv
    scale = depth**-0.5 * math.log2(math.e)
    payloads = [own_ref, near_ref]
    payloads += [straight_ref.at[i] for i in range(straight_ref.shape[0])]
    payloads += [forwarded_ref.at[i] for i in range(forwarded_ref.shape[0])]
    first = lax.axis_index("mem") * blocks
    column = lax.broadcasted_iota(jnp.int32, (all_blocks, LANES), 1)
    pick = (lax.broadcasted_iota(jnp.int32, (all_blocks, LANES), 0) == column + first) & (
        column < blocks
    )
    pick = pick.astype(jnp.float32).astype(jnp.bfloat16)
    span = blocks * tokens
    fence = jnp.where(
        lax.broadcasted_iota(jnp.int32, (span, LANES), 0) // tokens
        == lax.broadcasted_iota(jnp.int32, (span, LANES), 1),
        MASKED,
        0.0,
    ).astype(jnp.bfloat16)
    hits = jnp.zeros((1, LANES), jnp.float32)
    batch = min(len(payloads), 8)
    pair = math.gcd(group_q, 2)
    rows = batch * rows_each
    lane = lax.broadcasted_iota(jnp.int32, (rows, LANES), 1)
    for start in range(0, len(payloads), batch):
        part = payloads[start : start + batch]
        marks = jnp.concatenate([p[:, width:] for p in part], axis=0)
        chosen = jnp.dot(marks, pick, preferred_element_type=jnp.float32)
        hits = hits + jnp.sum(chosen, axis=0, keepdims=True)
        blocked = (1.0 - chosen).astype(jnp.bfloat16)
        stats = jnp.zeros((rows, LANES), jnp.float32)
        for kv in range(heads_kv):
            keys = cache_ref[:, 0, kv].reshape(span, depth)
            keys = jnp.concatenate([keys, fence], axis=1)
            values = cache_ref[:, 1, kv].reshape(span, depth)
            values = jnp.concatenate([values, jnp.ones((span, LANES), jnp.bfloat16)], axis=1)
            for first_head in range(kv * group_q, (kv + 1) * group_q, pair):
                query = jnp.concatenate(
                    [
                        jnp.concatenate(
                            [
                                jnp.concatenate(
                                    [p[:, h * depth : (h + 1) * depth] for p in part], axis=0
                                ),
                                blocked,
                            ],
                            axis=1,
                        )
                        for h in range(first_head, first_head + pair)
                    ],
                    axis=0,
                )
                scores = lax.dot_general(
                    query, keys, (((1,), (1,)), ((), ())), preferred_element_type=jnp.float32
                )
                peak = jnp.max(scores, axis=1, keepdims=True)
                weights = jnp.exp2((scores - peak) * scale).astype(jnp.bfloat16)
                sums = jnp.dot(weights, values, preferred_element_type=jnp.float32)
                out = sums[:, :depth].astype(jnp.bfloat16)
                total = sums[:, depth : depth + 1]
                for j in range(pair):
                    h = first_head + j
                    for i in range(batch):
                        at = j * rows + i * rows_each
                        messages[start + i][:, h * depth : (h + 1) * depth] = out[
                            at : at + rows_each
                        ]
                    stats = jnp.where(lane == h, peak[j * rows : (j + 1) * rows], stats)
                    stats = jnp.where(lane == heads + h, total[j * rows : (j + 1) * rows], stats)
        high = stats.astype(jnp.bfloat16).astype(jnp.float32)
        rest = stats - high
        middle = rest.astype(jnp.bfloat16).astype(jnp.float32)
        low = rest - middle
        packed = (
            high + pltpu.roll(middle, 2 * heads, 1) + pltpu.roll(low, 4 * heads, 1)
        ).astype(jnp.bfloat16)
        for i in range(batch):
            messages[start + i][:, width:] = packed[i * rows_each : (i + 1) * rows_each]
    hits_ref[...] = hits


def project_kernel(*refs, sources, heads):
    messages = refs[:sources]
    weight_ref = refs[sources]
    outs = refs[sources + 1 :]
    me = lax.axis_index("head")
    rows = messages[0].shape[0]
    width = weight_ref.shape[0]
    depth = width // heads
    scale = depth**-0.5 * math.log2(math.e)
    stats = []
    for m in messages:
        packed = m[:, width:].astype(jnp.float32)
        stats.append(
            packed
            + pltpu.roll(packed, LANES - 2 * heads, 1)
            + pltpu.roll(packed, LANES - 4 * heads, 1)
        )
    lane = lax.broadcasted_iota(jnp.int32, (rows, LANES), 1)
    highest = functools.reduce(jnp.maximum, stats)
    factors = [jnp.where(lane < heads, jnp.exp2((s - highest) * scale), 0.0) for s in stats]
    total = sum(f * pltpu.roll(s, LANES - heads, 1) for f, s in zip(factors, stats))
    inverse = 1.0 / jnp.where(lane < heads, total, 1.0)
    factors = [f * inverse for f in factors]
    attended = []
    for h in range(heads):
        acc = None
        for f, m in zip(factors, messages):
            term = f[:, h : h + 1] * m[:, h * depth : (h + 1) * depth].astype(jnp.float32)
            acc = term if acc is None else acc + term
        attended.append(acc.astype(jnp.bfloat16))
    attended = jnp.concatenate(attended, axis=1)
    columns = weight_ref.shape[1] // len(outs)
    for i, out in enumerate(outs):
        at = pl.multiple_of((me ^ i) * columns, columns)
        out[...] = jnp.dot(
            attended, weight_ref[:, pl.ds(at, columns)], preferred_element_type=jnp.float32
        ).astype(jnp.bfloat16)


def per_device(queries, cache_blocks, selected, counts, output_weight):
    devices_mem = lax.axis_size("mem")
    devices_head = lax.axis_size("head")
    rows, heads, depth = queries.shape
    blocks = cache_blocks.shape[0]
    width = heads * depth
    all_blocks = devices_mem * blocks
    vmem = pl.BlockSpec(memory_space=pltpu.VMEM)
    hbm = pl.BlockSpec(memory_space=pltpu.HBM)
    keep = functools.partial(pltpu.with_memory_space_constraint, memory_space=pltpu.HBM)
    payload = pl.pallas_call(
        payload_kernel,
        in_specs=[hbm] * 2,
        out_specs=vmem,
        out_shape=jax.ShapeDtypeStruct((rows, width + all_blocks), jnp.bfloat16),
        scratch_shapes=[
            pltpu.VMEM(queries.shape, queries.dtype),
            pltpu.VMEM(selected.shape, selected.dtype),
            pltpu.SemaphoreType.DMA((2,)),
        ],
        compiler_params=pltpu.CompilerParams(vmem_limit_bytes=4 * 2**20),
        name="payload",
    )(keep(queries), keep(selected))

    def stage(array, after):
        return pl.pallas_call(
            stage_kernel,
            in_specs=[hbm, vmem],
            out_specs=vmem,
            out_shape=jax.ShapeDtypeStruct(array.shape, array.dtype),
            scratch_shapes=[pltpu.SemaphoreType.DMA(())],
            compiler_params=pltpu.CompilerParams(vmem_limit_bytes=4 * 2**20),
        )(keep(array), after)

    even = list(range(devices_mem - 2, 0, -2))
    straight = jnp.stack([exchange(payload, "mem", k) for k in even])
    near = exchange(payload, "mem", 1)
    cache_blocks = stage(cache_blocks, payload)
    forwarded = exchange(straight, "mem", 1)
    output_weight = stage(output_weight, straight)
    steps = [0, 1] + even + [k ^ 1 for k in even]
    message_shape = jax.ShapeDtypeStruct((rows, width + LANES), jnp.bfloat16)
    *messages, hits = pl.pallas_call(
        functools.partial(attend_kernel, heads=heads),
        in_specs=[vmem] * 5,
        out_specs=[vmem] * (devices_mem + 1),
        out_shape=[message_shape] * devices_mem + [jax.ShapeDtypeStruct((1, LANES), jnp.float32)],
        compiler_params=pltpu.CompilerParams(vmem_limit_bytes=32 * 2**20),
        name="attend",
    )(payload, near, straight, forwarded, cache_blocks)
    returned = [m if k == 0 else exchange(m, "mem", k) for k, m in zip(steps, messages)]
    columns = output_weight.shape[1] // devices_head
    shares = pl.pallas_call(
        functools.partial(project_kernel, sources=devices_mem, heads=heads),
        in_specs=[vmem] * (devices_mem + 1),
        out_specs=[vmem] * devices_head,
        out_shape=[jax.ShapeDtypeStruct((rows, columns), jnp.bfloat16)] * devices_head,
        compiler_params=pltpu.CompilerParams(vmem_limit_bytes=24 * 2**20),
        name="project",
    )(*returned, output_weight)
    arrived = {k: exchange(shares[k], "head", k) for k in range(devices_head - 1, 0, -1)}
    layer_out = shares[0].astype(jnp.float32)
    for k in range(1, devices_head):
        layer_out = layer_out + arrived[k].astype(jnp.float32)
    decays = 0.5 ** jnp.arange(counts.shape[0], dtype=jnp.float32)
    block_heat = jnp.sum(decays[:, None] * counts.astype(jnp.float32), axis=0) + hits[0, :blocks]
    return (layer_out.astype(jnp.bfloat16), block_heat)


def solution(mesh):
    return jax.shard_map(
        per_device,
        mesh=mesh,
        in_specs=(
            P("mem", "head", None),
            P("mem", None, "head", None, None),
            P("mem", None),
            P(None, "mem"),
            P("head", None),
        ),
        out_specs=(P("mem", "head"), P("mem")),
        check_vma=False,
    )
```

profile of v0, /device:TPU:0, one launch (start us, length us, event | category | flops | bytes accessed | tf_op | source)
XLA Modules:
  0.0 44.6 jit_solution(3903516095442364713)
XLA Ops:
  0.6 0.9 %payload.1._.own_ref = bf16[16,1280]{1,0:T(8,128)(2,1)S(1)} custom-call(bf16[16,8,128]{2,1,0:T(8,128)(2,1)} %queries_hbm.1, s32[16,32]{1,0:T(8,128)} %selected_hbm.1), custom_call_target="tpu_custom_call" | custom-call | tf_op jit(solution)/shard_map/payload/pallas_call | solution.py:184
  1.6 3.1 %collective-permute-start.3 = (bf16[16,1280]{1,0:T(8,128)(2,1)S(1)}, bf16[16,1280]{1,0:T(8,128)(2,1)S(1)}, u32[]{:S(2)}, u32[]{:S(2)}) collective-permute-start(bf16[16,1280]{1,0:T(8,128)(2,1)S(1)} %payload.1._.own_ref), channel_id=1, source_target_pairs={{0,8},{4,12},{8,0},{12,4},{16,24},{20,28},{24,16},{28,20},{1,9},{5... | collective-permute-start | bytes 122888 | tf_op jit(solution)/shard_map/ppermute | solution.py:18
  4.7 2.6 %collective-permute-start.2 = (bf16[16,1280]{1,0:T(8,128)(2,1)S(1)}, bf16[16,1280]{1,0:T(8,128)(2,1)S(1)}, u32[]{:S(2)}, u32[]{:S(2)}) collective-permute-start(bf16[16,1280]{1,0:T(8,128)(2,1)S(1)} %payload.1._.own_ref), channel_id=1, source_target_pairs={{0,16},{4,20},{8,24},{12,28},{16,0},{20,4},{24,8},{28,12},{1,17},{... | collective-permute-start | bytes 122888 | tf_op jit(solution)/shard_map/ppermute | solution.py:18
  7.3 0.0 collective-permute-start.1
  7.3 0.0 collective-permute-done.3
  7.3 3.1 %collective-permute-done.2 = bf16[16,1280]{1,0:T(8,128)(2,1)S(1)} collective-permute-done((bf16[16,1280]{1,0:T(8,128)(2,1)S(1)}, bf16[16,1280]{1,0:T(8,128)(2,1)S(1)}, u32[]{:S(2)}, u32[]{:S(2)}) %collective-permute-start.2) | collective-permute-done | bytes 40992 | tf_op jit(solution)/shard_map/ppermute | solution.py:18
  10.3 2.7 %collective-permute-done.1 = bf16[16,1280]{1,0:T(8,128)(2,1)S(1)} collective-permute-done((bf16[16,1280]{1,0:T(8,128)(2,1)S(1)}, bf16[16,1280]{1,0:T(8,128)(2,1)S(1)}, u32[]{:S(2)}, u32[]{:S(2)}) %collective-permute-start.1) | collective-permute-done | bytes 40992 | tf_op jit(solution)/shard_map/ppermute | solution.py:18
  13.1 1.6 %collective-permute-start.4 = (bf16[3,16,1280]{2,1,0:T(8,128)(2,1)S(1)}, bf16[3,16,1280]{2,1,0:T(8,128)(2,1)S(1)}, u32[]{:S(2)}, u32[]{:S(2)}) collective-permute-start(bf16[3,16,1280]{2,1,0:T(8,128)(2,1)S(1)} %pad_maximum_fusion.straight_ref._), channel_id=1, source_target_pairs={{0,4},{4,0},{8,12},{12,8},{16,20},{20,16},{24,28},{28,24},{1,5},{5... | collective-permute-start | bytes 368648 | tf_op jit(solution)/shard_map/ppermute | solution.py:18
  14.7 0.5 %collective-permute-start = (bf16[16,1280]{1,0:T(8,128)(2,1)S(1)}, bf16[16,1280]{1,0:T(8,128)(2,1)S(1)}, u32[]{:S(2)}, u32[]{:S(2)}) collective-permute-start(bf16[16,1280]{1,0:T(8,128)(2,1)S(1)} %payload.1._.own_ref), channel_id=1, source_target_pairs={{0,4},{4,0},{8,12},{12,8},{16,20},{20,16},{24,28},{28,24},{1,5},{5... | collective-permute-start | bytes 122888 | tf_op jit(solution)/shard_map/ppermute | solution.py:18
  15.2 1.6 %shard_map.68.cache_ref = bf16[32,2,2,64,128]{4,3,2,1,0:T(8,128)(2,1)S(1)} custom-call(bf16[32,2,2,64,128]{4,3,2,1,0:T(8,128)(2,1)} %source_hbm.2, bf16[16,1280]{1,0:T(8,128)(2,1)S(1)} %payload.1._.own_ref), custom_call_target="tpu_custom_call" | custom-call | tf_op jit(solution)/shard_map/pallas_call | solution.py:199
  16.8 1.9 %collective-permute-done.near_ref = bf16[16,1280]{1,0:T(8,128)(2,1)S(1)} collective-permute-done((bf16[16,1280]{1,0:T(8,128)(2,1)S(1)}, bf16[16,1280]{1,0:T(8,128)(2,1)S(1)}, u32[]{:S(2)}, u32[]{:S(2)}) %collective-permute-start) | collective-permute-done | bytes 40992 | tf_op jit(solution)/shard_map/ppermute | solution.py:18
  18.7 0.0 collective-permute-done.4.forwarded_ref
  18.7 3.5 %attend.1 = (bf16[16,1152]{1,0:T(8,128)(2,1)S(1)}, bf16[16,1152]{1,0:T(8,128)(2,1)S(1)}, bf16[16,1152]{1,0:T(8,128)(2,1)S(1)}, bf16[16,1152]{1,0:T(8,128)(2,1)S(...) custom-call(bf16[16,1280]{1,0:T(8,128)(2,1)S(1)} %payload.1._.own_re, ...), custom_call_target="tpu_custom_call" | custom-call | tf_op jit(solution)/shard_map/attend/pallas_call | solution.py:216
  22.1 1.4 %collective-permute-start.5 = (bf16[16,1152]{1,0:T(8,128)(2,1)S(1)}, bf16[16,1152]{1,0:T(8,128)(2,1)S(1)}, u32[]{:S(2)}, u32[]{:S(2)}) collective-permute-start(bf16[16,1152]{1,0:T(8,128)(2,1)S(1)} %get-tuple-element.16), channel_id=1, source_target_pairs={{0,4},{4,0},{8,12},{12,8},{16,20},{20,16},{24,28},{28,24},{1,5},{5... | collective-permute-start | bytes 110600 | tf_op jit(solution)/shard_map/ppermute | solution.py:18
  23.5 0.5 %collective-permute-start.6 = (bf16[16,1152]{1,0:T(8,128)(2,1)S(1)}, bf16[16,1152]{1,0:T(8,128)(2,1)S(1)}, u32[]{:S(2)}, u32[]{:S(2)}) collective-permute-start(bf16[16,1152]{1,0:T(8,128)(2,1)S(1)} %get-tuple-element.17), channel_id=1, source_target_pairs={{0,24},{4,28},{8,16},{12,20},{16,8},{20,12},{24,0},{28,4},{1,25},{... | collective-permute-start | bytes 110600 | tf_op jit(solution)/shard_map/ppermute | solution.py:18
  24.1 0.0 collective-permute-start.7
  24.1 3.8 %collective-permute-start.8 = (bf16[16,1152]{1,0:T(8,128)(2,1)S(1)}, bf16[16,1152]{1,0:T(8,128)(2,1)S(1)}, u32[]{:S(2)}, u32[]{:S(2)}) collective-permute-start(bf16[16,1152]{1,0:T(8,128)(2,1)S(1)} %get-tuple-element.19), channel_id=1, source_target_pairs={{0,8},{4,12},{8,0},{12,4},{16,24},{20,28},{24,16},{28,20},{1,9},{5... | collective-permute-start | bytes 110600 | tf_op jit(solution)/shard_map/ppermute | solution.py:18
  27.9 0.7 %collective-permute-start.9 = (bf16[16,1152]{1,0:T(8,128)(2,1)S(1)}, bf16[16,1152]{1,0:T(8,128)(2,1)S(1)}, u32[]{:S(2)}, u32[]{:S(2)}) collective-permute-start(bf16[16,1152]{1,0:T(8,128)(2,1)S(1)} %get-tuple-element.20), channel_id=1, source_target_pairs={{0,28},{4,24},{8,20},{12,16},{16,12},{20,8},{24,4},{28,0},{1,29},{... | collective-permute-start | bytes 110600 | tf_op jit(solution)/shard_map/ppermute | solution.py:18
  28.6 0.0 collective-permute-done.5.refs_1_
  28.6 1.7 %collective-permute-start.10 = (bf16[16,1152]{1,0:T(8,128)(2,1)S(1)}, bf16[16,1152]{1,0:T(8,128)(2,1)S(1)}, u32[]{:S(2)}, u32[]{:S(2)}) collective-permute-start(bf16[16,1152]{1,0:T(8,128)(2,1)S(1)} %get-tuple-element.21), channel_id=1, source_target_pairs={{0,20},{4,16},{8,28},{12,24},{16,4},{20,0},{24,12},{28,8},{1,21},{... | collective-permute-start | bytes 110600 | tf_op jit(solution)/shard_map/ppermute | solution.py:18
  30.3 0.0 collective-permute-done.6.refs_2_
  30.3 3.1 %collective-permute-start.11 = (bf16[16,1152]{1,0:T(8,128)(2,1)S(1)}, bf16[16,1152]{1,0:T(8,128)(2,1)S(1)}, u32[]{:S(2)}, u32[]{:S(2)}) collective-permute-start(bf16[16,1152]{1,0:T(8,128)(2,1)S(1)} %get-tuple-element.22), channel_id=1, source_target_pairs={{0,12},{4,8},{8,4},{12,0},{16,28},{20,24},{24,20},{28,16},{1,13},{... | collective-permute-start | bytes 110600 | tf_op jit(solution)/shard_map/ppermute | solution.py:18
  33.4 0.8 %multiply_reduce_fusion = f32[32]{0:T(128)S(1)} fusion(s32[16,32]{1,0:T(8,128)} %param.8, f32[16]{0:T(128)S(1)} %iota_power_fusion), kind=kLoop, calls=%fused_computation.2 | loop fusion | flops 1504 | bytes 2240 | tf_op jit(solution)/shard_map/reduce_sum | solution.py:239
  34.2 3.4 %shard_map.69.refs_8_ = bf16[1024,4096]{1,0:T(8,128)(2,1)S(1)} custom-call(bf16[1024,4096]{1,0:T(8,128)(2,1)} %source_hbm.3, bf16[3,16,1280]{2,1,0:T(8,128)(2,1)S(1)} %pad_maximum_fusion.straight_ref._), custom_call_target="tpu_custom_call" | custom-call | tf_op jit(solution)/shard_map/pallas_call | solution.py:199
  37.5 0.0 collective-permute-done.7.refs_3_
  37.6 0.0 collective-permute-done.8.refs_4_
  37.6 0.0 collective-permute-done.9.refs_5_
  37.6 0.0 collective-permute-done.10.refs_6_
  37.6 0.0 collective-permute-done.11.refs_7_
  37.6 1.5 %project.1 = (bf16[16,1024]{1,0:T(8,128)(2,1)S(1)}, bf16[16,1024]{1,0:T(8,128)(2,1)S(1)}, bf16[16,1024]{1,0:T(8,128)(2,1)S(1)}, bf16[16,1024]{1,0:T(8,128)(2,1)S(1)}) custom-call(bf16[16,1152]{1,0:T(8,128)(2,1)S(1)} %get-tuple-element.15.refs_0_, bf16[16,1152]{1,0:T(8,128)(2,1)S(1)} %collective-permute-done.5.refs_1_, ...), custom_call_target="tpu_custom_call" | custom-call | tf_op jit(solution)/shard_map/project/pallas_call | solution.py:226
  39.1 0.0 collective-permute-start.12
  39.1 1.6 %collective-permute-start.13 = (bf16[16,1024]{1,0:T(8,128)(2,1)S(1)}, bf16[16,1024]{1,0:T(8,128)(2,1)S(1)}, u32[]{:S(2)}, u32[]{:S(2)}) collective-permute-start(bf16[16,1024]{1,0:T(8,128)(2,1)S(1)} %get-tuple-element.25), channel_id=1, source_target_pairs={{0,2},{1,3},{2,0},{3,1},{4,6},{5,7},{6,4},{7,5},{8,10},{9,11},{10,... | collective-permute-start | bytes 98312 | tf_op jit(solution)/shard_map/ppermute | solution.py:18
  40.7 0.3 collective-permute-start.14
  41.0 0.5 %bitcast_add_fusion = f32[32]{0:T(128)} fusion(f32[32]{0:T(128)S(1)} %multiply_reduce_fusion, f32[1,128]{1,0:T(1,128)S(1)} %get-tuple-element.27), kind=kLoop, calls=%fused_computation.3 | loop fusion | flops 32 | bytes 384 | tf_op jit(solution)/shard_map/add | solution.py:239
  41.5 0.0 collective-permute-done.12
  41.5 1.6 %collective-permute-done.13 = bf16[16,1024]{1,0:T(8,128)(2,1)S(1)} collective-permute-done((bf16[16,1024]{1,0:T(8,128)(2,1)S(1)}, bf16[16,1024]{1,0:T(8,128)(2,1)S(1)}, u32[]{:S(2)}, u32[]{:S(2)}) %collective-permute-start.13) | collective-permute-done | bytes 32800 | tf_op jit(solution)/shard_map/ppermute | solution.py:18
  43.1 0.9 %collective-permute-done.14 = bf16[16,1024]{1,0:T(8,128)(2,1)S(1)} collective-permute-done((bf16[16,1024]{1,0:T(8,128)(2,1)S(1)}, bf16[16,1024]{1,0:T(8,128)(2,1)S(1)}, u32[]{:S(2)}, u32[]{:S(2)}) %collective-permute-start.14) | collective-permute-done | bytes 32800 | tf_op jit(solution)/shard_map/ppermute | solution.py:18
  44.0 0.6 %add_convert_fusion = bf16[16,1024]{1,0:T(8,128)(2,1)} fusion(bf16[16,1024]{1,0:T(8,128)(2,1)S(1)} %collective-permute-done.14, bf16[16,1024]{1,0:T(8,128)(2,1)S(1)} %collective-permute-done.13, bf16[16,1024]{1,0:T(8,128)(2,1)S(1)} %collective-permute-done.12, bf16[16,1024]{1,0:T(8,128)(2,1)S(1)} %get-tuple-element.23), kind=kLoop, calls=%fused_computation.1 | loop fusion | flops 131072 | bytes 163840 | tf_op jit(solution)/shard_map/convert_element_type | solution.py:240
  (2 shorter events, 0.0 us)
Async XLA Ops:
  1.6 5.7 %collective-permute-start.3 = (bf16[16,1280]{1,0:T(8,128)(2,1)S(1)}, bf16[16,1280]{1,0:T(8,128)(2,1)S(1)}, u32[]{:S(2)}, u32[]{:S(2)}) collective-permute-start(bf16[16,1280]{1,0:T(8,128)(2,1)S(1)} %payload.1._.own_ref), channel_id=1, source_target_pairs={{0,8},{4,12},{8,0},{12,4},{16,24},{20,28},{24,16},{28,20},{1,9},{5... | collective-permute-start | bytes 122888 | tf_op jit(solution)/shard_map/ppermute | solution.py:18
  4.7 5.7 %collective-permute-start.2 = (bf16[16,1280]{1,0:T(8,128)(2,1)S(1)}, bf16[16,1280]{1,0:T(8,128)(2,1)S(1)}, u32[]{:S(2)}, u32[]{:S(2)}) collective-permute-start(bf16[16,1280]{1,0:T(8,128)(2,1)S(1)} %payload.1._.own_ref), channel_id=1, source_target_pairs={{0,16},{4,20},{8,24},{12,28},{16,0},{20,4},{24,8},{28,12},{1,17},{... | collective-permute-start | bytes 122888 | tf_op jit(solution)/shard_map/ppermute | solution.py:18
  7.3 5.8 %collective-permute-start.1 = (bf16[16,1280]{1,0:T(8,128)(2,1)S(1)}, bf16[16,1280]{1,0:T(8,128)(2,1)S(1)}, u32[]{:S(2)}, u32[]{:S(2)}) collective-permute-start(bf16[16,1280]{1,0:T(8,128)(2,1)S(1)} %payload.1._.own_ref), channel_id=1, source_target_pairs={{0,24},{4,28},{8,16},{12,20},{16,8},{20,12},{24,0},{28,4},{1,25},{... | collective-permute-start | bytes 122888 | tf_op jit(solution)/shard_map/ppermute | solution.py:18
  13.1 5.6 %collective-permute-start.4 = (bf16[3,16,1280]{2,1,0:T(8,128)(2,1)S(1)}, bf16[3,16,1280]{2,1,0:T(8,128)(2,1)S(1)}, u32[]{:S(2)}, u32[]{:S(2)}) collective-permute-start(bf16[3,16,1280]{2,1,0:T(8,128)(2,1)S(1)} %pad_maximum_fusion.straight_ref._), channel_id=1, source_target_pairs={{0,4},{4,0},{8,12},{12,8},{16,20},{20,16},{24,28},{28,24},{1,5},{5... | collective-permute-start | bytes 368648 | tf_op jit(solution)/shard_map/ppermute | solution.py:18
  14.7 4.0 %collective-permute-start = (bf16[16,1280]{1,0:T(8,128)(2,1)S(1)}, bf16[16,1280]{1,0:T(8,128)(2,1)S(1)}, u32[]{:S(2)}, u32[]{:S(2)}) collective-permute-start(bf16[16,1280]{1,0:T(8,128)(2,1)S(1)} %payload.1._.own_ref), channel_id=1, source_target_pairs={{0,4},{4,0},{8,12},{12,8},{16,20},{20,16},{24,28},{28,24},{1,5},{5... | collective-permute-start | bytes 122888 | tf_op jit(solution)/shard_map/ppermute | solution.py:18
  22.1 6.5 %collective-permute-start.5 = (bf16[16,1152]{1,0:T(8,128)(2,1)S(1)}, bf16[16,1152]{1,0:T(8,128)(2,1)S(1)}, u32[]{:S(2)}, u32[]{:S(2)}) collective-permute-start(bf16[16,1152]{1,0:T(8,128)(2,1)S(1)} %get-tuple-element.16), channel_id=1, source_target_pairs={{0,4},{4,0},{8,12},{12,8},{16,20},{20,16},{24,28},{28,24},{1,5},{5... | collective-permute-start | bytes 110600 | tf_op jit(solution)/shard_map/ppermute | solution.py:18
  23.5 6.8 %collective-permute-start.6 = (bf16[16,1152]{1,0:T(8,128)(2,1)S(1)}, bf16[16,1152]{1,0:T(8,128)(2,1)S(1)}, u32[]{:S(2)}, u32[]{:S(2)}) collective-permute-start(bf16[16,1152]{1,0:T(8,128)(2,1)S(1)} %get-tuple-element.17), channel_id=1, source_target_pairs={{0,24},{4,28},{8,16},{12,20},{16,8},{20,12},{24,0},{28,4},{1,25},{... | collective-permute-start | bytes 110600 | tf_op jit(solution)/shard_map/ppermute | solution.py:18
  24.1 13.5 %collective-permute-start.7 = (bf16[16,1152]{1,0:T(8,128)(2,1)S(1)}, bf16[16,1152]{1,0:T(8,128)(2,1)S(1)}, u32[]{:S(2)}, u32[]{:S(2)}) collective-permute-start(bf16[16,1152]{1,0:T(8,128)(2,1)S(1)} %get-tuple-element.18), channel_id=1, source_target_pairs={{0,16},{4,20},{8,24},{12,28},{16,0},{20,4},{24,8},{28,12},{1,17},{... | collective-permute-start | bytes 110600 | tf_op jit(solution)/shard_map/ppermute | solution.py:18
  24.1 13.5 %collective-permute-start.8 = (bf16[16,1152]{1,0:T(8,128)(2,1)S(1)}, bf16[16,1152]{1,0:T(8,128)(2,1)S(1)}, u32[]{:S(2)}, u32[]{:S(2)}) collective-permute-start(bf16[16,1152]{1,0:T(8,128)(2,1)S(1)} %get-tuple-element.19), channel_id=1, source_target_pairs={{0,8},{4,12},{8,0},{12,4},{16,24},{20,28},{24,16},{28,20},{1,9},{5... | collective-permute-start | bytes 110600 | tf_op jit(solution)/shard_map/ppermute | solution.py:18
  27.9 9.6 %collective-permute-start.9 = (bf16[16,1152]{1,0:T(8,128)(2,1)S(1)}, bf16[16,1152]{1,0:T(8,128)(2,1)S(1)}, u32[]{:S(2)}, u32[]{:S(2)}) collective-permute-start(bf16[16,1152]{1,0:T(8,128)(2,1)S(1)} %get-tuple-element.20), channel_id=1, source_target_pairs={{0,28},{4,24},{8,20},{12,16},{16,12},{20,8},{24,4},{28,0},{1,29},{... | collective-permute-start | bytes 110600 | tf_op jit(solution)/shard_map/ppermute | solution.py:18
  28.6 9.0 %collective-permute-start.10 = (bf16[16,1152]{1,0:T(8,128)(2,1)S(1)}, bf16[16,1152]{1,0:T(8,128)(2,1)S(1)}, u32[]{:S(2)}, u32[]{:S(2)}) collective-permute-start(bf16[16,1152]{1,0:T(8,128)(2,1)S(1)} %get-tuple-element.21), channel_id=1, source_target_pairs={{0,20},{4,16},{8,28},{12,24},{16,4},{20,0},{24,12},{28,8},{1,21},{... | collective-permute-start | bytes 110600 | tf_op jit(solution)/shard_map/ppermute | solution.py:18
  30.3 7.3 %collective-permute-start.11 = (bf16[16,1152]{1,0:T(8,128)(2,1)S(1)}, bf16[16,1152]{1,0:T(8,128)(2,1)S(1)}, u32[]{:S(2)}, u32[]{:S(2)}) collective-permute-start(bf16[16,1152]{1,0:T(8,128)(2,1)S(1)} %get-tuple-element.22), channel_id=1, source_target_pairs={{0,12},{4,8},{8,4},{12,0},{16,28},{20,24},{24,20},{28,16},{1,13},{... | collective-permute-start | bytes 110600 | tf_op jit(solution)/shard_map/ppermute | solution.py:18
  39.1 2.4 %collective-permute-start.12 = (bf16[16,1024]{1,0:T(8,128)(2,1)S(1)}, bf16[16,1024]{1,0:T(8,128)(2,1)S(1)}, u32[]{:S(2)}, u32[]{:S(2)}) collective-permute-start(bf16[16,1024]{1,0:T(8,128)(2,1)S(1)} %get-tuple-element.24), channel_id=1, source_target_pairs={{0,1},{1,0},{2,3},{3,2},{4,5},{5,4},{6,7},{7,6},{8,9},{9,8},{10,11... | collective-permute-start | bytes 98312 | tf_op jit(solution)/shard_map/ppermute | solution.py:18
  39.1 4.0 %collective-permute-start.13 = (bf16[16,1024]{1,0:T(8,128)(2,1)S(1)}, bf16[16,1024]{1,0:T(8,128)(2,1)S(1)}, u32[]{:S(2)}, u32[]{:S(2)}) collective-permute-start(bf16[16,1024]{1,0:T(8,128)(2,1)S(1)} %get-tuple-element.25), channel_id=1, source_target_pairs={{0,2},{1,3},{2,0},{3,1},{4,6},{5,7},{6,4},{7,5},{8,10},{9,11},{10,... | collective-permute-start | bytes 98312 | tf_op jit(solution)/shard_map/ppermute | solution.py:18
  40.7 3.3 %collective-permute-start.14 = (bf16[16,1024]{1,0:T(8,128)(2,1)S(1)}, bf16[16,1024]{1,0:T(8,128)(2,1)S(1)}, u32[]{:S(2)}, u32[]{:S(2)}) collective-permute-start(bf16[16,1024]{1,0:T(8,128)(2,1)S(1)} %get-tuple-element.26), channel_id=1, source_target_pairs={{0,3},{1,2},{2,1},{3,0},{4,7},{5,6},{6,5},{7,4},{8,11},{9,10},{10,... | collective-permute-start | bytes 98312 | tf_op jit(solution)/shard_map/ppermute | solution.py:18
where the time goes:
time: 44.9 us; the launch traced here: 44.6 us
  starting transfers between devices  20.9 us (47%)
  Pallas kernels  10.9 us (24%)
  waiting for transfers between devices  10.2 us (23%)
  other arithmetic  1.95 us (4%)
  between operations  0.71 us (2%)
    ppermute x15, starting transfers between devices, exchange(): return lax.ppermute(value, axis, [(i, i ^ step) for i in range(count)])  20.9 us
    ppermute x15, waiting for transfers between devices, exchange(): return lax.ppermute(value, axis, [(i, i ^ step) for i in range(count)])  10.2 us
    pallas_call x2, Pallas kernels, stage(): pl.pallas_call(stage_kernel, in_specs=[hbm, vmem], out_specs=vmem, out_sh...  4.99 us
    pallas_call x1, Pallas kernels, per_device(): pl.pallas_call(functools.partial(attend_kernel, heads=heads), in_specs=[v...  3.48 us
    pallas_call x1, Pallas kernels, per_device(): pl.pallas_call(functools.partial(project_kernel, sources=devices_mem, hea...  1.5 us
    pallas_call x1, Pallas kernels, per_device(): pl.pallas_call(payload_kernel, in_specs=[hbm] * 2, out_specs=vmem, out_sh...  0.93 us
  transfers between devices with their start and end apart: 15, of which 5 were waited for; matrix products, arithmetic and copies ran while one was open for 3% of the time, Pallas kernels for 11%

commit v1 on v0

--- a/solution.py
+++ b/solution.py
@@ -16,6 +16,44 @@
 def exchange(value, axis, step):
     count = lax.axis_size(axis)
     return lax.ppermute(value, axis, [(i, i ^ step) for i in range(count)])
+
+
+def split_stats(stats, heads):
+    high = stats.astype(jnp.bfloat16).astype(jnp.float32)
+    rest = stats - high
+    middle = rest.astype(jnp.bfloat16).astype(jnp.float32)
+    low = rest - middle
+    packed = high + pltpu.roll(middle, 2 * heads, 1) + pltpu.roll(low, 4 * heads, 1)
+    return packed.astype(jnp.bfloat16)
+
+
+def join_stats(packed, heads):
+    packed = packed.astype(jnp.float32)
+    return (
+        packed
+        + pltpu.roll(packed, LANES - 2 * heads, 1)
+        + pltpu.roll(packed, LANES - 4 * heads, 1)
+    )
+
+
+def merge_partials(messages, heads, width):
+    depth = width // heads
+    scale = depth**-0.5 * math.log2(math.e)
+    stats = [join_stats(m[:, width:], heads) for m in messages]
+    lane = lax.broadcasted_iota(jnp.int32, stats[0].shape, 1)
+    highest = functools.reduce(jnp.maximum, stats)
+    factors = [jnp.where(lane < heads, jnp.exp2((s - highest) * scale), 0.0) for s in stats]
+    total = sum(f * pltpu.roll(s, LANES - heads, 1) for f, s in zip(factors, stats))
+    return highest, total, factors, lane
+
+
+def weighted_sums(messages, factors, heads, depth):
+    for h in range(heads):
+        acc = None
+        for f, m in zip(factors, messages):
+            term = f[:, h : h + 1] * m[:, h * depth : (h + 1) * depth].astype(jnp.float32)
+            acc = term if acc is None else acc + term
+        yield h, acc.astype(jnp.bfloat16)
 
 
 def payload_kernel(queries_hbm, selected_hbm, out_ref, queries_ref, selected_ref, sems):
@@ -45,18 +83,14 @@
     copy.wait()
 
 
-def attend_kernel(own_ref, near_ref, straight_ref, forwarded_ref, cache_ref, *refs, heads):
-    messages = refs[:-1]
-    hits_ref = refs[-1]
+def attend_kernel(single_ref, several_ref, cache_ref, messages_ref, hits_ref, *, heads):
     blocks, _, heads_kv, tokens, depth = cache_ref.shape
     width = heads * depth
-    rows_each = own_ref.shape[0]
-    all_blocks = own_ref.shape[1] - width
+    rows_each = single_ref.shape[0]
+    all_blocks = single_ref.shape[1] - width
     group_q = heads // heads_kv
     scale = depth**-0.5 * math.log2(math.e)
-    payloads = [own_ref, near_ref]
-    payloads += [straight_ref.at[i] for i in range(straight_ref.shape[0])]
-    payloads += [forwarded_ref.at[i] for i in range(forwarded_ref.shape[0])]
+    payloads = [single_ref] + [several_ref.at[i] for i in range(several_ref.shape[0])]
     first = lax.axis_index("mem") * blocks
     column = lax.broadcasted_iota(jnp.int32, (all_blocks, LANES), 1)
     pick = (lax.broadcasted_iota(jnp.int32, (all_blocks, LANES), 0) == column + first) & (
@@ -72,7 +106,7 @@
     ).astype(jnp.bfloat16)
     hits = jnp.zeros((1, LANES), jnp.float32)
     batch = min(len(payloads), 8)
-    pair = math.gcd(group_q, 2)
+    pair = math.gcd(group_q, max(1, 256 // (batch * rows_each)))
     rows = batch * rows_each
     lane = lax.broadcasted_iota(jnp.int32, (rows, LANES), 1)
     for start in range(0, len(payloads), batch):
@@ -115,60 +149,58 @@
                     h = first_head + j
                     for i in range(batch):
                         at = j * rows + i * rows_each
-                        messages[start + i][:, h * depth : (h + 1) * depth] = out[
+                        messages_ref[start + i, :, h * depth : (h + 1) * depth] = out[
                             at : at + rows_each
                         ]
                     stats = jnp.where(lane == h, peak[j * rows : (j + 1) * rows], stats)
                     stats = jnp.where(lane == heads + h, total[j * rows : (j + 1) * rows], stats)
-        high = stats.astype(jnp.bfloat16).astype(jnp.float32)
-        rest = stats - high
-        middle = rest.astype(jnp.bfloat16).astype(jnp.float32)
-        low = rest - middle
-        packed = (
-            high + pltpu.roll(middle, 2 * heads, 1) + pltpu.roll(low, 4 * heads, 1)
-        ).astype(jnp.bfloat16)
+        packed = split_stats(stats, heads)
         for i in range(batch):
-            messages[start + i][:, width:] = packed[i * rows_each : (i + 1) * rows_each]
+            messages_ref[start + i, :, width:] = packed[i * rows_each : (i + 1) * rows_each]
     hits_ref[...] = hits
 
 
-def project_kernel(*refs, sources, heads):
-    messages = refs[:sources]
-    weight_ref = refs[sources]
-    outs = refs[sources + 1 :]
+def merge_kernel(mine_ref, theirs_ref, *outs, heads):
+    width = mine_ref.shape[2] - LANES
+    depth = width // heads
+    for i, out in enumerate(outs):
+        pair = [mine_ref.at[i], theirs_ref.at[i]]
+        highest, total, factors, lane = merge_partials(pair, heads, width)
+        for h, merged in weighted_sums(pair, factors, heads, depth):
+            out[:, h * depth : (h + 1) * depth] = merged
+        stats = jnp.where(lane < heads, highest, pltpu.roll(total, heads, 1))
+        stats = jnp.where(lane < 2 * heads, stats, 0.0)
+        out[:, width:] = split_stats(stats, heads)
+
+
+def project(attended, weight_ref, steps, outs):
     me = lax.axis_index("head")
-    rows = messages[0].shape[0]
-    width = weight_ref.shape[0]
-    depth = width // heads
-    scale = depth**-0.5 * math.log2(math.e)
-    stats = []
-    for m in messages:
-        packed = m[:, width:].astype(jnp.float32)
-        stats.append(
-            packed
-            + pltpu.roll(packed, LANES - 2 * heads, 1)
-            + pltpu.roll(packed, LANES - 4 * heads, 1)
-        )
-    lane = lax.broadcasted_iota(jnp.int32, (rows, LANES), 1)
-    highest = functools.reduce(jnp.maximum, stats)
-    factors = [jnp.where(lane < heads, jnp.exp2((s - highest) * scale), 0.0) for s in stats]
-    total = sum(f * pltpu.roll(s, LANES - heads, 1) for f, s in zip(factors, stats))
-    inverse = 1.0 / jnp.where(lane < heads, total, 1.0)
-    factors = [f * inverse for f in factors]
-    attended = []
-    for h in range(heads):
-        acc = None
-        for f, m in zip(factors, messages):
-            term = f[:, h : h + 1] * m[:, h * depth : (h + 1) * depth].astype(jnp.float32)
-            acc = term if acc is None else acc + term
-        attended.append(acc.astype(jnp.bfloat16))
-    attended = jnp.concatenate(attended, axis=1)
-    columns = weight_ref.shape[1] // len(outs)
-    for i, out in enumerate(outs):
-        at = pl.multiple_of((me ^ i) * columns, columns)
+    columns = outs[0].shape[1]
+    for k, out in zip(steps, outs):
+        at = pl.multiple_of((me ^ k) * columns, columns)
         out[...] = jnp.dot(
             attended, weight_ref[:, pl.ds(at, columns)], preferred_element_type=jnp.float32
         ).astype(jnp.bfloat16)
+
+
+def project_far_kernel(*refs, sources, heads, steps):
+    messages = refs[:sources]
+    weight_ref, attended_ref = refs[sources : sources + 2]
+    outs = refs[sources + 2 :]
+    width = attended_ref.shape[1]
+    depth = width // heads
+    _, total, factors, lane = merge_partials(messages, heads, width)
+    inverse = 1.0 / jnp.where(lane < heads, total, 1.0)
+    factors = [f * inverse for f in factors]
+    attended = jnp.concatenate(
+        [a for _, a in weighted_sums(messages, factors, heads, depth)], axis=1
+    )
+    attended_ref[...] = attended
+    project(attended, weight_ref, steps, outs)
+
+
+def project_near_kernel(attended_ref, weight_ref, *outs, steps):
+    project(attended_ref[...], weight_ref, steps, outs)
 
 
 def per_device(queries, cache_blocks, selected, counts, output_weight):
@@ -195,48 +227,69 @@
         name="payload",
     )(keep(queries), keep(selected))
 
+    def call(kernel, operands, specs, shapes, limit, scratch=()):
+        return pl.pallas_call(
+            kernel,
+            in_specs=specs,
+            out_specs=[vmem] * len(shapes),
+            out_shape=shapes,
+            scratch_shapes=list(scratch),
+            compiler_params=pltpu.CompilerParams(vmem_limit_bytes=limit * 2**20),
+        )(*operands)
+
     def stage(array, after):
-        return pl.pallas_call(
-            stage_kernel,
-            in_specs=[hbm, vmem],
-            out_specs=vmem,
-            out_shape=jax.ShapeDtypeStruct(array.shape, array.dtype),
-            scratch_shapes=[pltpu.SemaphoreType.DMA(())],
-            compiler_params=pltpu.CompilerParams(vmem_limit_bytes=4 * 2**20),
-        )(keep(array), after)
+        shape = jax.ShapeDtypeStruct(array.shape, array.dtype)
+        operands = (keep(array), after)
+        sem = [pltpu.SemaphoreType.DMA(())]
+        return call(stage_kernel, operands, [hbm, vmem], [shape], 4, sem)[0]
 
     even = list(range(devices_mem - 2, 0, -2))
     straight = jnp.stack([exchange(payload, "mem", k) for k in even])
     near = exchange(payload, "mem", 1)
     cache_blocks = stage(cache_blocks, payload)
     forwarded = exchange(straight, "mem", 1)
-    output_weight = stage(output_weight, straight)
-    steps = [0, 1] + even + [k ^ 1 for k in even]
-    message_shape = jax.ShapeDtypeStruct((rows, width + LANES), jnp.bfloat16)
-    *messages, hits = pl.pallas_call(
-        functools.partial(attend_kernel, heads=heads),
-        in_specs=[vmem] * 5,
-        out_specs=[vmem] * (devices_mem + 1),
-        out_shape=[message_shape] * devices_mem + [jax.ShapeDtypeStruct((1, LANES), jnp.float32)],
-        compiler_params=pltpu.CompilerParams(vmem_limit_bytes=32 * 2**20),
-        name="attend",
-    )(payload, near, straight, forwarded, cache_blocks)
-    returned = [m if k == 0 else exchange(m, "mem", k) for k, m in zip(steps, messages)]
-    columns = output_weight.shape[1] // devices_head
-    shares = pl.pallas_call(
-        functools.partial(project_kernel, sources=devices_mem, heads=heads),
-        in_specs=[vmem] * (devices_mem + 1),
-        out_specs=[vmem] * devices_head,
-        out_shape=[jax.ShapeDtypeStruct((rows, columns), jnp.bfloat16)] * devices_head,
-        compiler_params=pltpu.CompilerParams(vmem_limit_bytes=24 * 2**20),
-        name="project",
-    )(*returned, output_weight)
-    arrived = {k: exchange(shares[k], "head", k) for k in range(devices_head - 1, 0, -1)}
-    layer_out = shares[0].astype(jnp.float32)
+    message = jax.ShapeDtypeStruct((rows, width + LANES), jnp.bfloat16)
+    messages = jax.ShapeDtypeStruct((len(even) + 1,) + message.shape, message.dtype)
+    hits = jax.ShapeDtypeStruct((1, LANES), jnp.float32)
+    attend = functools.partial(attend_kernel, heads=heads)
+    mine, hits_a = call(attend, (payload, straight, cache_blocks), [vmem] * 3, [messages, hits], 24)
+    theirs, hits_b = call(attend, (near, forwarded, cache_blocks), [vmem] * 3, [messages, hits], 24)
+    crossed = exchange(theirs, "mem", 1)
+    output_weight = stage(output_weight, theirs)
+    merged = call(
+        functools.partial(merge_kernel, heads=heads),
+        (mine, crossed),
+        [vmem] * 2,
+        [message] * (len(even) + 1),
+        8,
+    )
+    returned = [merged[0]] + [exchange(m, "mem", k) for k, m in zip(even, merged[1:])]
+    share = jax.ShapeDtypeStruct((rows, output_weight.shape[1] // devices_head), jnp.bfloat16)
+    far_steps = tuple(range(devices_head - 1, 1, -1))
+    near_steps = (1, 0)
+    attended, *far = call(
+        functools.partial(
+            project_far_kernel, sources=len(returned), heads=heads, steps=far_steps
+        ),
+        (*returned, output_weight),
+        [vmem] * (len(returned) + 1),
+        [jax.ShapeDtypeStruct((rows, width), jnp.bfloat16)] + [share] * len(far_steps),
+        16,
+    )
+    arrived = {k: exchange(s, "head", k) for k, s in zip(far_steps, far)}
+    beside, own = call(
+        functools.partial(project_near_kernel, steps=near_steps),
+        (attended, output_weight),
+        [vmem] * 2,
+        [share] * 2,
+        16,
+    )
+    arrived[1] = exchange(beside, "head", 1)
+    layer_out = own.astype(jnp.float32)
     for k in range(1, devices_head):
         layer_out = layer_out + arrived[k].astype(jnp.float32)
     decays = 0.5 ** jnp.arange(counts.shape[0], dtype=jnp.float32)
-    block_heat = jnp.sum(decays[:, None] * counts.astype(jnp.float32), axis=0) + hits[0, :blocks]
+    block_heat = jnp.sum(decays[:, None] * counts.astype(jnp.float32), axis=0) + (hits_a + hits_b)[0, :blocks]
     return (layer_out.astype(jnp.bfloat16), block_heat)
 
 

time: 44.9 us -> 42 us (0.935)
  starting transfers between devices: 20.9 us -> 15.5 us
  waiting for transfers between devices: 10.2 us -> 11.8 us
  Pallas kernels: 10.9 us -> 12.4 us
  other arithmetic: 1.95 us -> 1.26 us
    ppermute x15 -> x12, starting transfers between devices: 20.9 us -> 15.5 us  [exchange(): return lax.ppermute(value, axis, [(i, i ^ step) for i in range(count)])]
    ppermute x15 -> x12, waiting for transfers between devices: 10.2 us -> 11.8 us  [exchange(): return lax.ppermute(value, axis, [(i, i ^ step) for i in range(count)])]
    pallas_call x4 -> x7, Pallas kernels: 9.97 us -> 11.5 us  [call(): pl.pallas_call(kernel, in_specs=specs, out_specs=[vmem] * len(shapes), ou...]
    reduce_sum x1, other arithmetic: 0.78 us -> 0.09 us  [per_device(): jnp.sum(decays[:, None] * counts.astype(jnp.float32), axis=0)]
  transfers between devices with their start and end apart: 15 -> 12, of which waited for: 5 -> 6; matrix products, arithmetic and copies ran while one was open for 3% -> 1% of each run, Pallas kernels for 11% -> 17%
where the time goes in v1:
time: 42 us; the launch traced here: 41.7 us
  starting transfers between devices  15.5 us (37%)
  Pallas kernels  12.4 us (30%)
  waiting for transfers between devices  11.8 us (28%)
  other arithmetic  1.26 us (3%)
  between operations  0.72 us (2%)
    ppermute x12, starting transfers between devices, exchange(): return lax.ppermute(value, axis, [(i, i ^ step) for i in range(count)])  15.5 us
    ppermute x12, waiting for transfers between devices, exchange(): return lax.ppermute(value, axis, [(i, i ^ step) for i in range(count)])  11.8 us
    pallas_call x7, Pallas kernels, call(): pl.pallas_call(kernel, in_specs=specs, out_specs=[vmem] * len(shapes), ou...  11.5 us
    pallas_call x1, Pallas kernels, per_device(): pl.pallas_call(payload_kernel, in_specs=[hbm] * 2, out_specs=vmem, out_sh...  0.94 us
  transfers between devices with their start and end apart: 12, of which 6 were waited for; matrix products, arithmetic and copies ran while one was open for 1% of the time, Pallas kernels for 17%

profile of v1, /device:TPU:0, one launch (start us, length us, event | category | flops | bytes accessed | tf_op | source)
XLA Modules:
  0.0 41.7 jit_solution(16987215634013600707)
XLA Ops:
  0.6 0.0 copy-start
  0.6 0.9 %payload.1._.single_ref = bf16[16,1280]{1,0:T(8,128)(2,1)S(1)} custom-call(bf16[16,8,128]{2,1,0:T(8,128)(2,1)} %queries_hbm.1, s32[16,32]{1,0:T(8,128)} %selected_hbm.1), custom_call_target="tpu_custom_call" | custom-call | tf_op jit(solution)/shard_map/payload/pallas_call | solution.py:216
  1.6 3.1 %collective-permute-start.2 = (bf16[16,1280]{1,0:T(8,128)(2,1)S(1)}, bf16[16,1280]{1,0:T(8,128)(2,1)S(1)}, u32[]{:S(2)}, u32[]{:S(2)}) collective-permute-start(bf16[16,1280]{1,0:T(8,128)(2,1)S(1)} %payload.1._.single_ref), channel_id=1, source_target_pairs={{0,8},{4,12},{8,0},{12,4},{16,24},{20,28},{24,16},{28,20},{1,9},{5... | collective-permute-start | bytes 122888 | tf_op jit(solution)/shard_map/ppermute | solution.py:18
  4.7 2.6 %collective-permute-start.1 = (bf16[16,1280]{1,0:T(8,128)(2,1)S(1)}, bf16[16,1280]{1,0:T(8,128)(2,1)S(1)}, u32[]{:S(2)}, u32[]{:S(2)}) collective-permute-start(bf16[16,1280]{1,0:T(8,128)(2,1)S(1)} %payload.1._.single_ref), channel_id=1, source_target_pairs={{0,16},{4,20},{8,24},{12,28},{16,0},{20,4},{24,8},{28,12},{1,17},{... | collective-permute-start | bytes 122888 | tf_op jit(solution)/shard_map/ppermute | solution.py:18
  7.3 0.0 collective-permute-start
  7.3 0.0 collective-permute-done.2
  7.3 3.1 %collective-permute-done.1 = bf16[16,1280]{1,0:T(8,128)(2,1)S(1)} collective-permute-done((bf16[16,1280]{1,0:T(8,128)(2,1)S(1)}, bf16[16,1280]{1,0:T(8,128)(2,1)S(1)}, u32[]{:S(2)}, u32[]{:S(2)}) %collective-permute-start.1) | collective-permute-done | bytes 40992 | tf_op jit(solution)/shard_map/ppermute | solution.py:18
  10.4 2.7 %collective-permute-done = bf16[16,1280]{1,0:T(8,128)(2,1)S(1)} collective-permute-done((bf16[16,1280]{1,0:T(8,128)(2,1)S(1)}, bf16[16,1280]{1,0:T(8,128)(2,1)S(1)}, u32[]{:S(2)}, u32[]{:S(2)}) %collective-permute-start) | collective-permute-done | bytes 40992 | tf_op jit(solution)/shard_map/ppermute | solution.py:18
  13.1 1.6 %collective-permute-start.4 = (bf16[3,16,1280]{2,1,0:T(8,128)(2,1)S(1)}, bf16[3,16,1280]{2,1,0:T(8,128)(2,1)S(1)}, u32[]{:S(2)}, u32[]{:S(2)}) collective-permute-start(bf16[3,16,1280]{2,1,0:T(8,128)(2,1)S(1)} %pad_maximum_fusion.several_ref), channel_id=1, source_target_pairs={{0,4},{4,0},{8,12},{12,8},{16,20},{20,16},{24,28},{28,24},{1,5},{5... | collective-permute-start | bytes 368648 | tf_op jit(solution)/shard_map/ppermute | solution.py:18
  14.7 0.5 %collective-permute-start.3 = (bf16[16,1280]{1,0:T(8,128)(2,1)S(1)}, bf16[16,1280]{1,0:T(8,128)(2,1)S(1)}, u32[]{:S(2)}, u32[]{:S(2)}) collective-permute-start(bf16[16,1280]{1,0:T(8,128)(2,1)S(1)} %payload.1._.single_ref), channel_id=1, source_target_pairs={{0,4},{4,0},{8,12},{12,8},{16,20},{20,16},{24,28},{28,24},{1,5},{5... | collective-permute-start | bytes 122888 | tf_op jit(solution)/shard_map/ppermute | solution.py:18
  15.2 1.6 %shard_map.68.cache_ref = bf16[32,2,2,64,128]{4,3,2,1,0:T(8,128)(2,1)S(1)} custom-call(bf16[32,2,2,64,128]{4,3,2,1,0:T(8,128)(2,1)} %source_hbm.2, bf16[16,1280]{1,0:T(8,128)(2,1)S(1)} %payload.1._.single_ref), custom_call_target="tpu_custom_call" | custom-call | tf_op jit(solution)/shard_map/pallas_call | solution.py:231
  16.8 1.9 %collective-permute-done.3.single_ref = bf16[16,1280]{1,0:T(8,128)(2,1)S(1)} collective-permute-done((bf16[16,1280]{1,0:T(8,128)(2,1)S(1)}, bf16[16,1280]{1,0:T(8,128)(2,1)S(1)}, u32[]{:S(2)}, u32[]{:S(2)}) %collective-permute-start.3) | collective-permute-done | bytes 40992 | tf_op jit(solution)/shard_map/ppermute | solution.py:18
  18.7 0.0 collective-permute-done.4.several_ref
  18.7 2.2 %shard_map.70 = (bf16[4,16,1152]{2,1,0:T(8,128)(2,1)S(1)}, f32[1,128]{1,0:T(1,128)S(1)}) custom-call(bf16[16,1280]{1,0:T(8,128)(2,1)S(1)} %collective-permute-done.3.single_ref, bf16[3,16,1280]{2,1,0:T(8,128)(2,1)S(1)} %collective-permute-done.4.several_ref, bf16[32,2,2,64,128]{4,3,2,1,0:T(8,128)(2,1)S(1)} %shard_map.68.cache_ref), custom_call_target="tpu_custom_call" | custom-call | tf_op jit(solution)/shard_map/pallas_call | solution.py:231
  20.9 1.4 %collective-permute-start.5 = (bf16[4,16,1152]{2,1,0:T(8,128)(2,1)S(1)}, bf16[4,16,1152]{2,1,0:T(8,128)(2,1)S(1)}, u32[]{:S(2)}, u32[]{:S(2)}) collective-permute-start(bf16[4,16,1152]{2,1,0:T(8,128)(2,1)S(1)} %get-tuple-element.16._), channel_id=1, source_target_pairs={{0,4},{4,0},{8,12},{12,8},{16,20},{20,16},{24,28},{28,24},{1,5},{5... | collective-permute-start | bytes 442376 | tf_op jit(solution)/shard_map/ppermute | solution.py:18
  22.3 2.2 %shard_map.69 = (bf16[4,16,1152]{2,1,0:T(8,128)(2,1)S(1)}, f32[1,128]{1,0:T(1,128)S(1)}) custom-call(bf16[16,1280]{1,0:T(8,128)(2,1)S(1)} %payload.1._.single_ref, bf16[3,16,1280]{2,1,0:T(8,128)(2,1)S(1)} %pad_maximum_fusion.several_ref, bf16[32,2,2,64,128]{4,3,2,1,0:T(8,128)(2,1)S(1)} %shard_map.68.cache_ref), custom_call_target="tpu_custom_call" | custom-call | tf_op jit(solution)/shard_map/pallas_call | solution.py:231
  24.5 1.6 %collective-permute-done.5.theirs_ref = bf16[4,16,1152]{2,1,0:T(8,128)(2,1)S(1)} collective-permute-done((bf16[4,16,1152]{2,1,0:T(8,128)(2,1)S(1)}, bf16[4,16,1152]{2,1,0:T(8,128)(2,1)S(1)}, u32[]{:S(2)}, u32[]{:S(2)}) %collective-permute-start.5) | collective-permute-done | bytes 147488 | tf_op jit(solution)/shard_map/ppermute | solution.py:18
  26.1 0.6 %shard_map.71 = (bf16[16,1152]{1,0:T(8,128)(2,1)S(1)}, bf16[16,1152]{1,0:T(8,128)(2,1)S(1)}, bf16[16,1152]{1,0:T(8,128)(2,1)S(1)}, bf16[16,1152]{1,0:T(8,128)(2,1)S(1)}) custom-call(bf16[4,16,1152]{2,1,0:T(8,128)(2,1)S(1)} %get-tuple-element.15.mine_ref, bf16[4,16,1152]{2,1,0:T(8,128)(2,1)S(1)} %collective-permute-done.5.theirs_ref), custom_call_target="tpu_custom_call" | custom-call | tf_op jit(solution)/shard_map/pallas_call | solution.py:231
  26.7 0.6 %collective-permute-start.6 = (bf16[16,1152]{1,0:T(8,128)(2,1)S(1)}, bf16[16,1152]{1,0:T(8,128)(2,1)S(1)}, u32[]{:S(2)}, u32[]{:S(2)}) collective-permute-start(bf16[16,1152]{1,0:T(8,128)(2,1)S(1)} %get-tuple-element.18), channel_id=1, source_target_pairs={{0,24},{4,28},{8,16},{12,20},{16,8},{20,12},{24,0},{28,4},{1,25},{... | collective-permute-start | bytes 110600 | tf_op jit(solution)/shard_map/ppermute | solution.py:18
  27.3 0.0 collective-permute-start.7
  27.3 3.8 %collective-permute-start.8 = (bf16[16,1152]{1,0:T(8,128)(2,1)S(1)}, bf16[16,1152]{1,0:T(8,128)(2,1)S(1)}, u32[]{:S(2)}, u32[]{:S(2)}) collective-permute-start(bf16[16,1152]{1,0:T(8,128)(2,1)S(1)} %get-tuple-element.20), channel_id=1, source_target_pairs={{0,8},{4,12},{8,0},{12,4},{16,24},{20,28},{24,16},{28,20},{1,9},{5... | collective-permute-start | bytes 110600 | tf_op jit(solution)/shard_map/ppermute | solution.py:18
  31.1 0.0 copy-done
  31.1 0.1 multiply_reduce_fusion
  31.2 3.4 %shard_map.72.refs_4_.weight_ref = bf16[1024,4096]{1,0:T(8,128)(2,1)S(1)} custom-call(bf16[1024,4096]{1,0:T(8,128)(2,1)} %source_hbm.3, bf16[4,16,1152]{2,1,0:T(8,128)(2,1)S(1)} %get-tuple-element.16._), custom_call_target="tpu_custom_call" | custom-call | tf_op jit(solution)/shard_map/pallas_call | solution.py:231
  34.6 0.0 collective-permute-done.6.refs_1_
  34.6 0.0 collective-permute-done.7.refs_2_
  34.6 0.0 collective-permute-done.8.refs_3_
  34.6 0.9 %shard_map.73 = (bf16[16,1024]{1,0:T(8,128)(2,1)S(1)}, bf16[16,1024]{1,0:T(8,128)(2,1)S(1)}, bf16[16,1024]{1,0:T(8,128)(2,1)S(1)}) custom-call(bf16[16,1152]{1,0:T(8,128)(2,1)S(1)} %get-tuple-element.17.refs_0_, bf16[16,1152]{1,0:T(8,128)(2,1)S(1)} %collective-permute-done.6.refs_1_, bf16[16,1152]{1,0:T(8,128)(2,1)S(1)} %collective-permute-done.7.refs_2_, ...), custom_call_target="tpu_custom_call" | custom-call | tf_op jit(solution)/shard_map/pallas_call | solution.py:231
  35.5 0.7 %shard_map.74 = (bf16[16,1024]{1,0:T(8,128)(2,1)S(1)}, bf16[16,1024]{1,0:T(8,128)(2,1)S(1)}) custom-call(bf16[16,1024]{1,0:T(8,128)(2,1)S(1)} %get-tuple-element.21.attended_ref, bf16[1024,4096]{1,0:T(8,128)(2,1)S(1)} %shard_map.72.refs_4_.weight_ref), custom_call_target="tpu_custom_call" | custom-call | tf_op jit(solution)/shard_map/pallas_call | solution.py:231
  36.2 0.0 collective-permute-start.9
  36.2 1.6 %collective-permute-start.10 = (bf16[16,1024]{1,0:T(8,128)(2,1)S(1)}, bf16[16,1024]{1,0:T(8,128)(2,1)S(1)}, u32[]{:S(2)}, u32[]{:S(2)}) collective-permute-start(bf16[16,1024]{1,0:T(8,128)(2,1)S(1)} %get-tuple-element.24), channel_id=1, source_target_pairs={{0,2},{1,3},{2,0},{3,1},{4,6},{5,7},{6,4},{7,5},{8,10},{9,11},{10,... | collective-permute-start | bytes 98312 | tf_op jit(solution)/shard_map/ppermute | solution.py:18
  37.7 0.3 collective-permute-start.11
  38.1 0.5 %bitcast_add_fusion = f32[32]{0:T(128)} fusion(f32[32]{0:T(128)S(1)} %multiply_reduce_fusion, f32[1,128]{1,0:T(1,128)S(1)} %add.18), kind=kLoop, calls=%fused_computation.3 | loop fusion | flops 32 | bytes 384 | tf_op jit(solution)/shard_map/add | solution.py:292
  38.6 0.0 collective-permute-done.9
  38.6 1.6 %collective-permute-done.10 = bf16[16,1024]{1,0:T(8,128)(2,1)S(1)} collective-permute-done((bf16[16,1024]{1,0:T(8,128)(2,1)S(1)}, bf16[16,1024]{1,0:T(8,128)(2,1)S(1)}, u32[]{:S(2)}, u32[]{:S(2)}) %collective-permute-start.10) | collective-permute-done | bytes 32800 | tf_op jit(solution)/shard_map/ppermute | solution.py:18
  40.1 0.9 %collective-permute-done.11 = bf16[16,1024]{1,0:T(8,128)(2,1)S(1)} collective-permute-done((bf16[16,1024]{1,0:T(8,128)(2,1)S(1)}, bf16[16,1024]{1,0:T(8,128)(2,1)S(1)}, u32[]{:S(2)}, u32[]{:S(2)}) %collective-permute-start.11) | collective-permute-done | bytes 32800 | tf_op jit(solution)/shard_map/ppermute | solution.py:18
  41.1 0.6 %add_convert_fusion = bf16[16,1024]{1,0:T(8,128)(2,1)} fusion(bf16[16,1024]{1,0:T(8,128)(2,1)S(1)} %collective-permute-done.11, bf16[16,1024]{1,0:T(8,128)(2,1)S(1)} %collective-permute-done.10, bf16[16,1024]{1,0:T(8,128)(2,1)S(1)} %collective-permute-done.9, bf16[16,1024]{1,0:T(8,128)(2,1)S(1)} %get-tuple-element.22), kind=kLoop, calls=%fused_computation.1 | loop fusion | flops 131072 | bytes 163840 | tf_op jit(solution)/shard_map/convert_element_type | solution.py:293
  (3 shorter events, 0.0 us)
Async XLA Ops:
  0.6 30.5 %copy-start = (s32[16,32]{1,0:T(8,128)S(1)}, s32[16,32]{1,0:T(8,128)}, u32[]{:S(2)}) copy-start(s32[16,32]{1,0:T(8,128)} %param.8) | copy-start | bytes 6148
  1.6 5.7 %collective-permute-start.2 = (bf16[16,1280]{1,0:T(8,128)(2,1)S(1)}, bf16[16,1280]{1,0:T(8,128)(2,1)S(1)}, u32[]{:S(2)}, u32[]{:S(2)}) collective-permute-start(bf16[16,1280]{1,0:T(8,128)(2,1)S(1)} %payload.1._.single_ref), channel_id=1, source_target_pairs={{0,8},{4,12},{8,0},{12,4},{16,24},{20,28},{24,16},{28,20},{1,9},{5... | collective-permute-start | bytes 122888 | tf_op jit(solution)/shard_map/ppermute | solution.py:18
  4.7 5.7 %collective-permute-start.1 = (bf16[16,1280]{1,0:T(8,128)(2,1)S(1)}, bf16[16,1280]{1,0:T(8,128)(2,1)S(1)}, u32[]{:S(2)}, u32[]{:S(2)}) collective-permute-start(bf16[16,1280]{1,0:T(8,128)(2,1)S(1)} %payload.1._.single_ref), channel_id=1, source_target_pairs={{0,16},{4,20},{8,24},{12,28},{16,0},{20,4},{24,8},{28,12},{1,17},{... | collective-permute-start | bytes 122888 | tf_op jit(solution)/shard_map/ppermute | solution.py:18
  7.3 5.8 %collective-permute-start = (bf16[16,1280]{1,0:T(8,128)(2,1)S(1)}, bf16[16,1280]{1,0:T(8,128)(2,1)S(1)}, u32[]{:S(2)}, u32[]{:S(2)}) collective-permute-start(bf16[16,1280]{1,0:T(8,128)(2,1)S(1)} %payload.1._.single_ref), channel_id=1, source_target_pairs={{0,24},{4,28},{8,16},{12,20},{16,8},{20,12},{24,0},{28,4},{1,25},{... | collective-permute-start | bytes 122888 | tf_op jit(solution)/shard_map/ppermute | solution.py:18
  13.1 5.6 %collective-permute-start.4 = (bf16[3,16,1280]{2,1,0:T(8,128)(2,1)S(1)}, bf16[3,16,1280]{2,1,0:T(8,128)(2,1)S(1)}, u32[]{:S(2)}, u32[]{:S(2)}) collective-permute-start(bf16[3,16,1280]{2,1,0:T(8,128)(2,1)S(1)} %pad_maximum_fusion.several_ref), channel_id=1, source_target_pairs={{0,4},{4,0},{8,12},{12,8},{16,20},{20,16},{24,28},{28,24},{1,5},{5... | collective-permute-start | bytes 368648 | tf_op jit(solution)/shard_map/ppermute | solution.py:18
  14.7 4.0 %collective-permute-start.3 = (bf16[16,1280]{1,0:T(8,128)(2,1)S(1)}, bf16[16,1280]{1,0:T(8,128)(2,1)S(1)}, u32[]{:S(2)}, u32[]{:S(2)}) collective-permute-start(bf16[16,1280]{1,0:T(8,128)(2,1)S(1)} %payload.1._.single_ref), channel_id=1, source_target_pairs={{0,4},{4,0},{8,12},{12,8},{16,20},{20,16},{24,28},{28,24},{1,5},{5... | collective-permute-start | bytes 122888 | tf_op jit(solution)/shard_map/ppermute | solution.py:18
  20.9 5.2 %collective-permute-start.5 = (bf16[4,16,1152]{2,1,0:T(8,128)(2,1)S(1)}, bf16[4,16,1152]{2,1,0:T(8,128)(2,1)S(1)}, u32[]{:S(2)}, u32[]{:S(2)}) collective-permute-start(bf16[4,16,1152]{2,1,0:T(8,128)(2,1)S(1)} %get-tuple-element.16._), channel_id=1, source_target_pairs={{0,4},{4,0},{8,12},{12,8},{16,20},{20,16},{24,28},{28,24},{1,5},{5... | collective-permute-start | bytes 442376 | tf_op jit(solution)/shard_map/ppermute | solution.py:18
  26.7 8.0 %collective-permute-start.6 = (bf16[16,1152]{1,0:T(8,128)(2,1)S(1)}, bf16[16,1152]{1,0:T(8,128)(2,1)S(1)}, u32[]{:S(2)}, u32[]{:S(2)}) collective-permute-start(bf16[16,1152]{1,0:T(8,128)(2,1)S(1)} %get-tuple-element.18), channel_id=1, source_target_pairs={{0,24},{4,28},{8,16},{12,20},{16,8},{20,12},{24,0},{28,4},{1,25},{... | collective-permute-start | bytes 110600 | tf_op jit(solution)/shard_map/ppermute | solution.py:18
  27.3 7.4 %collective-permute-start.7 = (bf16[16,1152]{1,0:T(8,128)(2,1)S(1)}, bf16[16,1152]{1,0:T(8,128)(2,1)S(1)}, u32[]{:S(2)}, u32[]{:S(2)}) collective-permute-start(bf16[16,1152]{1,0:T(8,128)(2,1)S(1)} %get-tuple-element.19), channel_id=1, source_target_pairs={{0,16},{4,20},{8,24},{12,28},{16,0},{20,4},{24,8},{28,12},{1,17},{... | collective-permute-start | bytes 110600 | tf_op jit(solution)/shard_map/ppermute | solution.py:18
  27.3 7.4 %collective-permute-start.8 = (bf16[16,1152]{1,0:T(8,128)(2,1)S(1)}, bf16[16,1152]{1,0:T(8,128)(2,1)S(1)}, u32[]{:S(2)}, u32[]{:S(2)}) collective-permute-start(bf16[16,1152]{1,0:T(8,128)(2,1)S(1)} %get-tuple-element.20), channel_id=1, source_target_pairs={{0,8},{4,12},{8,0},{12,4},{16,24},{20,28},{24,16},{28,20},{1,9},{5... | collective-permute-start | bytes 110600 | tf_op jit(solution)/shard_map/ppermute | solution.py:18
  36.2 2.4 %collective-permute-start.9 = (bf16[16,1024]{1,0:T(8,128)(2,1)S(1)}, bf16[16,1024]{1,0:T(8,128)(2,1)S(1)}, u32[]{:S(2)}, u32[]{:S(2)}) collective-permute-start(bf16[16,1024]{1,0:T(8,128)(2,1)S(1)} %get-tuple-element.23), channel_id=1, source_target_pairs={{0,1},{1,0},{2,3},{3,2},{4,5},{5,4},{6,7},{7,6},{8,9},{9,8},{10,11... | collective-permute-start | bytes 98312 | tf_op jit(solution)/shard_map/ppermute | solution.py:18
  36.2 4.0 %collective-permute-start.10 = (bf16[16,1024]{1,0:T(8,128)(2,1)S(1)}, bf16[16,1024]{1,0:T(8,128)(2,1)S(1)}, u32[]{:S(2)}, u32[]{:S(2)}) collective-permute-start(bf16[16,1024]{1,0:T(8,128)(2,1)S(1)} %get-tuple-element.24), channel_id=1, source_target_pairs={{0,2},{1,3},{2,0},{3,1},{4,6},{5,7},{6,4},{7,5},{8,10},{9,11},{10,... | collective-permute-start | bytes 98312 | tf_op jit(solution)/shard_map/ppermute | solution.py:18
  37.7 3.3 %collective-permute-start.11 = (bf16[16,1024]{1,0:T(8,128)(2,1)S(1)}, bf16[16,1024]{1,0:T(8,128)(2,1)S(1)}, u32[]{:S(2)}, u32[]{:S(2)}) collective-permute-start(bf16[16,1024]{1,0:T(8,128)(2,1)S(1)} %get-tuple-element.25), channel_id=1, source_target_pairs={{0,3},{1,2},{2,1},{3,0},{4,7},{5,6},{6,5},{7,4},{8,11},{9,10},{10,... | collective-permute-start | bytes 98312 | tf_op jit(solution)/shard_map/ppermute | solution.py:18

commit v2 on v1

v2 whole, which is shorter than its diff:
```python
import functools
import math

import jax
import jax.numpy as jnp
from jax import lax
from jax.experimental import pallas as pl
from jax.experimental.pallas import tpu as pltpu
from jax.sharding import PartitionSpec as P


MASKED = -1e30
LANES = 128


def exchange(value, axis, step):
    count = lax.axis_size(axis)
    return lax.ppermute(value, axis, [(i, i ^ step) for i in range(count)])


def even_steps(count):
    half = count // 2
    return [half] + [k for k in range(count - 2, 0, -2) if k != half]


def split_stats(stats, heads):
    high = stats.astype(jnp.bfloat16).astype(jnp.float32)
    rest = stats - high
    middle = rest.astype(jnp.bfloat16).astype(jnp.float32)
    low = rest - middle
    packed = high + pltpu.roll(middle, 2 * heads, 1) + pltpu.roll(low, 4 * heads, 1)
    return packed.astype(jnp.bfloat16)


def join_stats(packed, heads):
    packed = packed.astype(jnp.float32)
    return (
        packed
        + pltpu.roll(packed, LANES - 2 * heads, 1)
        + pltpu.roll(packed, LANES - 4 * heads, 1)
    )


def merge_partials(messages, heads, width):
    depth = width // heads
    scale = depth**-0.5 * math.log2(math.e)
    stats = [join_stats(m[:, width:], heads) for m in messages]
    lane = lax.broadcasted_iota(jnp.int32, stats[0].shape, 1)
    highest = functools.reduce(jnp.maximum, stats)
    factors = [jnp.where(lane < heads, jnp.exp2((s - highest) * scale), 0.0) for s in stats]
    total = sum(f * pltpu.roll(s, LANES - heads, 1) for f, s in zip(factors, stats))
    return highest, total, factors, lane


def weighted_sums(messages, factors, heads, depth):
    for h in range(heads):
        acc = None
        for f, m in zip(factors, messages):
            term = f[:, h : h + 1] * m[:, h * depth : (h + 1) * depth].astype(jnp.float32)
            acc = term if acc is None else acc + term
        yield h, acc.astype(jnp.bfloat16)


def payload_kernel(
    queries_hbm, selected_hbm, out_ref, queries_ref, selected_ref, sems, *, owners, all_blocks
):
    copies = [
        pltpu.make_async_copy(selected_hbm, selected_ref, sems.at[0]),
        pltpu.make_async_copy(queries_hbm, queries_ref, sems.at[1]),
    ]
    for copy in copies:
        copy.start()
    rows, heads, depth = queries_ref.shape
    width = heads * depth
    blocks = all_blocks // owners
    copies[0].wait()
    chosen = selected_ref[...]
    owner = jnp.zeros(chosen.shape, jnp.int32)
    for m in range(1, owners):
        owner = owner + (chosen >= m * blocks).astype(jnp.int32)
    local = chosen - owner * blocks
    fill = jnp.full((rows, LANES - 2 * chosen.shape[1]), -1, jnp.int32)
    tags = jnp.concatenate([owner, local, fill], axis=1)
    out_ref[:, width:] = tags.astype(jnp.float32).astype(jnp.bfloat16)
    copies[1].wait()
    for h in range(heads):
        out_ref[:, h * depth : (h + 1) * depth] = queries_ref[:, h, :]


def stage_kernel(source_hbm, _, out_ref, sem):
    copy = pltpu.make_async_copy(source_hbm, out_ref, sem)
    copy.start()
    copy.wait()


def stage_columns_kernel(weight_hbm, _, *refs, steps):
    outs = refs[:-1]
    me = lax.axis_index("head")
    columns = outs[0].shape[1]
    copies = []
    for i, (k, out) in enumerate(zip(steps, outs)):
        at = pl.multiple_of((me ^ k) * columns, columns)
        copies.append(
            pltpu.make_async_copy(weight_hbm.at[:, pl.ds(at, columns)], out, refs[-1].at[i])
        )
    for copy in copies:
        copy.start()
    for copy in copies:
        copy.wait()


def attend_kernel(
    single_ref, several_ref, cache_ref, first_ref, others_ref, hits_ref, *, heads, picks
):
    blocks, _, heads_kv, tokens, depth = cache_ref.shape
    width = heads * depth
    rows_each = single_ref.shape[0]
    group_q = heads // heads_kv
    scale = depth**-0.5 * math.log2(math.e)
    payloads = [single_ref] + [several_ref.at[i] for i in range(several_ref.shape[0])]
    messages = [first_ref] + [others_ref.at[i] for i in range(others_ref.shape[0])]
    me = lax.axis_index("mem").astype(jnp.float32)
    span = blocks * tokens
    fence = jnp.where(
        lax.broadcasted_iota(jnp.int32, (span, LANES), 0) // tokens
        == lax.broadcasted_iota(jnp.int32, (span, LANES), 1),
        MASKED,
        0.0,
    ).astype(jnp.bfloat16)
    hits = jnp.zeros((1, LANES), jnp.float32)
    batch = min(len(payloads), 8)
    rows = batch * rows_each
    pair = math.gcd(group_q, max(1, 256 // rows))
    lane = lax.broadcasted_iota(jnp.int32, (rows, LANES), 1)
    blocked = []
    for start in range(0, len(payloads), batch):
        tags = jnp.concatenate([p[:, width:] for p in payloads[start : start + batch]], axis=0)
        tags = tags.astype(jnp.float32)
        local = jnp.where(tags == me, pltpu.roll(tags, LANES - picks, 1), -1.0)
        chosen = jnp.zeros((rows, LANES), jnp.float32)
        for i in range(picks):
            chosen = jnp.where(local[:, i : i + 1] == lane.astype(jnp.float32), 1.0, chosen)
        hits = hits + jnp.sum(chosen, axis=0, keepdims=True)
        blocked.append((1.0 - chosen).astype(jnp.bfloat16))
    hits_ref[...] = hits

    def scores_of(start, kv, first_head):
        part = payloads[start : start + batch]
        keys = jnp.concatenate([cache_ref[:, 0, kv].reshape(span, depth), fence], axis=1)
        stacked = []
        for h in range(first_head, first_head + pair):
            query = jnp.concatenate([p[:, h * depth : (h + 1) * depth] for p in part], axis=0)
            stacked.append(jnp.concatenate([query, blocked[start // batch]], axis=1))
        query = jnp.concatenate(stacked, axis=0)
        return lax.dot_general(
            query, keys, (((1,), (1,)), ((), ())), preferred_element_type=jnp.float32
        )

    units = [
        (start, kv, first_head)
        for start in range(0, len(payloads), batch)
        for kv in range(heads_kv)
        for first_head in range(kv * group_q, (kv + 1) * group_q, pair)
    ]
    ahead = scores_of(*units[0])
    stats = None
    for n, (start, kv, first_head) in enumerate(units):
        scores = ahead
        if n + 1 < len(units):
            ahead = scores_of(*units[n + 1])
        values = cache_ref[:, 1, kv].reshape(span, depth)
        values = jnp.concatenate([values, jnp.ones((span, LANES), jnp.bfloat16)], axis=1)
        peak = jnp.max(scores, axis=1, keepdims=True)
        weights = jnp.exp2((scores - peak) * scale).astype(jnp.bfloat16)
        sums = jnp.dot(weights, values, preferred_element_type=jnp.float32)
        out = sums[:, :depth].astype(jnp.bfloat16)
        total = sums[:, depth : depth + 1]
        if first_head == 0:
            stats = jnp.zeros((rows, LANES), jnp.float32)
        for j in range(pair):
            h = first_head + j
            for i in range(batch):
                at = j * rows + i * rows_each
                messages[start + i][:, h * depth : (h + 1) * depth] = out[at : at + rows_each]
            stats = jnp.where(lane == h, peak[j * rows : (j + 1) * rows], stats)
            stats = jnp.where(lane == heads + h, total[j * rows : (j + 1) * rows], stats)
        if first_head + pair == heads:
            packed = split_stats(stats, heads)
            for i in range(batch):
                messages[start + i][:, width:] = packed[i * rows_each : (i + 1) * rows_each]


def merge_kernel(mine_ref, theirs_ref, *outs, heads):
    width = mine_ref.shape[2] - LANES
    depth = width // heads
    for i, out in enumerate(outs):
        pair = [mine_ref.at[i], theirs_ref.at[i]]
        highest, total, factors, lane = merge_partials(pair, heads, width)
        for h, merged in weighted_sums(pair, factors, heads, depth):
            out[:, h * depth : (h + 1) * depth] = merged
        stats = jnp.where(lane < heads, highest, pltpu.roll(total, heads, 1))
        stats = jnp.where(lane < 2 * heads, stats, 0.0)
        out[:, width:] = split_stats(stats, heads)


def project(attended, weights, outs):
    for weight_ref, out in zip(weights, outs):
        out[...] = jnp.dot(
            attended, weight_ref[...], preferred_element_type=jnp.float32
        ).astype(jnp.bfloat16)


def project_far_kernel(*refs, sources, parts, heads):
    messages = refs[:sources]
    weights = refs[sources : sources + parts]
    attended_ref = refs[sources + parts]
    width = attended_ref.shape[1]
    depth = width // heads
    _, total, factors, lane = merge_partials(messages, heads, width)
    inverse = 1.0 / jnp.where(lane < heads, total, 1.0)
    factors = [f * inverse for f in factors]
    attended = jnp.concatenate(
        [a for _, a in weighted_sums(messages, factors, heads, depth)], axis=1
    )
    attended_ref[...] = attended
    project(attended, weights, refs[sources + parts + 1 :])


def project_near_kernel(attended_ref, *refs):
    parts = len(refs) // 2
    project(attended_ref[...], refs[:parts], refs[parts:])


def per_device(queries, cache_blocks, selected, counts, output_weight):
    devices_mem = lax.axis_size("mem")
    devices_head = lax.axis_size("head")
    rows, heads, depth = queries.shape
    blocks = cache_blocks.shape[0]
    picks = selected.shape[1]
    width = heads * depth
    message = jax.ShapeDtypeStruct((rows, width + LANES), jnp.bfloat16)
    vmem = pl.BlockSpec(memory_space=pltpu.VMEM)
    hbm = pl.BlockSpec(memory_space=pltpu.HBM)
    keep = functools.partial(pltpu.with_memory_space_constraint, memory_space=pltpu.HBM)
    payload = pl.pallas_call(
        functools.partial(
            payload_kernel, owners=devices_mem, all_blocks=devices_mem * blocks
        ),
        in_specs=[hbm] * 2,
        out_specs=vmem,
        out_shape=message,
        scratch_shapes=[
            pltpu.VMEM(queries.shape, queries.dtype),
            pltpu.VMEM(selected.shape, selected.dtype),
            pltpu.SemaphoreType.DMA((2,)),
        ],
        compiler_params=pltpu.CompilerParams(vmem_limit_bytes=4 * 2**20),
        name="payload",
    )(keep(queries), keep(selected))

    def call(kernel, operands, specs, shapes, limit, scratch=()):
        return pl.pallas_call(
            kernel,
            in_specs=specs,
            out_specs=[vmem] * len(shapes),
            out_shape=shapes,
            scratch_shapes=list(scratch),
            compiler_params=pltpu.CompilerParams(vmem_limit_bytes=limit * 2**20),
        )(*operands)

    def stage(array, after):
        shape = jax.ShapeDtypeStruct(array.shape, array.dtype)
        operands = (keep(array), after)
        sem = [pltpu.SemaphoreType.DMA(())]
        return call(stage_kernel, operands, [hbm, vmem], [shape], 4, sem)[0]

    even = even_steps(devices_mem)
    straight = jnp.stack([exchange(payload, "mem", k) for k in even])
    near = exchange(payload, "mem", 1)
    cache_blocks = stage(cache_blocks, payload)
    forwarded = exchange(straight, "mem", 1)
    several = jax.ShapeDtypeStruct(straight.shape, straight.dtype)
    hits = jax.ShapeDtypeStruct((1, LANES), jnp.float32)
    attend = functools.partial(attend_kernel, heads=heads, picks=picks)
    own, mine, hits_a = call(
        attend, (payload, straight, cache_blocks), [vmem] * 3, [message, several, hits], 24
    )
    beside, theirs, hits_b = call(
        attend, (near, forwarded, cache_blocks), [vmem] * 3, [message, several, hits], 24
    )
    crossed = exchange(theirs, "mem", 1)
    far_steps = tuple(range(devices_head - 1, 1, -1))
    near_steps = (1, 0)
    columns = output_weight.shape[1] // devices_head
    part = jax.ShapeDtypeStruct((output_weight.shape[0], columns), output_weight.dtype)

    def stage_columns(steps, after):
        return call(
            functools.partial(stage_columns_kernel, steps=steps),
            (keep(output_weight), after),
            [hbm, vmem],
            [part] * len(steps),
            4,
            [pltpu.SemaphoreType.DMA((len(steps),))],
        )

    weight_far = stage_columns(far_steps, theirs)
    merged = call(
        functools.partial(merge_kernel, heads=heads),
        (mine, crossed),
        [vmem] * 2,
        [message] * len(even),
        8,
    )
    returned = [own] + [exchange(m, "mem", k) for k, m in zip(even, merged)]
    returned.append(exchange(beside, "mem", 1))
    weight_near = stage_columns(near_steps, merged[0])
    share = jax.ShapeDtypeStruct((rows, columns), jnp.bfloat16)
    attended, *far = call(
        functools.partial(
            project_far_kernel, sources=len(returned), parts=len(far_steps), heads=heads
        ),
        (*returned, *weight_far),
        [vmem] * (len(returned) + len(far_steps)),
        [jax.ShapeDtypeStruct((rows, width), jnp.bfloat16)] + [share] * len(far_steps),
        16,
    )
    arrived = {k: exchange(s, "head", k) for k, s in zip(far_steps, far)}
    beside, own = call(project_near_kernel, (attended, *weight_near), [vmem] * 3, [share] * 2, 16)
    arrived[1] = exchange(beside, "head", 1)
    layer_out = own.astype(jnp.float32)
    for k in range(1, devices_head):
        layer_out = layer_out + arrived[k].astype(jnp.float32)
    decays = 0.5 ** jnp.arange(counts.shape[0], dtype=jnp.float32)
    block_heat = jnp.sum(decays[:, None] * counts.astype(jnp.float32), axis=0) + (hits_a + hits_b)[0, :blocks]
    return (layer_out.astype(jnp.bfloat16), block_heat)


def solution(mesh):
    return jax.shard_map(
        per_device,
        mesh=mesh,
        in_specs=(
            P("mem", "head", None),
            P("mem", None, "head", None, None),
            P("mem", None),
            P(None, "mem"),
            P("head", None),
        ),
        out_specs=(P("mem", "head"), P("mem")),
        check_vma=False,
    )
```

time: 42 us -> 39.5 us (0.940)
  waiting for transfers between devices: 11.8 us -> 9.21 us
    ppermute x12 -> x13, waiting for transfers between devices: 11.8 us -> 9.21 us  [exchange(): return lax.ppermute(value, axis, [(i, i ^ step) for i in range(count)])]
    pallas_call x7 -> x8, Pallas kernels: 11.5 us -> 11.9 us  [call(): pl.pallas_call(kernel, in_specs=specs, out_specs=[vmem] * len(shapes), ou...]
    ppermute x12 -> x13, starting transfers between devices: 15.5 us -> 15.4 us  [exchange(): return lax.ppermute(value, axis, [(i, i ^ step) for i in range(count)])]
  transfers between devices with their start and end apart: 12 -> 13, of which waited for: 6 -> 6; matrix products, arithmetic and copies ran while one was open for 1% -> 2% of each run, Pallas kernels for 17% -> 21%
where the time goes in v2:
time: 39.5 us; the launch traced here: 39.3 us
  starting transfers between devices  15.4 us (39%)
  Pallas kernels  12.7 us (32%)
  waiting for transfers between devices  9.21 us (23%)
  other arithmetic  1.26 us (3%)
  between operations  0.74 us (2%)
    ppermute x13, starting transfers between devices, exchange(): return lax.ppermute(value, axis, [(i, i ^ step) for i in range(count)])  15.4 us
    pallas_call x8, Pallas kernels, call(): pl.pallas_call(kernel, in_specs=specs, out_specs=[vmem] * len(shapes), ou...  11.9 us
    ppermute x13, waiting for transfers between devices, exchange(): return lax.ppermute(value, axis, [(i, i ^ step) for i in range(count)])  9.21 us
    pallas_call x1, Pallas kernels, per_device(): pl.pallas_call(functools.partial(payload_kernel, owners=devices_mem, all_...  0.84 us
  transfers between devices with their start and end apart: 13, of which 6 were waited for; matrix products, arithmetic and copies ran while one was open for 2% of the time, Pallas kernels for 21%

profile of v2, /device:TPU:0, one launch (start us, length us, event | category | flops | bytes accessed | tf_op | source)
XLA Modules:
  0.0 39.3 jit_solution(8333121547113155283)
XLA Ops:
  0.6 0.8 %payload.1._.single_ref = bf16[16,1152]{1,0:T(8,128)(2,1)S(1)} custom-call(bf16[16,8,128]{2,1,0:T(8,128)(2,1)} %queries_hbm.1, s32[16,32]{1,0:T(8,128)} %selected_hbm.1), custom_call_target="tpu_custom_call" | custom-call | tf_op jit(solution)/shard_map/payload/pallas_call | solution.py:245
  1.5 4.1 %collective-permute-start = (bf16[16,1152]{1,0:T(8,128)(2,1)S(1)}, bf16[16,1152]{1,0:T(8,128)(2,1)S(1)}, u32[]{:S(2)}, u32[]{:S(2)}) collective-permute-start(bf16[16,1152]{1,0:T(8,128)(2,1)S(1)} %payload.1._.single_ref), channel_id=1, source_target_pairs={{0,16},{4,20},{8,24},{12,28},{16,0},{20,4},{24,8},{28,12},{1,17},{... | collective-permute-start | bytes 110600 | tf_op jit(solution)/shard_map/ppermute | solution.py:18
  5.6 1.3 %collective-permute-start.1 = (bf16[16,1152]{1,0:T(8,128)(2,1)S(1)}, bf16[16,1152]{1,0:T(8,128)(2,1)S(1)}, u32[]{:S(2)}, u32[]{:S(2)}) collective-permute-start(bf16[16,1152]{1,0:T(8,128)(2,1)S(1)} %payload.1._.single_ref), channel_id=1, source_target_pairs={{0,24},{4,28},{8,16},{12,20},{16,8},{20,12},{24,0},{28,4},{1,25},{... | collective-permute-start | bytes 110600 | tf_op jit(solution)/shard_map/ppermute | solution.py:18
  7.0 0.2 collective-permute-start.2
  7.2 0.8 %collective-permute-done = bf16[16,1152]{1,0:T(8,128)(2,1)S(1)} collective-permute-done((bf16[16,1152]{1,0:T(8,128)(2,1)S(1)}, bf16[16,1152]{1,0:T(8,128)(2,1)S(1)}, u32[]{:S(2)}, u32[]{:S(2)}) %collective-permute-start) | collective-permute-done | bytes 36896 | tf_op jit(solution)/shard_map/ppermute | solution.py:18
  7.9 3.4 %collective-permute-done.1 = bf16[16,1152]{1,0:T(8,128)(2,1)S(1)} collective-permute-done((bf16[16,1152]{1,0:T(8,128)(2,1)S(1)}, bf16[16,1152]{1,0:T(8,128)(2,1)S(1)}, u32[]{:S(2)}, u32[]{:S(2)}) %collective-permute-start.1) | collective-permute-done | bytes 36896 | tf_op jit(solution)/shard_map/ppermute | solution.py:18
  11.4 0.0 collective-permute-done.2
  11.4 1.6 %collective-permute-start.4 = (bf16[3,16,1152]{2,1,0:T(8,128)(2,1)S(1)}, bf16[3,16,1152]{2,1,0:T(8,128)(2,1)S(1)}, u32[]{:S(2)}, u32[]{:S(2)}) collective-permute-start(bf16[3,16,1152]{2,1,0:T(8,128)(2,1)S(1)} %pad_maximum_fusion.several_ref), channel_id=1, source_target_pairs={{0,4},{4,0},{8,12},{12,8},{16,20},{20,16},{24,28},{28,24},{1,5},{5... | collective-permute-start | bytes 331784 | tf_op jit(solution)/shard_map/ppermute | solution.py:18
  13.0 0.5 %collective-permute-start.3 = (bf16[16,1152]{1,0:T(8,128)(2,1)S(1)}, bf16[16,1152]{1,0:T(8,128)(2,1)S(1)}, u32[]{:S(2)}, u32[]{:S(2)}) collective-permute-start(bf16[16,1152]{1,0:T(8,128)(2,1)S(1)} %payload.1._.single_ref), channel_id=1, source_target_pairs={{0,4},{4,0},{8,12},{12,8},{16,20},{20,16},{24,28},{28,24},{1,5},{5... | collective-permute-start | bytes 110600 | tf_op jit(solution)/shard_map/ppermute | solution.py:18
  13.5 1.6 %shard_map.68.cache_ref = bf16[32,2,2,64,128]{4,3,2,1,0:T(8,128)(2,1)S(1)} custom-call(bf16[32,2,2,64,128]{4,3,2,1,0:T(8,128)(2,1)} %source_hbm.1, bf16[16,1152]{1,0:T(8,128)(2,1)S(1)} %payload.1._.single_ref), custom_call_target="tpu_custom_call" | custom-call | tf_op jit(solution)/shard_map/pallas_call | solution.py:262
  15.1 0.0 copy-start
  15.1 1.8 %collective-permute-done.3.single_ref = bf16[16,1152]{1,0:T(8,128)(2,1)S(1)} collective-permute-done((bf16[16,1152]{1,0:T(8,128)(2,1)S(1)}, bf16[16,1152]{1,0:T(8,128)(2,1)S(1)}, u32[]{:S(2)}, u32[]{:S(2)}) %collective-permute-start.3) | collective-permute-done | bytes 36896 | tf_op jit(solution)/shard_map/ppermute | solution.py:18
  16.9 0.0 collective-permute-done.4.several_ref
  16.9 1.9 %shard_map.70 = (bf16[16,1152]{1,0:T(8,128)(2,1)S(1)}, bf16[3,16,1152]{2,1,0:T(8,128)(2,1)S(1)}, f32[1,128]{1,0:T(1,128)S(1)}) custom-call(bf16[16,1152]{1,0:T(8,128)(2,1)S(1)} %collective-permute-done.3.single_ref, bf16[3,16,1152]{2,1,0:T(8,128)(2,1)S(1)} %collective-permute-done.4.several_ref, bf16[32,2,2,64,128]{4,3,2,1,0:T(8,128)(2,1)S(1)} %shard_map.68.cache_ref), custom_call_target="tpu_custom_call" | custom-call | tf_op jit(solution)/shard_map/pallas_call | solution.py:262
  18.9 1.3 %collective-permute-start.5 = (bf16[3,16,1152]{2,1,0:T(8,128)(2,1)S(1)}, bf16[3,16,1152]{2,1,0:T(8,128)(2,1)S(1)}, u32[]{:S(2)}, u32[]{:S(2)}) collective-permute-start(bf16[3,16,1152]{2,1,0:T(8,128)(2,1)S(1)} %get-tuple-element.22._), channel_id=1, source_target_pairs={{0,4},{4,0},{8,12},{12,8},{16,20},{20,16},{24,28},{28,24},{1,5},{5... | collective-permute-start | bytes 331784 | tf_op jit(solution)/shard_map/ppermute | solution.py:18
  20.1 1.9 %shard_map.69 = (bf16[16,1152]{1,0:T(8,128)(2,1)S(1)}, bf16[3,16,1152]{2,1,0:T(8,128)(2,1)S(1)}, f32[1,128]{1,0:T(1,128)S(1)}) custom-call(bf16[16,1152]{1,0:T(8,128)(2,1)S(1)} %payload.1._.single_ref, bf16[3,16,1152]{2,1,0:T(8,128)(2,1)S(1)} %pad_maximum_fusion.several_ref, bf16[32,2,2,64,128]{4,3,2,1,0:T(8,128)(2,1)S(1)} %shard_map.68.cache_ref), custom_call_target="tpu_custom_call" | custom-call | tf_op jit(solution)/shard_map/pallas_call | solution.py:262
  22.1 0.9 %collective-permute-start.9 = (bf16[16,1152]{1,0:T(8,128)(2,1)S(1)}, bf16[16,1152]{1,0:T(8,128)(2,1)S(1)}, u32[]{:S(2)}, u32[]{:S(2)}) collective-permute-start(bf16[16,1152]{1,0:T(8,128)(2,1)S(1)} %get-tuple-element.26), channel_id=1, source_target_pairs={{0,4},{4,0},{8,12},{12,8},{16,20},{20,16},{24,28},{28,24},{1,5},{5... | collective-permute-start | bytes 110600 | tf_op jit(solution)/shard_map/ppermute | solution.py:18
  23.0 0.7 %collective-permute-done.5.theirs_ref = bf16[3,16,1152]{2,1,0:T(8,128)(2,1)S(1)} collective-permute-done((bf16[3,16,1152]{2,1,0:T(8,128)(2,1)S(1)}, bf16[3,16,1152]{2,1,0:T(8,128)(2,1)S(1)}, u32[]{:S(2)}, u32[]{:S(2)}) %collective-permute-start.5) | collective-permute-done | bytes 110624 | tf_op jit(solution)/shard_map/ppermute | solution.py:18
  23.7 0.4 shard_map.71
  24.0 1.3 %collective-permute-start.6 = (bf16[16,1152]{1,0:T(8,128)(2,1)S(1)}, bf16[16,1152]{1,0:T(8,128)(2,1)S(1)}, u32[]{:S(2)}, u32[]{:S(2)}) collective-permute-start(bf16[16,1152]{1,0:T(8,128)(2,1)S(1)} %get-tuple-element.23._), channel_id=1, source_target_pairs={{0,16},{4,20},{8,24},{12,28},{16,0},{20,4},{24,8},{28,12},{1,17},{... | collective-permute-start | bytes 110600 | tf_op jit(solution)/shard_map/ppermute | solution.py:18
  25.3 1.1 %collective-permute-start.7 = (bf16[16,1152]{1,0:T(8,128)(2,1)S(1)}, bf16[16,1152]{1,0:T(8,128)(2,1)S(1)}, u32[]{:S(2)}, u32[]{:S(2)}) collective-permute-start(bf16[16,1152]{1,0:T(8,128)(2,1)S(1)} %get-tuple-element.24), channel_id=1, source_target_pairs={{0,24},{4,28},{8,16},{12,20},{16,8},{20,12},{24,0},{28,4},{1,25},{... | collective-permute-start | bytes 110600 | tf_op jit(solution)/shard_map/ppermute | solution.py:18
  26.4 1.1 %collective-permute-start.8 = (bf16[16,1152]{1,0:T(8,128)(2,1)S(1)}, bf16[16,1152]{1,0:T(8,128)(2,1)S(1)}, u32[]{:S(2)}, u32[]{:S(2)}) collective-permute-start(bf16[16,1152]{1,0:T(8,128)(2,1)S(1)} %get-tuple-element.25), channel_id=1, source_target_pairs={{0,8},{4,12},{8,0},{12,4},{16,24},{20,28},{24,16},{28,20},{1,9},{5... | collective-permute-start | bytes 110600 | tf_op jit(solution)/shard_map/ppermute | solution.py:18
  27.6 0.0 copy-done
  27.6 0.1 multiply_reduce_fusion
  27.7 2.2 %shard_map.72 = (bf16[1024,1024]{1,0:T(8,128)(2,1)S(1)}, bf16[1024,1024]{1,0:T(8,128)(2,1)S(1)}) custom-call(bf16[1024,4096]{1,0:T(8,128)(2,1)} %weight_hbm.3, bf16[3,16,1152]{2,1,0:T(8,128)(2,1)S(1)} %get-tuple-element.22._), custom_call_target="tpu_custom_call" | custom-call | tf_op jit(solution)/shard_map/pallas_call | solution.py:262
  29.9 2.3 %shard_map.74 = (bf16[1024,1024]{1,0:T(8,128)(2,1)S(1)}, bf16[1024,1024]{1,0:T(8,128)(2,1)S(1)}) custom-call(bf16[1024,4096]{1,0:T(8,128)(2,1)} %weight_hbm.3, bf16[16,1152]{1,0:T(8,128)(2,1)S(1)} %get-tuple-element.23._), custom_call_target="tpu_custom_call" | custom-call | tf_op jit(solution)/shard_map/pallas_call | solution.py:262
  32.2 0.0 collective-permute-done.9.refs_4_
  32.2 0.0 collective-permute-done.6.refs_1_
  32.2 0.0 collective-permute-done.7.refs_2_
  32.2 0.0 collective-permute-done.8.refs_3_
  32.2 0.9 %shard_map.73 = (bf16[16,1024]{1,0:T(8,128)(2,1)S(1)}, bf16[16,1024]{1,0:T(8,128)(2,1)S(1)}, bf16[16,1024]{1,0:T(8,128)(2,1)S(1)}) custom-call(bf16[16,1152]{1,0:T(8,128)(2,1)S(1)} %get-tuple-element.20.refs_0_, bf16[16,1152]{1,0:T(8,128)(2,1)S(1)} %collective-permute-done.6.refs_1_, bf16[16,1152]{1,0:T(8,128)(2,1)S(1)} %collective-permute-done.7.refs_2_, ...), custom_call_target="tpu_custom_call" | custom-call | tf_op jit(solution)/shard_map/pallas_call | solution.py:262
  33.1 0.7 %shard_map.75 = (bf16[16,1024]{1,0:T(8,128)(2,1)S(1)}, bf16[16,1024]{1,0:T(8,128)(2,1)S(1)}) custom-call(bf16[16,1024]{1,0:T(8,128)(2,1)S(1)} %get-tuple-element.29.attended_ref, bf16[1024,1024]{1,0:T(8,128)(2,1)S(1)} %get-tuple-element.30.refs_0_, bf16[1024,1024]{1,0:T(8,128)(2,1)S(1)} %get-tuple-element.31.refs_1_), custom_call_target="tpu_custom_call" | custom-call | tf_op jit(solution)/shard_map/pallas_call | solution.py:262
  33.8 0.0 collective-permute-start.10
  33.8 1.6 %collective-permute-start.11 = (bf16[16,1024]{1,0:T(8,128)(2,1)S(1)}, bf16[16,1024]{1,0:T(8,128)(2,1)S(1)}, u32[]{:S(2)}, u32[]{:S(2)}) collective-permute-start(bf16[16,1024]{1,0:T(8,128)(2,1)S(1)} %get-tuple-element.34), channel_id=1, source_target_pairs={{0,2},{1,3},{2,0},{3,1},{4,6},{5,7},{6,4},{7,5},{8,10},{9,11},{10,... | collective-permute-start | bytes 98312 | tf_op jit(solution)/shard_map/ppermute | solution.py:18
  35.3 0.3 collective-permute-start.12
  35.7 0.5 %bitcast_add_fusion = f32[32]{0:T(128)} fusion(f32[32]{0:T(128)S(1)} %multiply_reduce_fusion, f32[1,128]{1,0:T(1,128)S(1)} %add.18), kind=kLoop, calls=%fused_computation.3 | loop fusion | flops 32 | bytes 384 | tf_op jit(solution)/shard_map/add | solution.py:335
  36.2 0.0 collective-permute-done.10
  36.2 1.6 %collective-permute-done.11 = bf16[16,1024]{1,0:T(8,128)(2,1)S(1)} collective-permute-done((bf16[16,1024]{1,0:T(8,128)(2,1)S(1)}, bf16[16,1024]{1,0:T(8,128)(2,1)S(1)}, u32[]{:S(2)}, u32[]{:S(2)}) %collective-permute-start.11) | collective-permute-done | bytes 32800 | tf_op jit(solution)/shard_map/ppermute | solution.py:18
  37.7 0.9 %collective-permute-done.12 = bf16[16,1024]{1,0:T(8,128)(2,1)S(1)} collective-permute-done((bf16[16,1024]{1,0:T(8,128)(2,1)S(1)}, bf16[16,1024]{1,0:T(8,128)(2,1)S(1)}, u32[]{:S(2)}, u32[]{:S(2)}) %collective-permute-start.12) | collective-permute-done | bytes 32800 | tf_op jit(solution)/shard_map/ppermute | solution.py:18
  38.7 0.6 %add_convert_fusion = bf16[16,1024]{1,0:T(8,128)(2,1)} fusion(bf16[16,1024]{1,0:T(8,128)(2,1)S(1)} %collective-permute-done.12, bf16[16,1024]{1,0:T(8,128)(2,1)S(1)} %collective-permute-done.11, bf16[16,1024]{1,0:T(8,128)(2,1)S(1)} %collective-permute-done.10, bf16[16,1024]{1,0:T(8,128)(2,1)S(1)} %get-tuple-element.32), kind=kLoop, calls=%fused_computation.1 | loop fusion | flops 131072 | bytes 163840 | tf_op jit(solution)/shard_map/convert_element_type | solution.py:336
  (3 shorter events, 0.0 us)
Async XLA Ops:
  1.5 6.5 %collective-permute-start = (bf16[16,1152]{1,0:T(8,128)(2,1)S(1)}, bf16[16,1152]{1,0:T(8,128)(2,1)S(1)}, u32[]{:S(2)}, u32[]{:S(2)}) collective-permute-start(bf16[16,1152]{1,0:T(8,128)(2,1)S(1)} %payload.1._.single_ref), channel_id=1, source_target_pairs={{0,16},{4,20},{8,24},{12,28},{16,0},{20,4},{24,8},{28,12},{1,17},{... | collective-permute-start | bytes 110600 | tf_op jit(solution)/shard_map/ppermute | solution.py:18
  5.6 5.8 %collective-permute-start.1 = (bf16[16,1152]{1,0:T(8,128)(2,1)S(1)}, bf16[16,1152]{1,0:T(8,128)(2,1)S(1)}, u32[]{:S(2)}, u32[]{:S(2)}) collective-permute-start(bf16[16,1152]{1,0:T(8,128)(2,1)S(1)} %payload.1._.single_ref), channel_id=1, source_target_pairs={{0,24},{4,28},{8,16},{12,20},{16,8},{20,12},{24,0},{28,4},{1,25},{... | collective-permute-start | bytes 110600 | tf_op jit(solution)/shard_map/ppermute | solution.py:18
  7.0 4.4 %collective-permute-start.2 = (bf16[16,1152]{1,0:T(8,128)(2,1)S(1)}, bf16[16,1152]{1,0:T(8,128)(2,1)S(1)}, u32[]{:S(2)}, u32[]{:S(2)}) collective-permute-start(bf16[16,1152]{1,0:T(8,128)(2,1)S(1)} %payload.1._.single_ref), channel_id=1, source_target_pairs={{0,8},{4,12},{8,0},{12,4},{16,24},{20,28},{24,16},{28,20},{1,9},{5... | collective-permute-start | bytes 110600 | tf_op jit(solution)/shard_map/ppermute | solution.py:18
  11.4 5.5 %collective-permute-start.4 = (bf16[3,16,1152]{2,1,0:T(8,128)(2,1)S(1)}, bf16[3,16,1152]{2,1,0:T(8,128)(2,1)S(1)}, u32[]{:S(2)}, u32[]{:S(2)}) collective-permute-start(bf16[3,16,1152]{2,1,0:T(8,128)(2,1)S(1)} %pad_maximum_fusion.several_ref), channel_id=1, source_target_pairs={{0,4},{4,0},{8,12},{12,8},{16,20},{20,16},{24,28},{28,24},{1,5},{5... | collective-permute-start | bytes 331784 | tf_op jit(solution)/shard_map/ppermute | solution.py:18
  13.0 4.0 %collective-permute-start.3 = (bf16[16,1152]{1,0:T(8,128)(2,1)S(1)}, bf16[16,1152]{1,0:T(8,128)(2,1)S(1)}, u32[]{:S(2)}, u32[]{:S(2)}) collective-permute-start(bf16[16,1152]{1,0:T(8,128)(2,1)S(1)} %payload.1._.single_ref), channel_id=1, source_target_pairs={{0,4},{4,0},{8,12},{12,8},{16,20},{20,16},{24,28},{28,24},{1,5},{5... | collective-permute-start | bytes 110600 | tf_op jit(solution)/shard_map/ppermute | solution.py:18
  15.1 12.5 %copy-start = (s32[16,32]{1,0:T(8,128)S(1)}, s32[16,32]{1,0:T(8,128)}, u32[]{:S(2)}) copy-start(s32[16,32]{1,0:T(8,128)} %param.8) | copy-start | bytes 6148
  18.9 4.8 %collective-permute-start.5 = (bf16[3,16,1152]{2,1,0:T(8,128)(2,1)S(1)}, bf16[3,16,1152]{2,1,0:T(8,128)(2,1)S(1)}, u32[]{:S(2)}, u32[]{:S(2)}) collective-permute-start(bf16[3,16,1152]{2,1,0:T(8,128)(2,1)S(1)} %get-tuple-element.22._), channel_id=1, source_target_pairs={{0,4},{4,0},{8,12},{12,8},{16,20},{20,16},{24,28},{28,24},{1,5},{5... | collective-permute-start | bytes 331784 | tf_op jit(solution)/shard_map/ppermute | solution.py:18
  22.1 10.1 %collective-permute-start.9 = (bf16[16,1152]{1,0:T(8,128)(2,1)S(1)}, bf16[16,1152]{1,0:T(8,128)(2,1)S(1)}, u32[]{:S(2)}, u32[]{:S(2)}) collective-permute-start(bf16[16,1152]{1,0:T(8,128)(2,1)S(1)} %get-tuple-element.26), channel_id=1, source_target_pairs={{0,4},{4,0},{8,12},{12,8},{16,20},{20,16},{24,28},{28,24},{1,5},{5... | collective-permute-start | bytes 110600 | tf_op jit(solution)/shard_map/ppermute | solution.py:18
  24.0 8.2 %collective-permute-start.6 = (bf16[16,1152]{1,0:T(8,128)(2,1)S(1)}, bf16[16,1152]{1,0:T(8,128)(2,1)S(1)}, u32[]{:S(2)}, u32[]{:S(2)}) collective-permute-start(bf16[16,1152]{1,0:T(8,128)(2,1)S(1)} %get-tuple-element.23._), channel_id=1, source_target_pairs={{0,16},{4,20},{8,24},{12,28},{16,0},{20,4},{24,8},{28,12},{1,17},{... | collective-permute-start | bytes 110600 | tf_op jit(solution)/shard_map/ppermute | solution.py:18
  25.3 6.9 %collective-permute-start.7 = (bf16[16,1152]{1,0:T(8,128)(2,1)S(1)}, bf16[16,1152]{1,0:T(8,128)(2,1)S(1)}, u32[]{:S(2)}, u32[]{:S(2)}) collective-permute-start(bf16[16,1152]{1,0:T(8,128)(2,1)S(1)} %get-tuple-element.24), channel_id=1, source_target_pairs={{0,24},{4,28},{8,16},{12,20},{16,8},{20,12},{24,0},{28,4},{1,25},{... | collective-permute-start | bytes 110600 | tf_op jit(solution)/shard_map/ppermute | solution.py:18
  26.4 5.8 %collective-permute-start.8 = (bf16[16,1152]{1,0:T(8,128)(2,1)S(1)}, bf16[16,1152]{1,0:T(8,128)(2,1)S(1)}, u32[]{:S(2)}, u32[]{:S(2)}) collective-permute-start(bf16[16,1152]{1,0:T(8,128)(2,1)S(1)} %get-tuple-element.25), channel_id=1, source_target_pairs={{0,8},{4,12},{8,0},{12,4},{16,24},{20,28},{24,16},{28,20},{1,9},{5... | collective-permute-start | bytes 110600 | tf_op jit(solution)/shard_map/ppermute | solution.py:18
  33.8 2.4 %collective-permute-start.10 = (bf16[16,1024]{1,0:T(8,128)(2,1)S(1)}, bf16[16,1024]{1,0:T(8,128)(2,1)S(1)}, u32[]{:S(2)}, u32[]{:S(2)}) collective-permute-start(bf16[16,1024]{1,0:T(8,128)(2,1)S(1)} %get-tuple-element.33), channel_id=1, source_target_pairs={{0,1},{1,0},{2,3},{3,2},{4,5},{5,4},{6,7},{7,6},{8,9},{9,8},{10,11... | collective-permute-start | bytes 98312 | tf_op jit(solution)/shard_map/ppermute | solution.py:18
  33.8 4.0 %collective-permute-start.11 = (bf16[16,1024]{1,0:T(8,128)(2,1)S(1)}, bf16[16,1024]{1,0:T(8,128)(2,1)S(1)}, u32[]{:S(2)}, u32[]{:S(2)}) collective-permute-start(bf16[16,1024]{1,0:T(8,128)(2,1)S(1)} %get-tuple-element.34), channel_id=1, source_target_pairs={{0,2},{1,3},{2,0},{3,1},{4,6},{5,7},{6,4},{7,5},{8,10},{9,11},{10,... | collective-permute-start | bytes 98312 | tf_op jit(solution)/shard_map/ppermute | solution.py:18
  35.3 3.3 %collective-permute-start.12 = (bf16[16,1024]{1,0:T(8,128)(2,1)S(1)}, bf16[16,1024]{1,0:T(8,128)(2,1)S(1)}, u32[]{:S(2)}, u32[]{:S(2)}) collective-permute-start(bf16[16,1024]{1,0:T(8,128)(2,1)S(1)} %get-tuple-element.35), channel_id=1, source_target_pairs={{0,3},{1,2},{2,1},{3,0},{4,7},{5,6},{6,5},{7,4},{8,11},{9,10},{10,... | collective-permute-start | bytes 98312 | tf_op jit(solution)/shard_map/ppermute | solution.py:18

commit v3 on v2

--- a/solution.py
+++ b/solution.py
@@ -109,62 +109,64 @@
         copy.wait()
 
 
-def attend_kernel(
-    single_ref, several_ref, cache_ref, first_ref, others_ref, hits_ref, *, heads, picks
-):
+def attend_kernel(*refs, singles, heads, picks, export):
+    several_ref, cache_ref = refs[singles : singles + 2]
+    if export:
+        *outs, others_ref, hits_ref, keys_ref = refs[singles + 2 :]
+    else:
+        keys_ref, *outs, others_ref, hits_ref = refs[singles + 2 :]
     blocks, _, heads_kv, tokens, depth = cache_ref.shape
     width = heads * depth
-    rows_each = single_ref.shape[0]
+    rows_each = several_ref.shape[1]
     group_q = heads // heads_kv
     scale = depth**-0.5 * math.log2(math.e)
-    payloads = [single_ref] + [several_ref.at[i] for i in range(several_ref.shape[0])]
-    messages = [first_ref] + [others_ref.at[i] for i in range(others_ref.shape[0])]
+    payloads = list(refs[:singles]) + [several_ref.at[i] for i in range(several_ref.shape[0])]
+    messages = outs + [others_ref.at[i] for i in range(others_ref.shape[0])]
     me = lax.axis_index("mem").astype(jnp.float32)
     span = blocks * tokens
-    fence = jnp.where(
-        lax.broadcasted_iota(jnp.int32, (span, LANES), 0) // tokens
-        == lax.broadcasted_iota(jnp.int32, (span, LANES), 1),
-        MASKED,
-        0.0,
-    ).astype(jnp.bfloat16)
+    if export:
+        fence = jnp.where(
+            lax.broadcasted_iota(jnp.int32, (span, LANES), 0) // tokens
+            == lax.broadcasted_iota(jnp.int32, (span, LANES), 1),
+            MASKED,
+            0.0,
+        ).astype(jnp.bfloat16)
+        for kv in range(heads_kv):
+            keys = cache_ref[:, 0, kv].reshape(span, depth)
+            keys_ref[kv] = jnp.concatenate([keys, fence], axis=1).T
     hits = jnp.zeros((1, LANES), jnp.float32)
-    batch = min(len(payloads), 8)
-    rows = batch * rows_each
-    pair = math.gcd(group_q, max(1, 256 // rows))
-    lane = lax.broadcasted_iota(jnp.int32, (rows, LANES), 1)
+    batches = [payloads[i : i + 8] for i in range(0, len(payloads), 8)]
     blocked = []
-    for start in range(0, len(payloads), batch):
-        tags = jnp.concatenate([p[:, width:] for p in payloads[start : start + batch]], axis=0)
-        tags = tags.astype(jnp.float32)
+    for part in batches:
+        tags = jnp.concatenate([p[:, width:] for p in part], axis=0).astype(jnp.float32)
+        lane = lax.broadcasted_iota(jnp.int32, tags.shape, 1).astype(jnp.float32)
         local = jnp.where(tags == me, pltpu.roll(tags, LANES - picks, 1), -1.0)
-        chosen = jnp.zeros((rows, LANES), jnp.float32)
+        chosen = jnp.zeros(tags.shape, jnp.float32)
         for i in range(picks):
-            chosen = jnp.where(local[:, i : i + 1] == lane.astype(jnp.float32), 1.0, chosen)
+            chosen = jnp.where(local[:, i : i + 1] == lane, 1.0, chosen)
         hits = hits + jnp.sum(chosen, axis=0, keepdims=True)
         blocked.append((1.0 - chosen).astype(jnp.bfloat16))
     hits_ref[...] = hits
 
-    def scores_of(start, kv, first_head):
-        part = payloads[start : start + batch]
-        keys = jnp.concatenate([cache_ref[:, 0, kv].reshape(span, depth), fence], axis=1)
+    def scores_of(b, kv, first_head, pair):
         stacked = []
         for h in range(first_head, first_head + pair):
-            query = jnp.concatenate([p[:, h * depth : (h + 1) * depth] for p in part], axis=0)
-            stacked.append(jnp.concatenate([query, blocked[start // batch]], axis=1))
+            query = jnp.concatenate(
+                [p[:, h * depth : (h + 1) * depth] for p in batches[b]], axis=0
+            )
+            stacked.append(jnp.concatenate([query, blocked[b]], axis=1))
         query = jnp.concatenate(stacked, axis=0)
-        return lax.dot_general(
-            query, keys, (((1,), (1,)), ((), ())), preferred_element_type=jnp.float32
-        )
-
-    units = [
-        (start, kv, first_head)
-        for start in range(0, len(payloads), batch)
-        for kv in range(heads_kv)
-        for first_head in range(kv * group_q, (kv + 1) * group_q, pair)
-    ]
+        return jnp.dot(query, keys_ref[kv], preferred_element_type=jnp.float32)
+
+    units = []
+    for b, part in enumerate(batches):
+        pair = group_q if len(part) * rows_each <= 96 else math.gcd(group_q, 2)
+        for kv in range(heads_kv):
+            for first_head in range(kv * group_q, (kv + 1) * group_q, pair):
+                units.append((b, kv, first_head, pair))
     ahead = scores_of(*units[0])
     stats = None
-    for n, (start, kv, first_head) in enumerate(units):
+    for n, (b, kv, first_head, pair) in enumerate(units):
         scores = ahead
         if n + 1 < len(units):
             ahead = scores_of(*units[n + 1])
@@ -175,19 +177,21 @@
         sums = jnp.dot(weights, values, preferred_element_type=jnp.float32)
         out = sums[:, :depth].astype(jnp.bfloat16)
         total = sums[:, depth : depth + 1]
+        rows = len(batches[b]) * rows_each
+        lane = lax.broadcasted_iota(jnp.int32, (rows, LANES), 1)
         if first_head == 0:
             stats = jnp.zeros((rows, LANES), jnp.float32)
         for j in range(pair):
             h = first_head + j
-            for i in range(batch):
+            for i in range(len(batches[b])):
                 at = j * rows + i * rows_each
-                messages[start + i][:, h * depth : (h + 1) * depth] = out[at : at + rows_each]
+                messages[8 * b + i][:, h * depth : (h + 1) * depth] = out[at : at + rows_each]
             stats = jnp.where(lane == h, peak[j * rows : (j + 1) * rows], stats)
             stats = jnp.where(lane == heads + h, total[j * rows : (j + 1) * rows], stats)
         if first_head + pair == heads:
             packed = split_stats(stats, heads)
-            for i in range(batch):
-                messages[start + i][:, width:] = packed[i * rows_each : (i + 1) * rows_each]
+            for i in range(len(batches[b])):
+                messages[8 * b + i][:, width:] = packed[i * rows_each : (i + 1) * rows_each]
 
 
 def merge_kernel(mine_ref, theirs_ref, *outs, heads):
@@ -281,13 +285,27 @@
     forwarded = exchange(straight, "mem", 1)
     several = jax.ShapeDtypeStruct(straight.shape, straight.dtype)
     hits = jax.ShapeDtypeStruct((1, LANES), jnp.float32)
-    attend = functools.partial(attend_kernel, heads=heads, picks=picks)
-    own, mine, hits_a = call(
-        attend, (payload, straight, cache_blocks), [vmem] * 3, [message, several, hits], 24
-    )
-    beside, theirs, hits_b = call(
-        attend, (near, forwarded, cache_blocks), [vmem] * 3, [message, several, hits], 24
-    )
+
+    keys = jax.ShapeDtypeStruct(
+        (cache_blocks.shape[2], depth + LANES, blocks * cache_blocks.shape[3]), jnp.bfloat16
+    )
+
+    def attend(single, group, keys_in):
+        operands = (*single, group, cache_blocks, *keys_in)
+        export = not keys_in
+        return call(
+            functools.partial(
+                attend_kernel, singles=len(single), heads=heads, picks=picks, export=export
+            ),
+            operands,
+            [vmem] * len(operands),
+            [message] * len(single) + [several, hits] + [keys] * export,
+            24,
+        )
+
+    own, beside, mine, hits_a, keys = attend([payload, near], straight, [])
+    returned_beside = exchange(beside, "mem", 1)
+    theirs, hits_b = attend([], forwarded, [keys])
     crossed = exchange(theirs, "mem", 1)
     far_steps = tuple(range(devices_head - 1, 1, -1))
     near_steps = (1, 0)
@@ -313,7 +331,7 @@
         8,
     )
     returned = [own] + [exchange(m, "mem", k) for k, m in zip(even, merged)]
-    returned.append(exchange(beside, "mem", 1))
+    returned.append(returned_beside)
     weight_near = stage_columns(near_steps, merged[0])
     share = jax.ShapeDtypeStruct((rows, columns), jnp.bfloat16)
     attended, *far = call(

time: 39.5 us -> 41.6 us (1.053)
  waiting for transfers between devices: 9.21 us -> 11.2 us
    ppermute x13, waiting for transfers between devices: 9.21 us -> 11.2 us  [exchange(): return lax.ppermute(value, axis, [(i, i ^ step) for i in range(count)])]
  transfers between devices with their start and end apart: 13 -> 13, of which waited for: 6 -> 6; matrix products, arithmetic and copies ran while one was open for 2% -> 1% of each run, Pallas kernels for 21% -> 21%
where the time goes in v3:
time: 41.6 us; the launch traced here: 41.4 us
  starting transfers between devices  15.3 us (37%)
  Pallas kernels  12.8 us (31%)
  waiting for transfers between devices  11.2 us (27%)
  other arithmetic  1.26 us (3%)
  between operations  0.74 us (2%)
    ppermute x13, starting transfers between devices, exchange(): return lax.ppermute(value, axis, [(i, i ^ step) for i in range(count)])  15.3 us
    pallas_call x8, Pallas kernels, call(): pl.pallas_call(kernel, in_specs=specs, out_specs=[vmem] * len(shapes), ou...  12 us
    ppermute x13, waiting for transfers between devices, exchange(): return lax.ppermute(value, axis, [(i, i ^ step) for i in range(count)])  11.2 us
    pallas_call x1, Pallas kernels, per_device(): pl.pallas_call(functools.partial(payload_kernel, owners=devices_mem, all_...  0.84 us
  transfers between devices with their start and end apart: 13, of which 6 were waited for; matrix products, arithmetic and copies ran while one was open for 1% of the time, Pallas kernels for 21%

profile of v3, /device:TPU:0, one launch (start us, length us, event | category | flops | bytes accessed | tf_op | source)
XLA Modules:
  0.0 41.4 jit_solution(229608125506976381)
XLA Ops:
  0.6 0.8 %payload.1._.refs_0_ = bf16[16,1152]{1,0:T(8,128)(2,1)S(1)} custom-call(bf16[16,8,128]{2,1,0:T(8,128)(2,1)} %queries_hbm.1, s32[16,32]{1,0:T(8,128)} %selected_hbm.1), custom_call_target="tpu_custom_call" | custom-call | tf_op jit(solution)/shard_map/payload/pallas_call | solution.py:249
  1.5 4.1 %collective-permute-start.1 = (bf16[16,1152]{1,0:T(8,128)(2,1)S(1)}, bf16[16,1152]{1,0:T(8,128)(2,1)S(1)}, u32[]{:S(2)}, u32[]{:S(2)}) collective-permute-start(bf16[16,1152]{1,0:T(8,128)(2,1)S(1)} %payload.1._.refs_0_), channel_id=1, source_target_pairs={{0,16},{4,20},{8,24},{12,28},{16,0},{20,4},{24,8},{28,12},{1,17},{... | collective-permute-start | bytes 110600 | tf_op jit(solution)/shard_map/ppermute | solution.py:18
  5.6 1.3 %collective-permute-start.2 = (bf16[16,1152]{1,0:T(8,128)(2,1)S(1)}, bf16[16,1152]{1,0:T(8,128)(2,1)S(1)}, u32[]{:S(2)}, u32[]{:S(2)}) collective-permute-start(bf16[16,1152]{1,0:T(8,128)(2,1)S(1)} %payload.1._.refs_0_), channel_id=1, source_target_pairs={{0,24},{4,28},{8,16},{12,20},{16,8},{20,12},{24,0},{28,4},{1,25},{... | collective-permute-start | bytes 110600 | tf_op jit(solution)/shard_map/ppermute | solution.py:18
  7.0 0.2 collective-permute-start.3
  7.2 0.8 %collective-permute-done.1 = bf16[16,1152]{1,0:T(8,128)(2,1)S(1)} collective-permute-done((bf16[16,1152]{1,0:T(8,128)(2,1)S(1)}, bf16[16,1152]{1,0:T(8,128)(2,1)S(1)}, u32[]{:S(2)}, u32[]{:S(2)}) %collective-permute-start.1) | collective-permute-done | bytes 36896 | tf_op jit(solution)/shard_map/ppermute | solution.py:18
  7.9 3.4 %collective-permute-done.2 = bf16[16,1152]{1,0:T(8,128)(2,1)S(1)} collective-permute-done((bf16[16,1152]{1,0:T(8,128)(2,1)S(1)}, bf16[16,1152]{1,0:T(8,128)(2,1)S(1)}, u32[]{:S(2)}, u32[]{:S(2)}) %collective-permute-start.2) | collective-permute-done | bytes 36896 | tf_op jit(solution)/shard_map/ppermute | solution.py:18
  11.4 0.0 collective-permute-done.3
  11.4 1.6 %collective-permute-start.4 = (bf16[3,16,1152]{2,1,0:T(8,128)(2,1)S(1)}, bf16[3,16,1152]{2,1,0:T(8,128)(2,1)S(1)}, u32[]{:S(2)}, u32[]{:S(2)}) collective-permute-start(bf16[3,16,1152]{2,1,0:T(8,128)(2,1)S(1)} %pad_maximum_fusion.refs_2_), channel_id=1, source_target_pairs={{0,4},{4,0},{8,12},{12,8},{16,20},{20,16},{24,28},{28,24},{1,5},{5... | collective-permute-start | bytes 331784 | tf_op jit(solution)/shard_map/ppermute | solution.py:18
  13.0 0.5 %collective-permute-start = (bf16[16,1152]{1,0:T(8,128)(2,1)S(1)}, bf16[16,1152]{1,0:T(8,128)(2,1)S(1)}, u32[]{:S(2)}, u32[]{:S(2)}) collective-permute-start(bf16[16,1152]{1,0:T(8,128)(2,1)S(1)} %payload.1._.refs_0_), channel_id=1, source_target_pairs={{0,4},{4,0},{8,12},{12,8},{16,20},{20,16},{24,28},{28,24},{1,5},{5... | collective-permute-start | bytes 110600 | tf_op jit(solution)/shard_map/ppermute | solution.py:18
  13.5 1.6 %shard_map.68.refs_3_.refs_1_ = bf16[32,2,2,64,128]{4,3,2,1,0:T(8,128)(2,1)S(1)} custom-call(bf16[32,2,2,64,128]{4,3,2,1,0:T(8,128)(2,1)} %source_hbm.1, bf16[16,1152]{1,0:T(8,128)(2,1)S(1)} %payload.1._.refs_0_), custom_call_target="tpu_custom_call" | custom-call | tf_op jit(solution)/shard_map/pallas_call | solution.py:266
  15.1 1.8 %collective-permute-done.refs_1_ = bf16[16,1152]{1,0:T(8,128)(2,1)S(1)} collective-permute-done((bf16[16,1152]{1,0:T(8,128)(2,1)S(1)}, bf16[16,1152]{1,0:T(8,128)(2,1)S(1)}, u32[]{:S(2)}, u32[]{:S(2)}) %collective-permute-start) | collective-permute-done | bytes 36896 | tf_op jit(solution)/shard_map/ppermute | solution.py:18
  16.9 2.4 %shard_map.69 = (bf16[16,1152]{1,0:T(8,128)(2,1)S(1)}, bf16[16,1152]{1,0:T(8,128)(2,1)S(1)}, bf16[3,16,1152]{2,1,0:T(8,128)(2,1)S(1)}, f32[1,128]{1,0:T(1,128)S(1)}, bf16[2,256,2048]{2,1,0:T(8,128)(2,1)S(1)}) custom-call(bf16[16,1152]{1,0:T(8,128)(2,1)S(1)} %payload.1._.refs_0_, bf16[16,1152]{1,0:T(8,128)(2,1)S(1)} %collective-permute-done.refs_1_, ...), custom_call_target="tpu_custom_call" | custom-call | tf_op jit(solution)/shard_map/pallas_call | solution.py:266
  19.3 0.0 collective-permute-done.4.refs_0_
  19.3 0.0 copy-start
  19.3 1.6 %shard_map.70 = (bf16[3,16,1152]{2,1,0:T(8,128)(2,1)S(1)}, f32[1,128]{1,0:T(1,128)S(1)}) custom-call(bf16[3,16,1152]{2,1,0:T(8,128)(2,1)S(1)} %collective-permute-done.4.refs_0_, bf16[32,2,2,64,128]{4,3,2,1,0:T(8,128)(2,1)S(1)} %shard_map.68.refs_3_.refs_1_, bf16[2,256,2048]{2,1,0:T(8,128)(2,1)S(1)} %get-tuple-element.23.refs_2_), custom_call_target="tpu_custom_call" | custom-call | tf_op jit(solution)/shard_map/pallas_call | solution.py:266
  20.9 1.2 %collective-permute-start.5 = (bf16[3,16,1152]{2,1,0:T(8,128)(2,1)S(1)}, bf16[3,16,1152]{2,1,0:T(8,128)(2,1)S(1)}, u32[]{:S(2)}, u32[]{:S(2)}) collective-permute-start(bf16[3,16,1152]{2,1,0:T(8,128)(2,1)S(1)} %get-tuple-element.24._), channel_id=1, source_target_pairs={{0,4},{4,0},{8,12},{12,8},{16,20},{20,16},{24,28},{28,24},{1,5},{5... | collective-permute-start | bytes 331784 | tf_op jit(solution)/shard_map/ppermute | solution.py:18
  22.2 0.8 %collective-permute-start.9 = (bf16[16,1152]{1,0:T(8,128)(2,1)S(1)}, bf16[16,1152]{1,0:T(8,128)(2,1)S(1)}, u32[]{:S(2)}, u32[]{:S(2)}) collective-permute-start(bf16[16,1152]{1,0:T(8,128)(2,1)S(1)} %get-tuple-element.28), channel_id=1, source_target_pairs={{0,4},{4,0},{8,12},{12,8},{16,20},{20,16},{24,28},{28,24},{1,5},{5... | collective-permute-start | bytes 110600 | tf_op jit(solution)/shard_map/ppermute | solution.py:18
  23.0 2.7 %collective-permute-done.5.theirs_ref = bf16[3,16,1152]{2,1,0:T(8,128)(2,1)S(1)} collective-permute-done((bf16[3,16,1152]{2,1,0:T(8,128)(2,1)S(1)}, bf16[3,16,1152]{2,1,0:T(8,128)(2,1)S(1)}, u32[]{:S(2)}, u32[]{:S(2)}) %collective-permute-start.5) | collective-permute-done | bytes 110624 | tf_op jit(solution)/shard_map/ppermute | solution.py:18
  25.7 0.4 shard_map.71
  26.1 1.3 %collective-permute-start.6 = (bf16[16,1152]{1,0:T(8,128)(2,1)S(1)}, bf16[16,1152]{1,0:T(8,128)(2,1)S(1)}, u32[]{:S(2)}, u32[]{:S(2)}) collective-permute-start(bf16[16,1152]{1,0:T(8,128)(2,1)S(1)} %get-tuple-element.25._), channel_id=1, source_target_pairs={{0,16},{4,20},{8,24},{12,28},{16,0},{20,4},{24,8},{28,12},{1,17},{... | collective-permute-start | bytes 110600 | tf_op jit(solution)/shard_map/ppermute | solution.py:18
  27.4 1.1 %collective-permute-start.7 = (bf16[16,1152]{1,0:T(8,128)(2,1)S(1)}, bf16[16,1152]{1,0:T(8,128)(2,1)S(1)}, u32[]{:S(2)}, u32[]{:S(2)}) collective-permute-start(bf16[16,1152]{1,0:T(8,128)(2,1)S(1)} %get-tuple-element.26), channel_id=1, source_target_pairs={{0,24},{4,28},{8,16},{12,20},{16,8},{20,12},{24,0},{28,4},{1,25},{... | collective-permute-start | bytes 110600 | tf_op jit(solution)/shard_map/ppermute | solution.py:18
  28.4 1.2 %collective-permute-start.8 = (bf16[16,1152]{1,0:T(8,128)(2,1)S(1)}, bf16[16,1152]{1,0:T(8,128)(2,1)S(1)}, u32[]{:S(2)}, u32[]{:S(2)}) collective-permute-start(bf16[16,1152]{1,0:T(8,128)(2,1)S(1)} %get-tuple-element.27), channel_id=1, source_target_pairs={{0,8},{4,12},{8,0},{12,4},{16,24},{20,28},{24,16},{28,20},{1,9},{5... | collective-permute-start | bytes 110600 | tf_op jit(solution)/shard_map/ppermute | solution.py:18
  29.6 0.0 copy-done
  29.6 0.1 multiply_reduce_fusion
  29.7 2.2 %shard_map.72 = (bf16[1024,1024]{1,0:T(8,128)(2,1)S(1)}, bf16[1024,1024]{1,0:T(8,128)(2,1)S(1)}) custom-call(bf16[1024,4096]{1,0:T(8,128)(2,1)} %weight_hbm.3, bf16[3,16,1152]{2,1,0:T(8,128)(2,1)S(1)} %get-tuple-element.24._), custom_call_target="tpu_custom_call" | custom-call | tf_op jit(solution)/shard_map/pallas_call | solution.py:266
  32.0 2.3 %shard_map.74 = (bf16[1024,1024]{1,0:T(8,128)(2,1)S(1)}, bf16[1024,1024]{1,0:T(8,128)(2,1)S(1)}) custom-call(bf16[1024,4096]{1,0:T(8,128)(2,1)} %weight_hbm.3, bf16[16,1152]{1,0:T(8,128)(2,1)S(1)} %get-tuple-element.25._), custom_call_target="tpu_custom_call" | custom-call | tf_op jit(solution)/shard_map/pallas_call | solution.py:266
  34.2 0.0 collective-permute-done.9.refs_4_
  34.3 0.0 collective-permute-done.6.refs_1_
  34.3 0.0 collective-permute-done.7.refs_2_
  34.3 0.0 collective-permute-done.8.refs_3_
  34.3 0.9 %shard_map.73 = (bf16[16,1024]{1,0:T(8,128)(2,1)S(1)}, bf16[16,1024]{1,0:T(8,128)(2,1)S(1)}, bf16[16,1024]{1,0:T(8,128)(2,1)S(1)}) custom-call(bf16[16,1152]{1,0:T(8,128)(2,1)S(1)} %get-tuple-element.21.refs_0_, bf16[16,1152]{1,0:T(8,128)(2,1)S(1)} %collective-permute-done.6.refs_1_, bf16[16,1152]{1,0:T(8,128)(2,1)S(1)} %collective-permute-done.7.refs_2_, ...), custom_call_target="tpu_custom_call" | custom-call | tf_op jit(solution)/shard_map/pallas_call | solution.py:266
  35.2 0.7 %shard_map.75 = (bf16[16,1024]{1,0:T(8,128)(2,1)S(1)}, bf16[16,1024]{1,0:T(8,128)(2,1)S(1)}) custom-call(bf16[16,1024]{1,0:T(8,128)(2,1)S(1)} %get-tuple-element.31.attended_ref, bf16[1024,1024]{1,0:T(8,128)(2,1)S(1)} %get-tuple-element.32.refs_0_, bf16[1024,1024]{1,0:T(8,128)(2,1)S(1)} %get-tuple-element.33.refs_1_), custom_call_target="tpu_custom_call" | custom-call | tf_op jit(solution)/shard_map/pallas_call | solution.py:266
  35.8 0.0 collective-permute-start.10
  35.8 1.6 %collective-permute-start.11 = (bf16[16,1024]{1,0:T(8,128)(2,1)S(1)}, bf16[16,1024]{1,0:T(8,128)(2,1)S(1)}, u32[]{:S(2)}, u32[]{:S(2)}) collective-permute-start(bf16[16,1024]{1,0:T(8,128)(2,1)S(1)} %get-tuple-element.36), channel_id=1, source_target_pairs={{0,2},{1,3},{2,0},{3,1},{4,6},{5,7},{6,4},{7,5},{8,10},{9,11},{10,... | collective-permute-start | bytes 98312 | tf_op jit(solution)/shard_map/ppermute | solution.py:18
  37.4 0.3 collective-permute-start.12
  37.7 0.5 %bitcast_add_fusion = f32[32]{0:T(128)} fusion(f32[32]{0:T(128)S(1)} %multiply_reduce_fusion, f32[1,128]{1,0:T(1,128)S(1)} %add.18), kind=kLoop, calls=%fused_computation.3 | loop fusion | flops 32 | bytes 384 | tf_op jit(solution)/shard_map/add | solution.py:353
  38.2 0.0 collective-permute-done.10
  38.2 1.6 %collective-permute-done.11 = bf16[16,1024]{1,0:T(8,128)(2,1)S(1)} collective-permute-done((bf16[16,1024]{1,0:T(8,128)(2,1)S(1)}, bf16[16,1024]{1,0:T(8,128)(2,1)S(1)}, u32[]{:S(2)}, u32[]{:S(2)}) %collective-permute-start.11) | collective-permute-done | bytes 32800 | tf_op jit(solution)/shard_map/ppermute | solution.py:18
  39.8 0.9 %collective-permute-done.12 = bf16[16,1024]{1,0:T(8,128)(2,1)S(1)} collective-permute-done((bf16[16,1024]{1,0:T(8,128)(2,1)S(1)}, bf16[16,1024]{1,0:T(8,128)(2,1)S(1)}, u32[]{:S(2)}, u32[]{:S(2)}) %collective-permute-start.12) | collective-permute-done | bytes 32800 | tf_op jit(solution)/shard_map/ppermute | solution.py:18
  40.7 0.6 %add_convert_fusion = bf16[16,1024]{1,0:T(8,128)(2,1)} fusion(bf16[16,1024]{1,0:T(8,128)(2,1)S(1)} %collective-permute-done.12, bf16[16,1024]{1,0:T(8,128)(2,1)S(1)} %collective-permute-done.11, bf16[16,1024]{1,0:T(8,128)(2,1)S(1)} %collective-permute-done.10, bf16[16,1024]{1,0:T(8,128)(2,1)S(1)} %get-tuple-element.34), kind=kLoop, calls=%fused_computation.1 | loop fusion | flops 131072 | bytes 163840 | tf_op jit(solution)/shard_map/convert_element_type | solution.py:354
  (3 shorter events, 0.0 us)
Async XLA Ops:
  1.5 6.5 %collective-permute-start.1 = (bf16[16,1152]{1,0:T(8,128)(2,1)S(1)}, bf16[16,1152]{1,0:T(8,128)(2,1)S(1)}, u32[]{:S(2)}, u32[]{:S(2)}) collective-permute-start(bf16[16,1152]{1,0:T(8,128)(2,1)S(1)} %payload.1._.refs_0_), channel_id=1, source_target_pairs={{0,16},{4,20},{8,24},{12,28},{16,0},{20,4},{24,8},{28,12},{1,17},{... | collective-permute-start | bytes 110600 | tf_op jit(solution)/shard_map/ppermute | solution.py:18
  5.6 5.8 %collective-permute-start.2 = (bf16[16,1152]{1,0:T(8,128)(2,1)S(1)}, bf16[16,1152]{1,0:T(8,128)(2,1)S(1)}, u32[]{:S(2)}, u32[]{:S(2)}) collective-permute-start(bf16[16,1152]{1,0:T(8,128)(2,1)S(1)} %payload.1._.refs_0_), channel_id=1, source_target_pairs={{0,24},{4,28},{8,16},{12,20},{16,8},{20,12},{24,0},{28,4},{1,25},{... | collective-permute-start | bytes 110600 | tf_op jit(solution)/shard_map/ppermute | solution.py:18
  7.0 4.4 %collective-permute-start.3 = (bf16[16,1152]{1,0:T(8,128)(2,1)S(1)}, bf16[16,1152]{1,0:T(8,128)(2,1)S(1)}, u32[]{:S(2)}, u32[]{:S(2)}) collective-permute-start(bf16[16,1152]{1,0:T(8,128)(2,1)S(1)} %payload.1._.refs_0_), channel_id=1, source_target_pairs={{0,8},{4,12},{8,0},{12,4},{16,24},{20,28},{24,16},{28,20},{1,9},{5... | collective-permute-start | bytes 110600 | tf_op jit(solution)/shard_map/ppermute | solution.py:18
  11.4 7.9 %collective-permute-start.4 = (bf16[3,16,1152]{2,1,0:T(8,128)(2,1)S(1)}, bf16[3,16,1152]{2,1,0:T(8,128)(2,1)S(1)}, u32[]{:S(2)}, u32[]{:S(2)}) collective-permute-start(bf16[3,16,1152]{2,1,0:T(8,128)(2,1)S(1)} %pad_maximum_fusion.refs_2_), channel_id=1, source_target_pairs={{0,4},{4,0},{8,12},{12,8},{16,20},{20,16},{24,28},{28,24},{1,5},{5... | collective-permute-start | bytes 331784 | tf_op jit(solution)/shard_map/ppermute | solution.py:18
  13.0 4.0 %collective-permute-start = (bf16[16,1152]{1,0:T(8,128)(2,1)S(1)}, bf16[16,1152]{1,0:T(8,128)(2,1)S(1)}, u32[]{:S(2)}, u32[]{:S(2)}) collective-permute-start(bf16[16,1152]{1,0:T(8,128)(2,1)S(1)} %payload.1._.refs_0_), channel_id=1, source_target_pairs={{0,4},{4,0},{8,12},{12,8},{16,20},{20,16},{24,28},{28,24},{1,5},{5... | collective-permute-start | bytes 110600 | tf_op jit(solution)/shard_map/ppermute | solution.py:18
  19.3 10.3 %copy-start = (s32[16,32]{1,0:T(8,128)S(1)}, s32[16,32]{1,0:T(8,128)}, u32[]{:S(2)}) copy-start(s32[16,32]{1,0:T(8,128)} %param.8) | copy-start | bytes 6148
  20.9 4.8 %collective-permute-start.5 = (bf16[3,16,1152]{2,1,0:T(8,128)(2,1)S(1)}, bf16[3,16,1152]{2,1,0:T(8,128)(2,1)S(1)}, u32[]{:S(2)}, u32[]{:S(2)}) collective-permute-start(bf16[3,16,1152]{2,1,0:T(8,128)(2,1)S(1)} %get-tuple-element.24._), channel_id=1, source_target_pairs={{0,4},{4,0},{8,12},{12,8},{16,20},{20,16},{24,28},{28,24},{1,5},{5... | collective-permute-start | bytes 331784 | tf_op jit(solution)/shard_map/ppermute | solution.py:18
  22.2 12.1 %collective-permute-start.9 = (bf16[16,1152]{1,0:T(8,128)(2,1)S(1)}, bf16[16,1152]{1,0:T(8,128)(2,1)S(1)}, u32[]{:S(2)}, u32[]{:S(2)}) collective-permute-start(bf16[16,1152]{1,0:T(8,128)(2,1)S(1)} %get-tuple-element.28), channel_id=1, source_target_pairs={{0,4},{4,0},{8,12},{12,8},{16,20},{20,16},{24,28},{28,24},{1,5},{5... | collective-permute-start | bytes 110600 | tf_op jit(solution)/shard_map/ppermute | solution.py:18
  26.1 8.2 %collective-permute-start.6 = (bf16[16,1152]{1,0:T(8,128)(2,1)S(1)}, bf16[16,1152]{1,0:T(8,128)(2,1)S(1)}, u32[]{:S(2)}, u32[]{:S(2)}) collective-permute-start(bf16[16,1152]{1,0:T(8,128)(2,1)S(1)} %get-tuple-element.25._), channel_id=1, source_target_pairs={{0,16},{4,20},{8,24},{12,28},{16,0},{20,4},{24,8},{28,12},{1,17},{... | collective-permute-start | bytes 110600 | tf_op jit(solution)/shard_map/ppermute | solution.py:18
  27.4 6.9 %collective-permute-start.7 = (bf16[16,1152]{1,0:T(8,128)(2,1)S(1)}, bf16[16,1152]{1,0:T(8,128)(2,1)S(1)}, u32[]{:S(2)}, u32[]{:S(2)}) collective-permute-start(bf16[16,1152]{1,0:T(8,128)(2,1)S(1)} %get-tuple-element.26), channel_id=1, source_target_pairs={{0,24},{4,28},{8,16},{12,20},{16,8},{20,12},{24,0},{28,4},{1,25},{... | collective-permute-start | bytes 110600 | tf_op jit(solution)/shard_map/ppermute | solution.py:18
  28.4 5.8 %collective-permute-start.8 = (bf16[16,1152]{1,0:T(8,128)(2,1)S(1)}, bf16[16,1152]{1,0:T(8,128)(2,1)S(1)}, u32[]{:S(2)}, u32[]{:S(2)}) collective-permute-start(bf16[16,1152]{1,0:T(8,128)(2,1)S(1)} %get-tuple-element.27), channel_id=1, source_target_pairs={{0,8},{4,12},{8,0},{12,4},{16,24},{20,28},{24,16},{28,20},{1,9},{5... | collective-permute-start | bytes 110600 | tf_op jit(solution)/shard_map/ppermute | solution.py:18
  35.8 2.4 %collective-permute-start.10 = (bf16[16,1024]{1,0:T(8,128)(2,1)S(1)}, bf16[16,1024]{1,0:T(8,128)(2,1)S(1)}, u32[]{:S(2)}, u32[]{:S(2)}) collective-permute-start(bf16[16,1024]{1,0:T(8,128)(2,1)S(1)} %get-tuple-element.35), channel_id=1, source_target_pairs={{0,1},{1,0},{2,3},{3,2},{4,5},{5,4},{6,7},{7,6},{8,9},{9,8},{10,11... | collective-permute-start | bytes 98312 | tf_op jit(solution)/shard_map/ppermute | solution.py:18
  35.8 4.0 %collective-permute-start.11 = (bf16[16,1024]{1,0:T(8,128)(2,1)S(1)}, bf16[16,1024]{1,0:T(8,128)(2,1)S(1)}, u32[]{:S(2)}, u32[]{:S(2)}) collective-permute-start(bf16[16,1024]{1,0:T(8,128)(2,1)S(1)} %get-tuple-element.36), channel_id=1, source_target_pairs={{0,2},{1,3},{2,0},{3,1},{4,6},{5,7},{6,4},{7,5},{8,10},{9,11},{10,... | collective-permute-start | bytes 98312 | tf_op jit(solution)/shard_map/ppermute | solution.py:18
  37.4 3.3 %collective-permute-start.12 = (bf16[16,1024]{1,0:T(8,128)(2,1)S(1)}, bf16[16,1024]{1,0:T(8,128)(2,1)S(1)}, u32[]{:S(2)}, u32[]{:S(2)}) collective-permute-start(bf16[16,1024]{1,0:T(8,128)(2,1)S(1)} %get-tuple-element.37), channel_id=1, source_target_pairs={{0,3},{1,2},{2,1},{3,0},{4,7},{5,6},{6,5},{7,4},{8,11},{9,10},{10,... | collective-permute-start | bytes 98312 | tf_op jit(solution)/shard_map/ppermute | solution.py:18

commit v4 on v3

--- a/solution.py
+++ b/solution.py
@@ -93,20 +93,10 @@
     copy.wait()
 
 
-def stage_columns_kernel(weight_hbm, _, *refs, steps):
-    outs = refs[:-1]
-    me = lax.axis_index("head")
-    columns = outs[0].shape[1]
-    copies = []
-    for i, (k, out) in enumerate(zip(steps, outs)):
-        at = pl.multiple_of((me ^ k) * columns, columns)
-        copies.append(
-            pltpu.make_async_copy(weight_hbm.at[:, pl.ds(at, columns)], out, refs[-1].at[i])
-        )
-    for copy in copies:
-        copy.start()
-    for copy in copies:
-        copy.wait()
+def stage_rows_kernel(weight_hbm, _, out_ref, sem, *, first):
+    copy = pltpu.make_async_copy(weight_hbm.at[pl.ds(first, out_ref.shape[0])], out_ref, sem)
+    copy.start()
+    copy.wait()
 
 
 def attend_kernel(*refs, singles, heads, picks, export):
@@ -207,14 +197,22 @@
         out[:, width:] = split_stats(stats, heads)
 
 
-def project(attended, weights, outs):
-    for weight_ref, out in zip(weights, outs):
-        out[...] = jnp.dot(
-            attended, weight_ref[...], preferred_element_type=jnp.float32
+def project(attended, weights, outs, steps):
+    me = lax.axis_index("head")
+    half = weights[0].shape[0]
+    columns = outs[0].shape[1]
+    for k, out in zip(steps, outs):
+        at = pl.ds(pl.multiple_of((me ^ k) * columns, columns), columns)
+        out[...] = sum(
+            jnp.dot(
+                attended[:, i * half : (i + 1) * half], w[:, at], preferred_element_type=jnp.float32
+            )
+            for i, w in enumerate(weights)
         ).astype(jnp.bfloat16)
 
 
-def project_far_kernel(*refs, sources, parts, heads):
+def project_far_kernel(*refs, sources, heads, steps):
+    parts = 2
     messages = refs[:sources]
     weights = refs[sources : sources + parts]
     attended_ref = refs[sources + parts]
@@ -227,12 +225,11 @@
         [a for _, a in weighted_sums(messages, factors, heads, depth)], axis=1
     )
     attended_ref[...] = attended
-    project(attended, weights, refs[sources + parts + 1 :])
-
-
-def project_near_kernel(attended_ref, *refs):
-    parts = len(refs) // 2
-    project(attended_ref[...], refs[:parts], refs[parts:])
+    project(attended, weights, refs[sources + parts + 1 :], steps)
+
+
+def project_near_kernel(attended_ref, *refs, steps):
+    project(attended_ref[...], refs[:2], refs[2:], steps)
 
 
 def per_device(queries, cache_blocks, selected, counts, output_weight):
@@ -310,19 +307,20 @@
     far_steps = tuple(range(devices_head - 1, 1, -1))
     near_steps = (1, 0)
     columns = output_weight.shape[1] // devices_head
-    part = jax.ShapeDtypeStruct((output_weight.shape[0], columns), output_weight.dtype)
-
-    def stage_columns(steps, after):
+    half = output_weight.shape[0] // 2
+    part = jax.ShapeDtypeStruct((half, output_weight.shape[1]), output_weight.dtype)
+
+    def stage_rows(first, after):
         return call(
-            functools.partial(stage_columns_kernel, steps=steps),
+            functools.partial(stage_rows_kernel, first=first),
             (keep(output_weight), after),
             [hbm, vmem],
-            [part] * len(steps),
+            [part],
             4,
-            [pltpu.SemaphoreType.DMA((len(steps),))],
-        )
-
-    weight_far = stage_columns(far_steps, theirs)
+            [pltpu.SemaphoreType.DMA(())],
+        )[0]
+
+    weight_far = stage_rows(0, theirs)
     merged = call(
         functools.partial(merge_kernel, heads=heads),
         (mine, crossed),
@@ -332,19 +330,25 @@
     )
     returned = [own] + [exchange(m, "mem", k) for k, m in zip(even, merged)]
     returned.append(returned_beside)
-    weight_near = stage_columns(near_steps, merged[0])
+    weight_near = stage_rows(half, merged[0])
     share = jax.ShapeDtypeStruct((rows, columns), jnp.bfloat16)
     attended, *far = call(
         functools.partial(
-            project_far_kernel, sources=len(returned), parts=len(far_steps), heads=heads
+            project_far_kernel, sources=len(returned), heads=heads, steps=far_steps
         ),
-        (*returned, *weight_far),
-        [vmem] * (len(returned) + len(far_steps)),
+        (*returned, weight_far, weight_near),
+        [vmem] * (len(returned) + 2),
         [jax.ShapeDtypeStruct((rows, width), jnp.bfloat16)] + [share] * len(far_steps),
         16,
     )
     arrived = {k: exchange(s, "head", k) for k, s in zip(far_steps, far)}
-    beside, own = call(project_near_kernel, (attended, *weight_near), [vmem] * 3, [share] * 2, 16)
+    beside, own = call(
+        functools.partial(project_near_kernel, steps=near_steps),
+        (attended, weight_far, weight_near),
+        [vmem] * 3,
+        [share] * 2,
+        16,
+    )
     arrived[1] = exchange(beside, "head", 1)
     layer_out = own.astype(jnp.float32)
     for k in range(1, devices_head):

time: 41.6 us -> 41 us (0.986)
  waiting for transfers between devices: 11.2 us -> 10.7 us
    ppermute x13, waiting for transfers between devices: 11.2 us -> 10.7 us  [exchange(): return lax.ppermute(value, axis, [(i, i ^ step) for i in range(count)])]
  transfers between devices with their start and end apart: 13 -> 13, of which waited for: 6 -> 6; matrix products, arithmetic and copies ran while one was open for 1% -> 2% of each run, Pallas kernels for 21% -> 23%
where the time goes in v4:
time: 41 us; the launch traced here: 40.7 us
  starting transfers between devices  15.3 us (37%)
  Pallas kernels  12.7 us (31%)
  waiting for transfers between devices  10.7 us (26%)
  other arithmetic  1.26 us (3%)
  between operations  0.74 us (2%)
    ppermute x13, starting transfers between devices, exchange(): return lax.ppermute(value, axis, [(i, i ^ step) for i in range(count)])  15.3 us
    pallas_call x8, Pallas kernels, call(): pl.pallas_call(kernel, in_specs=specs, out_specs=[vmem] * len(shapes), ou...  11.9 us
    ppermute x13, waiting for transfers between devices, exchange(): return lax.ppermute(value, axis, [(i, i ^ step) for i in range(count)])  10.7 us
    pallas_call x1, Pallas kernels, per_device(): pl.pallas_call(functools.partial(payload_kernel, owners=devices_mem, all_...  0.84 us
  transfers between devices with their start and end apart: 13, of which 6 were waited for; matrix products, arithmetic and copies ran while one was open for 2% of the time, Pallas kernels for 23%

profile of v4, /device:TPU:0, one launch (start us, length us, event | category | flops | bytes accessed | tf_op | source)
XLA Modules:
  0.0 40.7 jit_solution(4276414086474958895)
XLA Ops:
  0.6 0.8 %payload.1._.refs_0_ = bf16[16,1152]{1,0:T(8,128)(2,1)S(1)} custom-call(bf16[16,8,128]{2,1,0:T(8,128)(2,1)} %queries_hbm.1, s32[16,32]{1,0:T(8,128)} %selected_hbm.1), custom_call_target="tpu_custom_call" | custom-call | tf_op jit(solution)/shard_map/payload/pallas_call | solution.py:246
  1.5 3.1 %collective-permute-start.3 = (bf16[16,1152]{1,0:T(8,128)(2,1)S(1)}, bf16[16,1152]{1,0:T(8,128)(2,1)S(1)}, u32[]{:S(2)}, u32[]{:S(2)}) collective-permute-start(bf16[16,1152]{1,0:T(8,128)(2,1)S(1)} %payload.1._.refs_0_), channel_id=1, source_target_pairs={{0,8},{4,12},{8,0},{12,4},{16,24},{20,28},{24,16},{28,20},{1,9},{5... | collective-permute-start | bytes 110600 | tf_op jit(solution)/shard_map/ppermute | solution.py:18
  4.6 2.5 %collective-permute-start.2 = (bf16[16,1152]{1,0:T(8,128)(2,1)S(1)}, bf16[16,1152]{1,0:T(8,128)(2,1)S(1)}, u32[]{:S(2)}, u32[]{:S(2)}) collective-permute-start(bf16[16,1152]{1,0:T(8,128)(2,1)S(1)} %payload.1._.refs_0_), channel_id=1, source_target_pairs={{0,24},{4,28},{8,16},{12,20},{16,8},{20,12},{24,0},{28,4},{1,25},{... | collective-permute-start | bytes 110600 | tf_op jit(solution)/shard_map/ppermute | solution.py:18
  7.1 0.1 collective-permute-start.1
  7.2 0.0 collective-permute-done.3
  7.2 3.7 %collective-permute-done.2 = bf16[16,1152]{1,0:T(8,128)(2,1)S(1)} collective-permute-done((bf16[16,1152]{1,0:T(8,128)(2,1)S(1)}, bf16[16,1152]{1,0:T(8,128)(2,1)S(1)}, u32[]{:S(2)}, u32[]{:S(2)}) %collective-permute-start.2) | collective-permute-done | bytes 36896 | tf_op jit(solution)/shard_map/ppermute | solution.py:18
  10.8 1.5 %collective-permute-done.1 = bf16[16,1152]{1,0:T(8,128)(2,1)S(1)} collective-permute-done((bf16[16,1152]{1,0:T(8,128)(2,1)S(1)}, bf16[16,1152]{1,0:T(8,128)(2,1)S(1)}, u32[]{:S(2)}, u32[]{:S(2)}) %collective-permute-start.1) | collective-permute-done | bytes 36896 | tf_op jit(solution)/shard_map/ppermute | solution.py:18
  12.3 1.6 %collective-permute-start.4 = (bf16[3,16,1152]{2,1,0:T(8,128)(2,1)S(1)}, bf16[3,16,1152]{2,1,0:T(8,128)(2,1)S(1)}, u32[]{:S(2)}, u32[]{:S(2)}) collective-permute-start(bf16[3,16,1152]{2,1,0:T(8,128)(2,1)S(1)} %pad_maximum_fusion.refs_2_), channel_id=1, source_target_pairs={{0,4},{4,0},{8,12},{12,8},{16,20},{20,16},{24,28},{28,24},{1,5},{5... | collective-permute-start | bytes 331784 | tf_op jit(solution)/shard_map/ppermute | solution.py:18
  13.9 0.5 %collective-permute-start = (bf16[16,1152]{1,0:T(8,128)(2,1)S(1)}, bf16[16,1152]{1,0:T(8,128)(2,1)S(1)}, u32[]{:S(2)}, u32[]{:S(2)}) collective-permute-start(bf16[16,1152]{1,0:T(8,128)(2,1)S(1)} %payload.1._.refs_0_), channel_id=1, source_target_pairs={{0,4},{4,0},{8,12},{12,8},{16,20},{20,16},{24,28},{28,24},{1,5},{5... | collective-permute-start | bytes 110600 | tf_op jit(solution)/shard_map/ppermute | solution.py:18
  14.4 1.6 %shard_map.68.refs_3_.refs_1_ = bf16[32,2,2,64,128]{4,3,2,1,0:T(8,128)(2,1)S(1)} custom-call(bf16[32,2,2,64,128]{4,3,2,1,0:T(8,128)(2,1)} %source_hbm.1, bf16[16,1152]{1,0:T(8,128)(2,1)S(1)} %payload.1._.refs_0_), custom_call_target="tpu_custom_call" | custom-call | tf_op jit(solution)/shard_map/pallas_call | solution.py:263
  16.0 0.0 copy-start
  16.1 1.8 %collective-permute-done.refs_1_ = bf16[16,1152]{1,0:T(8,128)(2,1)S(1)} collective-permute-done((bf16[16,1152]{1,0:T(8,128)(2,1)S(1)}, bf16[16,1152]{1,0:T(8,128)(2,1)S(1)}, u32[]{:S(2)}, u32[]{:S(2)}) %collective-permute-start) | collective-permute-done | bytes 36896 | tf_op jit(solution)/shard_map/ppermute | solution.py:18
  17.9 2.4 %shard_map.69 = (bf16[16,1152]{1,0:T(8,128)(2,1)S(1)}, bf16[16,1152]{1,0:T(8,128)(2,1)S(1)}, bf16[3,16,1152]{2,1,0:T(8,128)(2,1)S(1)}, f32[1,128]{1,0:T(1,128)S(1)}, bf16[2,256,2048]{2,1,0:T(8,128)(2,1)S(1)}) custom-call(bf16[16,1152]{1,0:T(8,128)(2,1)S(1)} %payload.1._.refs_0_, bf16[16,1152]{1,0:T(8,128)(2,1)S(1)} %collective-permute-done.refs_1_, ...), custom_call_target="tpu_custom_call" | custom-call | tf_op jit(solution)/shard_map/pallas_call | solution.py:263
  20.2 0.0 collective-permute-done.4.refs_0_
  20.3 1.6 %shard_map.70 = (bf16[3,16,1152]{2,1,0:T(8,128)(2,1)S(1)}, f32[1,128]{1,0:T(1,128)S(1)}) custom-call(bf16[3,16,1152]{2,1,0:T(8,128)(2,1)S(1)} %collective-permute-done.4.refs_0_, bf16[32,2,2,64,128]{4,3,2,1,0:T(8,128)(2,1)S(1)} %shard_map.68.refs_3_.refs_1_, bf16[2,256,2048]{2,1,0:T(8,128)(2,1)S(1)} %get-tuple-element.19.refs_2_), custom_call_target="tpu_custom_call" | custom-call | tf_op jit(solution)/shard_map/pallas_call | solution.py:263
  21.9 1.2 %collective-permute-start.5 = (bf16[3,16,1152]{2,1,0:T(8,128)(2,1)S(1)}, bf16[3,16,1152]{2,1,0:T(8,128)(2,1)S(1)}, u32[]{:S(2)}, u32[]{:S(2)}) collective-permute-start(bf16[3,16,1152]{2,1,0:T(8,128)(2,1)S(1)} %get-tuple-element.20._), channel_id=1, source_target_pairs={{0,4},{4,0},{8,12},{12,8},{16,20},{20,16},{24,28},{28,24},{1,5},{5... | collective-permute-start | bytes 331784 | tf_op jit(solution)/shard_map/ppermute | solution.py:18
  23.1 0.9 %collective-permute-start.9 = (bf16[16,1152]{1,0:T(8,128)(2,1)S(1)}, bf16[16,1152]{1,0:T(8,128)(2,1)S(1)}, u32[]{:S(2)}, u32[]{:S(2)}) collective-permute-start(bf16[16,1152]{1,0:T(8,128)(2,1)S(1)} %get-tuple-element.24), channel_id=1, source_target_pairs={{0,4},{4,0},{8,12},{12,8},{16,20},{20,16},{24,28},{28,24},{1,5},{5... | collective-permute-start | bytes 110600 | tf_op jit(solution)/shard_map/ppermute | solution.py:18
  24.0 2.7 %collective-permute-done.5.theirs_ref = bf16[3,16,1152]{2,1,0:T(8,128)(2,1)S(1)} collective-permute-done((bf16[3,16,1152]{2,1,0:T(8,128)(2,1)S(1)}, bf16[3,16,1152]{2,1,0:T(8,128)(2,1)S(1)}, u32[]{:S(2)}, u32[]{:S(2)}) %collective-permute-start.5) | collective-permute-done | bytes 110624 | tf_op jit(solution)/shard_map/ppermute | solution.py:18
  26.7 0.4 shard_map.71
  27.0 0.2 collective-permute-start.6
  27.2 2.6 %collective-permute-start.7 = (bf16[16,1152]{1,0:T(8,128)(2,1)S(1)}, bf16[16,1152]{1,0:T(8,128)(2,1)S(1)}, u32[]{:S(2)}, u32[]{:S(2)}) collective-permute-start(bf16[16,1152]{1,0:T(8,128)(2,1)S(1)} %get-tuple-element.22), channel_id=1, source_target_pairs={{0,24},{4,28},{8,16},{12,20},{16,8},{20,12},{24,0},{28,4},{1,25},{... | collective-permute-start | bytes 110600 | tf_op jit(solution)/shard_map/ppermute | solution.py:18
  29.8 0.7 %collective-permute-start.8 = (bf16[16,1152]{1,0:T(8,128)(2,1)S(1)}, bf16[16,1152]{1,0:T(8,128)(2,1)S(1)}, u32[]{:S(2)}, u32[]{:S(2)}) collective-permute-start(bf16[16,1152]{1,0:T(8,128)(2,1)S(1)} %get-tuple-element.23), channel_id=1, source_target_pairs={{0,8},{4,12},{8,0},{12,4},{16,24},{20,28},{24,16},{28,20},{1,9},{5... | collective-permute-start | bytes 110600 | tf_op jit(solution)/shard_map/ppermute | solution.py:18
  30.6 0.0 copy-done
  30.6 0.1 multiply_reduce_fusion
  30.7 2.2 %shard_map.72.refs_5_.refs_0_ = bf16[512,4096]{1,0:T(8,128)(2,1)S(1)} custom-call(bf16[1024,4096]{1,0:T(8,128)(2,1)} %weight_hbm.3, bf16[3,16,1152]{2,1,0:T(8,128)(2,1)S(1)} %get-tuple-element.20._), custom_call_target="tpu_custom_call" | custom-call | tf_op jit(solution)/shard_map/pallas_call | solution.py:263
  32.9 2.2 %shard_map.73.refs_6_.refs_1_ = bf16[512,4096]{1,0:T(8,128)(2,1)S(1)} custom-call(bf16[1024,4096]{1,0:T(8,128)(2,1)} %weight_hbm.3, bf16[16,1152]{1,0:T(8,128)(2,1)S(1)} %get-tuple-element.21._), custom_call_target="tpu_custom_call" | custom-call | tf_op jit(solution)/shard_map/pallas_call | solution.py:263
  35.1 0.0 collective-permute-done.9.refs_4_
  35.1 0.0 collective-permute-done.6.refs_1_
  35.1 0.0 collective-permute-done.7.refs_2_
  35.1 0.0 collective-permute-done.8.refs_3_
  35.1 0.9 %shard_map.74 = (bf16[16,1024]{1,0:T(8,128)(2,1)S(1)}, bf16[16,1024]{1,0:T(8,128)(2,1)S(1)}, bf16[16,1024]{1,0:T(8,128)(2,1)S(1)}) custom-call(bf16[16,1152]{1,0:T(8,128)(2,1)S(1)} %get-tuple-element.17.refs_0_, bf16[16,1152]{1,0:T(8,128)(2,1)S(1)} %collective-permute-done.6.refs_1_, bf16[16,1152]{1,0:T(8,128)(2,1)S(1)} %collective-permute-done.7.refs_2_, ...), custom_call_target="tpu_custom_call" | custom-call | tf_op jit(solution)/shard_map/pallas_call | solution.py:263
  36.0 0.0 collective-permute-start.12
  36.0 1.6 %collective-permute-start.11 = (bf16[16,1024]{1,0:T(8,128)(2,1)S(1)}, bf16[16,1024]{1,0:T(8,128)(2,1)S(1)}, u32[]{:S(2)}, u32[]{:S(2)}) collective-permute-start(bf16[16,1024]{1,0:T(8,128)(2,1)S(1)} %get-tuple-element.28), channel_id=1, source_target_pairs={{0,2},{1,3},{2,0},{3,1},{4,6},{5,7},{6,4},{7,5},{8,10},{9,11},{10,... | collective-permute-start | bytes 98312 | tf_op jit(solution)/shard_map/ppermute | solution.py:18
  37.6 0.6 %shard_map.75 = (bf16[16,1024]{1,0:T(8,128)(2,1)S(1)}, bf16[16,1024]{1,0:T(8,128)(2,1)S(1)}) custom-call(bf16[16,1024]{1,0:T(8,128)(2,1)S(1)} %get-tuple-element.25.attended_ref, bf16[512,4096]{1,0:T(8,128)(2,1)S(1)} %shard_map.72.refs_5_.refs_0_, bf16[512,4096]{1,0:T(8,128)(2,1)S(1)} %shard_map.73.refs_6_.refs_1_), custom_call_target="tpu_custom_call" | custom-call | tf_op jit(solution)/shard_map/pallas_call | solution.py:263
  38.2 0.3 collective-permute-start.10
  38.5 0.5 %bitcast_add_fusion = f32[32]{0:T(128)} fusion(f32[32]{0:T(128)S(1)} %multiply_reduce_fusion, f32[1,128]{1,0:T(1,128)S(1)} %add.18), kind=kLoop, calls=%fused_computation.3 | loop fusion | flops 32 | bytes 384 | tf_op jit(solution)/shard_map/add | solution.py:357
  39.0 0.6 %collective-permute-done.12 = bf16[16,1024]{1,0:T(8,128)(2,1)S(1)} collective-permute-done((bf16[16,1024]{1,0:T(8,128)(2,1)S(1)}, bf16[16,1024]{1,0:T(8,128)(2,1)S(1)}, u32[]{:S(2)}, u32[]{:S(2)}) %collective-permute-start.12) | collective-permute-done | bytes 32800 | tf_op jit(solution)/shard_map/ppermute | solution.py:18
  39.6 0.4 %collective-permute-done.11 = bf16[16,1024]{1,0:T(8,128)(2,1)S(1)} collective-permute-done((bf16[16,1024]{1,0:T(8,128)(2,1)S(1)}, bf16[16,1024]{1,0:T(8,128)(2,1)S(1)}, u32[]{:S(2)}, u32[]{:S(2)}) %collective-permute-start.11) | collective-permute-done | bytes 32800 | tf_op jit(solution)/shard_map/ppermute | solution.py:18
  40.1 0.0 collective-permute-done.10
  40.1 0.6 %add_convert_fusion = bf16[16,1024]{1,0:T(8,128)(2,1)} fusion(bf16[16,1024]{1,0:T(8,128)(2,1)S(1)} %collective-permute-done.12, bf16[16,1024]{1,0:T(8,128)(2,1)S(1)} %collective-permute-done.11, bf16[16,1024]{1,0:T(8,128)(2,1)S(1)} %collective-permute-done.10, bf16[16,1024]{1,0:T(8,128)(2,1)S(1)} %get-tuple-element.26), kind=kLoop, calls=%fused_computation.1 | loop fusion | flops 131072 | bytes 163840 | tf_op jit(solution)/shard_map/convert_element_type | solution.py:358
  (3 shorter events, 0.0 us)
Async XLA Ops:
  1.5 5.7 %collective-permute-start.3 = (bf16[16,1152]{1,0:T(8,128)(2,1)S(1)}, bf16[16,1152]{1,0:T(8,128)(2,1)S(1)}, u32[]{:S(2)}, u32[]{:S(2)}) collective-permute-start(bf16[16,1152]{1,0:T(8,128)(2,1)S(1)} %payload.1._.refs_0_), channel_id=1, source_target_pairs={{0,8},{4,12},{8,0},{12,4},{16,24},{20,28},{24,16},{28,20},{1,9},{5... | collective-permute-start | bytes 110600 | tf_op jit(solution)/shard_map/ppermute | solution.py:18
  4.6 6.2 %collective-permute-start.2 = (bf16[16,1152]{1,0:T(8,128)(2,1)S(1)}, bf16[16,1152]{1,0:T(8,128)(2,1)S(1)}, u32[]{:S(2)}, u32[]{:S(2)}) collective-permute-start(bf16[16,1152]{1,0:T(8,128)(2,1)S(1)} %payload.1._.refs_0_), channel_id=1, source_target_pairs={{0,24},{4,28},{8,16},{12,20},{16,8},{20,12},{24,0},{28,4},{1,25},{... | collective-permute-start | bytes 110600 | tf_op jit(solution)/shard_map/ppermute | solution.py:18
  7.1 5.3 %collective-permute-start.1 = (bf16[16,1152]{1,0:T(8,128)(2,1)S(1)}, bf16[16,1152]{1,0:T(8,128)(2,1)S(1)}, u32[]{:S(2)}, u32[]{:S(2)}) collective-permute-start(bf16[16,1152]{1,0:T(8,128)(2,1)S(1)} %payload.1._.refs_0_), channel_id=1, source_target_pairs={{0,16},{4,20},{8,24},{12,28},{16,0},{20,4},{24,8},{28,12},{1,17},{... | collective-permute-start | bytes 110600 | tf_op jit(solution)/shard_map/ppermute | solution.py:18
  12.3 7.9 %collective-permute-start.4 = (bf16[3,16,1152]{2,1,0:T(8,128)(2,1)S(1)}, bf16[3,16,1152]{2,1,0:T(8,128)(2,1)S(1)}, u32[]{:S(2)}, u32[]{:S(2)}) collective-permute-start(bf16[3,16,1152]{2,1,0:T(8,128)(2,1)S(1)} %pad_maximum_fusion.refs_2_), channel_id=1, source_target_pairs={{0,4},{4,0},{8,12},{12,8},{16,20},{20,16},{24,28},{28,24},{1,5},{5... | collective-permute-start | bytes 331784 | tf_op jit(solution)/shard_map/ppermute | solution.py:18
  13.9 4.0 %collective-permute-start = (bf16[16,1152]{1,0:T(8,128)(2,1)S(1)}, bf16[16,1152]{1,0:T(8,128)(2,1)S(1)}, u32[]{:S(2)}, u32[]{:S(2)}) collective-permute-start(bf16[16,1152]{1,0:T(8,128)(2,1)S(1)} %payload.1._.refs_0_), channel_id=1, source_target_pairs={{0,4},{4,0},{8,12},{12,8},{16,20},{20,16},{24,28},{28,24},{1,5},{5... | collective-permute-start | bytes 110600 | tf_op jit(solution)/shard_map/ppermute | solution.py:18
  16.0 14.5 %copy-start = (s32[16,32]{1,0:T(8,128)S(1)}, s32[16,32]{1,0:T(8,128)}, u32[]{:S(2)}) copy-start(s32[16,32]{1,0:T(8,128)} %param.8) | copy-start | bytes 6148
  21.9 4.8 %collective-permute-start.5 = (bf16[3,16,1152]{2,1,0:T(8,128)(2,1)S(1)}, bf16[3,16,1152]{2,1,0:T(8,128)(2,1)S(1)}, u32[]{:S(2)}, u32[]{:S(2)}) collective-permute-start(bf16[3,16,1152]{2,1,0:T(8,128)(2,1)S(1)} %get-tuple-element.20._), channel_id=1, source_target_pairs={{0,4},{4,0},{8,12},{12,8},{16,20},{20,16},{24,28},{28,24},{1,5},{5... | collective-permute-start | bytes 331784 | tf_op jit(solution)/shard_map/ppermute | solution.py:18
  23.1 12.0 %collective-permute-start.9 = (bf16[16,1152]{1,0:T(8,128)(2,1)S(1)}, bf16[16,1152]{1,0:T(8,128)(2,1)S(1)}, u32[]{:S(2)}, u32[]{:S(2)}) collective-permute-start(bf16[16,1152]{1,0:T(8,128)(2,1)S(1)} %get-tuple-element.24), channel_id=1, source_target_pairs={{0,4},{4,0},{8,12},{12,8},{16,20},{20,16},{24,28},{28,24},{1,5},{5... | collective-permute-start | bytes 110600 | tf_op jit(solution)/shard_map/ppermute | solution.py:18
  27.0 8.1 %collective-permute-start.6 = (bf16[16,1152]{1,0:T(8,128)(2,1)S(1)}, bf16[16,1152]{1,0:T(8,128)(2,1)S(1)}, u32[]{:S(2)}, u32[]{:S(2)}) collective-permute-start(bf16[16,1152]{1,0:T(8,128)(2,1)S(1)} %get-tuple-element.21._), channel_id=1, source_target_pairs={{0,16},{4,20},{8,24},{12,28},{16,0},{20,4},{24,8},{28,12},{1,17},{... | collective-permute-start | bytes 110600 | tf_op jit(solution)/shard_map/ppermute | solution.py:18
  27.2 7.9 %collective-permute-start.7 = (bf16[16,1152]{1,0:T(8,128)(2,1)S(1)}, bf16[16,1152]{1,0:T(8,128)(2,1)S(1)}, u32[]{:S(2)}, u32[]{:S(2)}) collective-permute-start(bf16[16,1152]{1,0:T(8,128)(2,1)S(1)} %get-tuple-element.22), channel_id=1, source_target_pairs={{0,24},{4,28},{8,16},{12,20},{16,8},{20,12},{24,0},{28,4},{1,25},{... | collective-permute-start | bytes 110600 | tf_op jit(solution)/shard_map/ppermute | solution.py:18
  29.8 5.3 %collective-permute-start.8 = (bf16[16,1152]{1,0:T(8,128)(2,1)S(1)}, bf16[16,1152]{1,0:T(8,128)(2,1)S(1)}, u32[]{:S(2)}, u32[]{:S(2)}) collective-permute-start(bf16[16,1152]{1,0:T(8,128)(2,1)S(1)} %get-tuple-element.23), channel_id=1, source_target_pairs={{0,8},{4,12},{8,0},{12,4},{16,24},{20,28},{24,16},{28,20},{1,9},{5... | collective-permute-start | bytes 110600 | tf_op jit(solution)/shard_map/ppermute | solution.py:18
  36.0 3.6 %collective-permute-start.12 = (bf16[16,1024]{1,0:T(8,128)(2,1)S(1)}, bf16[16,1024]{1,0:T(8,128)(2,1)S(1)}, u32[]{:S(2)}, u32[]{:S(2)}) collective-permute-start(bf16[16,1024]{1,0:T(8,128)(2,1)S(1)} %get-tuple-element.29), channel_id=1, source_target_pairs={{0,3},{1,2},{2,1},{3,0},{4,7},{5,6},{6,5},{7,4},{8,11},{9,10},{10,... | collective-permute-start | bytes 98312 | tf_op jit(solution)/shard_map/ppermute | solution.py:18
  36.0 4.0 %collective-permute-start.11 = (bf16[16,1024]{1,0:T(8,128)(2,1)S(1)}, bf16[16,1024]{1,0:T(8,128)(2,1)S(1)}, u32[]{:S(2)}, u32[]{:S(2)}) collective-permute-start(bf16[16,1024]{1,0:T(8,128)(2,1)S(1)} %get-tuple-element.28), channel_id=1, source_target_pairs={{0,2},{1,3},{2,0},{3,1},{4,6},{5,7},{6,4},{7,5},{8,10},{9,11},{10,... | collective-permute-start | bytes 98312 | tf_op jit(solution)/shard_map/ppermute | solution.py:18
  38.2 1.8 %collective-permute-start.10 = (bf16[16,1024]{1,0:T(8,128)(2,1)S(1)}, bf16[16,1024]{1,0:T(8,128)(2,1)S(1)}, u32[]{:S(2)}, u32[]{:S(2)}) collective-permute-start(bf16[16,1024]{1,0:T(8,128)(2,1)S(1)} %get-tuple-element.27), channel_id=1, source_target_pairs={{0,1},{1,0},{2,3},{3,2},{4,5},{5,4},{6,7},{7,6},{8,9},{9,8},{10,11... | collective-permute-start | bytes 98312 | tf_op jit(solution)/shard_map/ppermute | solution.py:18

commit v5 on v4

--- a/solution.py
+++ b/solution.py
@@ -329,8 +329,15 @@
         8,
     )
     returned = [own] + [exchange(m, "mem", k) for k, m in zip(even, merged)]
-    returned.append(returned_beside)
     weight_near = stage_rows(half, merged[0])
+    (local,) = call(
+        functools.partial(merge_kernel, heads=heads),
+        (own[None], returned_beside[None]),
+        [vmem] * 2,
+        [message],
+        8,
+    )
+    returned = [local] + returned[1:]
     share = jax.ShapeDtypeStruct((rows, columns), jnp.bfloat16)
     attended, *far = call(
         functools.partial(

time: 41 us -> 41.3 us (level)
    pallas_call x8 -> x9, Pallas kernels: 11.9 us -> 12.2 us  [call(): pl.pallas_call(kernel, in_specs=specs, out_specs=[vmem] * len(shapes), ou...]
  transfers between devices with their start and end apart: 13 -> 13, of which waited for: 6 -> 6; matrix products, arithmetic and copies ran while one was open for 2% -> 1% of each run, Pallas kernels for 23% -> 24%
where the time goes in v5:
time: 41.3 us; the launch traced here: 41 us
  starting transfers between devices  15.3 us (37%)
  Pallas kernels  13 us (31%)
  waiting for transfers between devices  10.7 us (26%)
  other arithmetic  1.26 us (3%)
  between operations  0.74 us (2%)
    ppermute x13, starting transfers between devices, exchange(): return lax.ppermute(value, axis, [(i, i ^ step) for i in range(count)])  15.3 us
    pallas_call x9, Pallas kernels, call(): pl.pallas_call(kernel, in_specs=specs, out_specs=[vmem] * len(shapes), ou...  12.2 us
    ppermute x13, waiting for transfers between devices, exchange(): return lax.ppermute(value, axis, [(i, i ^ step) for i in range(count)])  10.7 us
    pallas_call x1, Pallas kernels, per_device(): pl.pallas_call(functools.partial(payload_kernel, owners=devices_mem, all_...  0.84 us
  transfers between devices with their start and end apart: 13, of which 6 were waited for; matrix products, arithmetic and copies ran while one was open for 1% of the time, Pallas kernels for 24%

profile of v5, /device:TPU:0, one launch (start us, length us, event | category | flops | bytes accessed | tf_op | source)
XLA Modules:
  0.0 41.0 jit_solution(7161281239304777267)
XLA Ops:
  0.6 0.8 %payload.1._.refs_0_ = bf16[16,1152]{1,0:T(8,128)(2,1)S(1)} custom-call(bf16[16,8,128]{2,1,0:T(8,128)(2,1)} %queries_hbm.1, s32[16,32]{1,0:T(8,128)} %selected_hbm.1), custom_call_target="tpu_custom_call" | custom-call | tf_op jit(solution)/shard_map/payload/pallas_call | solution.py:246
  1.5 3.1 %collective-permute-start.3 = (bf16[16,1152]{1,0:T(8,128)(2,1)S(1)}, bf16[16,1152]{1,0:T(8,128)(2,1)S(1)}, u32[]{:S(2)}, u32[]{:S(2)}) collective-permute-start(bf16[16,1152]{1,0:T(8,128)(2,1)S(1)} %payload.1._.refs_0_), channel_id=1, source_target_pairs={{0,8},{4,12},{8,0},{12,4},{16,24},{20,28},{24,16},{28,20},{1,9},{5... | collective-permute-start | bytes 110600 | tf_op jit(solution)/shard_map/ppermute | solution.py:18
  4.6 2.5 %collective-permute-start.2 = (bf16[16,1152]{1,0:T(8,128)(2,1)S(1)}, bf16[16,1152]{1,0:T(8,128)(2,1)S(1)}, u32[]{:S(2)}, u32[]{:S(2)}) collective-permute-start(bf16[16,1152]{1,0:T(8,128)(2,1)S(1)} %payload.1._.refs_0_), channel_id=1, source_target_pairs={{0,24},{4,28},{8,16},{12,20},{16,8},{20,12},{24,0},{28,4},{1,25},{... | collective-permute-start | bytes 110600 | tf_op jit(solution)/shard_map/ppermute | solution.py:18
  7.1 0.1 collective-permute-start.1
  7.2 0.0 collective-permute-done.3
  7.2 3.7 %collective-permute-done.2 = bf16[16,1152]{1,0:T(8,128)(2,1)S(1)} collective-permute-done((bf16[16,1152]{1,0:T(8,128)(2,1)S(1)}, bf16[16,1152]{1,0:T(8,128)(2,1)S(1)}, u32[]{:S(2)}, u32[]{:S(2)}) %collective-permute-start.2) | collective-permute-done | bytes 36896 | tf_op jit(solution)/shard_map/ppermute | solution.py:18
  10.8 1.5 %collective-permute-done.1 = bf16[16,1152]{1,0:T(8,128)(2,1)S(1)} collective-permute-done((bf16[16,1152]{1,0:T(8,128)(2,1)S(1)}, bf16[16,1152]{1,0:T(8,128)(2,1)S(1)}, u32[]{:S(2)}, u32[]{:S(2)}) %collective-permute-start.1) | collective-permute-done | bytes 36896 | tf_op jit(solution)/shard_map/ppermute | solution.py:18
  12.3 1.6 %collective-permute-start.5 = (bf16[3,16,1152]{2,1,0:T(8,128)(2,1)S(1)}, bf16[3,16,1152]{2,1,0:T(8,128)(2,1)S(1)}, u32[]{:S(2)}, u32[]{:S(2)}) collective-permute-start(bf16[3,16,1152]{2,1,0:T(8,128)(2,1)S(1)} %pad_maximum_fusion.refs_2_), channel_id=1, source_target_pairs={{0,4},{4,0},{8,12},{12,8},{16,20},{20,16},{24,28},{28,24},{1,5},{5... | collective-permute-start | bytes 331784 | tf_op jit(solution)/shard_map/ppermute | solution.py:18
  13.9 0.5 %collective-permute-start = (bf16[16,1152]{1,0:T(8,128)(2,1)S(1)}, bf16[16,1152]{1,0:T(8,128)(2,1)S(1)}, u32[]{:S(2)}, u32[]{:S(2)}) collective-permute-start(bf16[16,1152]{1,0:T(8,128)(2,1)S(1)} %payload.1._.refs_0_), channel_id=1, source_target_pairs={{0,4},{4,0},{8,12},{12,8},{16,20},{20,16},{24,28},{28,24},{1,5},{5... | collective-permute-start | bytes 110600 | tf_op jit(solution)/shard_map/ppermute | solution.py:18
  14.4 1.6 %shard_map.68.refs_3_.refs_1_ = bf16[32,2,2,64,128]{4,3,2,1,0:T(8,128)(2,1)S(1)} custom-call(bf16[32,2,2,64,128]{4,3,2,1,0:T(8,128)(2,1)} %source_hbm.1, bf16[16,1152]{1,0:T(8,128)(2,1)S(1)} %payload.1._.refs_0_), custom_call_target="tpu_custom_call" | custom-call | tf_op jit(solution)/shard_map/pallas_call | solution.py:263
  16.0 0.0 copy-start
  16.1 1.8 %collective-permute-done.refs_1_ = bf16[16,1152]{1,0:T(8,128)(2,1)S(1)} collective-permute-done((bf16[16,1152]{1,0:T(8,128)(2,1)S(1)}, bf16[16,1152]{1,0:T(8,128)(2,1)S(1)}, u32[]{:S(2)}, u32[]{:S(2)}) %collective-permute-start) | collective-permute-done | bytes 36896 | tf_op jit(solution)/shard_map/ppermute | solution.py:18
  17.9 2.4 %shard_map.69 = (bf16[16,1152]{1,0:T(8,128)(2,1)S(1)}, bf16[16,1152]{1,0:T(8,128)(2,1)S(1)}, bf16[3,16,1152]{2,1,0:T(8,128)(2,1)S(1)}, f32[1,128]{1,0:T(1,128)S(1)}, bf16[2,256,2048]{2,1,0:T(8,128)(2,1)S(1)}) custom-call(bf16[16,1152]{1,0:T(8,128)(2,1)S(1)} %payload.1._.refs_0_, bf16[16,1152]{1,0:T(8,128)(2,1)S(1)} %collective-permute-done.refs_1_, ...), custom_call_target="tpu_custom_call" | custom-call | tf_op jit(solution)/shard_map/pallas_call | solution.py:263
  20.2 0.0 collective-permute-done.5.refs_0_
  20.3 1.6 %shard_map.71 = (bf16[3,16,1152]{2,1,0:T(8,128)(2,1)S(1)}, f32[1,128]{1,0:T(1,128)S(1)}) custom-call(bf16[3,16,1152]{2,1,0:T(8,128)(2,1)S(1)} %collective-permute-done.5.refs_0_, bf16[32,2,2,64,128]{4,3,2,1,0:T(8,128)(2,1)S(1)} %shard_map.68.refs_3_.refs_1_, bf16[2,256,2048]{2,1,0:T(8,128)(2,1)S(1)} %get-tuple-element.20.refs_2_), custom_call_target="tpu_custom_call" | custom-call | tf_op jit(solution)/shard_map/pallas_call | solution.py:263
  21.9 1.2 %collective-permute-start.6 = (bf16[3,16,1152]{2,1,0:T(8,128)(2,1)S(1)}, bf16[3,16,1152]{2,1,0:T(8,128)(2,1)S(1)}, u32[]{:S(2)}, u32[]{:S(2)}) collective-permute-start(bf16[3,16,1152]{2,1,0:T(8,128)(2,1)S(1)} %get-tuple-element.21._), channel_id=1, source_target_pairs={{0,4},{4,0},{8,12},{12,8},{16,20},{20,16},{24,28},{28,24},{1,5},{5... | collective-permute-start | bytes 331784 | tf_op jit(solution)/shard_map/ppermute | solution.py:18
  23.1 0.9 %collective-permute-start.4 = (bf16[16,1152]{1,0:T(8,128)(2,1)S(1)}, bf16[16,1152]{1,0:T(8,128)(2,1)S(1)}, u32[]{:S(2)}, u32[]{:S(2)}) collective-permute-start(bf16[16,1152]{1,0:T(8,128)(2,1)S(1)} %get-tuple-element.18), channel_id=1, source_target_pairs={{0,4},{4,0},{8,12},{12,8},{16,20},{20,16},{24,28},{28,24},{1,5},{5... | collective-permute-start | bytes 110600 | tf_op jit(solution)/shard_map/ppermute | solution.py:18
  24.0 2.7 %collective-permute-done.6.theirs_ref = bf16[3,16,1152]{2,1,0:T(8,128)(2,1)S(1)} collective-permute-done((bf16[3,16,1152]{2,1,0:T(8,128)(2,1)S(1)}, bf16[3,16,1152]{2,1,0:T(8,128)(2,1)S(1)}, u32[]{:S(2)}, u32[]{:S(2)}) %collective-permute-start.6) | collective-permute-done | bytes 110624 | tf_op jit(solution)/shard_map/ppermute | solution.py:18
  26.7 0.4 shard_map.72
  27.0 0.2 collective-permute-start.7
  27.2 2.6 %collective-permute-start.8 = (bf16[16,1152]{1,0:T(8,128)(2,1)S(1)}, bf16[16,1152]{1,0:T(8,128)(2,1)S(1)}, u32[]{:S(2)}, u32[]{:S(2)}) collective-permute-start(bf16[16,1152]{1,0:T(8,128)(2,1)S(1)} %get-tuple-element.23), channel_id=1, source_target_pairs={{0,24},{4,28},{8,16},{12,20},{16,8},{20,12},{24,0},{28,4},{1,25},{... | collective-permute-start | bytes 110600 | tf_op jit(solution)/shard_map/ppermute | solution.py:18
  29.8 0.7 %collective-permute-start.9 = (bf16[16,1152]{1,0:T(8,128)(2,1)S(1)}, bf16[16,1152]{1,0:T(8,128)(2,1)S(1)}, u32[]{:S(2)}, u32[]{:S(2)}) collective-permute-start(bf16[16,1152]{1,0:T(8,128)(2,1)S(1)} %get-tuple-element.24), channel_id=1, source_target_pairs={{0,8},{4,12},{8,0},{12,4},{16,24},{20,28},{24,16},{28,20},{1,9},{5... | collective-permute-start | bytes 110600 | tf_op jit(solution)/shard_map/ppermute | solution.py:18
  30.6 0.0 copy-done
  30.6 0.1 multiply_reduce_fusion
  30.7 0.0 collective-permute-done.4
  30.7 0.3 shard_map.70.refs_0_
  30.9 2.2 %shard_map.73.refs_4_.refs_0_ = bf16[512,4096]{1,0:T(8,128)(2,1)S(1)} custom-call(bf16[1024,4096]{1,0:T(8,128)(2,1)} %weight_hbm.3, bf16[3,16,1152]{2,1,0:T(8,128)(2,1)S(1)} %get-tuple-element.21._), custom_call_target="tpu_custom_call" | custom-call | tf_op jit(solution)/shard_map/pallas_call | solution.py:263
  33.2 2.2 %shard_map.74.refs_5_.refs_1_ = bf16[512,4096]{1,0:T(8,128)(2,1)S(1)} custom-call(bf16[1024,4096]{1,0:T(8,128)(2,1)} %weight_hbm.3, bf16[16,1152]{1,0:T(8,128)(2,1)S(1)} %get-tuple-element.22._), custom_call_target="tpu_custom_call" | custom-call | tf_op jit(solution)/shard_map/pallas_call | solution.py:263
  35.4 0.0 collective-permute-done.7.refs_1_
  35.4 0.0 collective-permute-done.8.refs_2_
  35.4 0.0 collective-permute-done.9.refs_3_
  35.4 0.9 %shard_map.75 = (bf16[16,1024]{1,0:T(8,128)(2,1)S(1)}, bf16[16,1024]{1,0:T(8,128)(2,1)S(1)}, bf16[16,1024]{1,0:T(8,128)(2,1)S(1)}) custom-call(bf16[16,1152]{1,0:T(8,128)(2,1)S(1)} %shard_map.70.refs_0_, bf16[16,1152]{1,0:T(8,128)(2,1)S(1)} %collective-permute-done.7.refs_1_, bf16[16,1152]{1,0:T(8,128)(2,1)S(1)} %collective-permute-done.8.refs_2_, ...), custom_call_target="tpu_custom_call" | custom-call | tf_op jit(solution)/shard_map/pallas_call | solution.py:263
  36.3 0.0 collective-permute-start.12
  36.3 1.6 %collective-permute-start.11 = (bf16[16,1024]{1,0:T(8,128)(2,1)S(1)}, bf16[16,1024]{1,0:T(8,128)(2,1)S(1)}, u32[]{:S(2)}, u32[]{:S(2)}) collective-permute-start(bf16[16,1024]{1,0:T(8,128)(2,1)S(1)} %get-tuple-element.28), channel_id=1, source_target_pairs={{0,2},{1,3},{2,0},{3,1},{4,6},{5,7},{6,4},{7,5},{8,10},{9,11},{10,... | collective-permute-start | bytes 98312 | tf_op jit(solution)/shard_map/ppermute | solution.py:18
  37.9 0.6 %shard_map.76 = (bf16[16,1024]{1,0:T(8,128)(2,1)S(1)}, bf16[16,1024]{1,0:T(8,128)(2,1)S(1)}) custom-call(bf16[16,1024]{1,0:T(8,128)(2,1)S(1)} %get-tuple-element.25.attended_ref, bf16[512,4096]{1,0:T(8,128)(2,1)S(1)} %shard_map.73.refs_4_.refs_0_, bf16[512,4096]{1,0:T(8,128)(2,1)S(1)} %shard_map.74.refs_5_.refs_1_), custom_call_target="tpu_custom_call" | custom-call | tf_op jit(solution)/shard_map/pallas_call | solution.py:263
  38.5 0.3 collective-permute-start.10
  38.8 0.5 %bitcast_add_fusion = f32[32]{0:T(128)} fusion(f32[32]{0:T(128)S(1)} %multiply_reduce_fusion, f32[1,128]{1,0:T(1,128)S(1)} %add.18), kind=kLoop, calls=%fused_computation.3 | loop fusion | flops 32 | bytes 384 | tf_op jit(solution)/shard_map/add | solution.py:364
  39.3 0.6 %collective-permute-done.12 = bf16[16,1024]{1,0:T(8,128)(2,1)S(1)} collective-permute-done((bf16[16,1024]{1,0:T(8,128)(2,1)S(1)}, bf16[16,1024]{1,0:T(8,128)(2,1)S(1)}, u32[]{:S(2)}, u32[]{:S(2)}) %collective-permute-start.12) | collective-permute-done | bytes 32800 | tf_op jit(solution)/shard_map/ppermute | solution.py:18
  39.9 0.4 %collective-permute-done.11 = bf16[16,1024]{1,0:T(8,128)(2,1)S(1)} collective-permute-done((bf16[16,1024]{1,0:T(8,128)(2,1)S(1)}, bf16[16,1024]{1,0:T(8,128)(2,1)S(1)}, u32[]{:S(2)}, u32[]{:S(2)}) %collective-permute-start.11) | collective-permute-done | bytes 32800 | tf_op jit(solution)/shard_map/ppermute | solution.py:18
  40.3 0.0 collective-permute-done.10
  40.3 0.6 %add_convert_fusion = bf16[16,1024]{1,0:T(8,128)(2,1)} fusion(bf16[16,1024]{1,0:T(8,128)(2,1)S(1)} %collective-permute-done.12, bf16[16,1024]{1,0:T(8,128)(2,1)S(1)} %collective-permute-done.11, bf16[16,1024]{1,0:T(8,128)(2,1)S(1)} %collective-permute-done.10, bf16[16,1024]{1,0:T(8,128)(2,1)S(1)} %get-tuple-element.26), kind=kLoop, calls=%fused_computation.1 | loop fusion | flops 131072 | bytes 163840 | tf_op jit(solution)/shard_map/convert_element_type | solution.py:365
  (3 shorter events, 0.0 us)
Async XLA Ops:
  1.5 5.7 %collective-permute-start.3 = (bf16[16,1152]{1,0:T(8,128)(2,1)S(1)}, bf16[16,1152]{1,0:T(8,128)(2,1)S(1)}, u32[]{:S(2)}, u32[]{:S(2)}) collective-permute-start(bf16[16,1152]{1,0:T(8,128)(2,1)S(1)} %payload.1._.refs_0_), channel_id=1, source_target_pairs={{0,8},{4,12},{8,0},{12,4},{16,24},{20,28},{24,16},{28,20},{1,9},{5... | collective-permute-start | bytes 110600 | tf_op jit(solution)/shard_map/ppermute | solution.py:18
  4.6 6.2 %collective-permute-start.2 = (bf16[16,1152]{1,0:T(8,128)(2,1)S(1)}, bf16[16,1152]{1,0:T(8,128)(2,1)S(1)}, u32[]{:S(2)}, u32[]{:S(2)}) collective-permute-start(bf16[16,1152]{1,0:T(8,128)(2,1)S(1)} %payload.1._.refs_0_), channel_id=1, source_target_pairs={{0,24},{4,28},{8,16},{12,20},{16,8},{20,12},{24,0},{28,4},{1,25},{... | collective-permute-start | bytes 110600 | tf_op jit(solution)/shard_map/ppermute | solution.py:18
  7.1 5.3 %collective-permute-start.1 = (bf16[16,1152]{1,0:T(8,128)(2,1)S(1)}, bf16[16,1152]{1,0:T(8,128)(2,1)S(1)}, u32[]{:S(2)}, u32[]{:S(2)}) collective-permute-start(bf16[16,1152]{1,0:T(8,128)(2,1)S(1)} %payload.1._.refs_0_), channel_id=1, source_target_pairs={{0,16},{4,20},{8,24},{12,28},{16,0},{20,4},{24,8},{28,12},{1,17},{... | collective-permute-start | bytes 110600 | tf_op jit(solution)/shard_map/ppermute | solution.py:18
  12.3 7.9 %collective-permute-start.5 = (bf16[3,16,1152]{2,1,0:T(8,128)(2,1)S(1)}, bf16[3,16,1152]{2,1,0:T(8,128)(2,1)S(1)}, u32[]{:S(2)}, u32[]{:S(2)}) collective-permute-start(bf16[3,16,1152]{2,1,0:T(8,128)(2,1)S(1)} %pad_maximum_fusion.refs_2_), channel_id=1, source_target_pairs={{0,4},{4,0},{8,12},{12,8},{16,20},{20,16},{24,28},{28,24},{1,5},{5... | collective-permute-start | bytes 331784 | tf_op jit(solution)/shard_map/ppermute | solution.py:18
  13.9 4.0 %collective-permute-start = (bf16[16,1152]{1,0:T(8,128)(2,1)S(1)}, bf16[16,1152]{1,0:T(8,128)(2,1)S(1)}, u32[]{:S(2)}, u32[]{:S(2)}) collective-permute-start(bf16[16,1152]{1,0:T(8,128)(2,1)S(1)} %payload.1._.refs_0_), channel_id=1, source_target_pairs={{0,4},{4,0},{8,12},{12,8},{16,20},{20,16},{24,28},{28,24},{1,5},{5... | collective-permute-start | bytes 110600 | tf_op jit(solution)/shard_map/ppermute | solution.py:18
  16.0 14.5 %copy-start = (s32[16,32]{1,0:T(8,128)S(1)}, s32[16,32]{1,0:T(8,128)}, u32[]{:S(2)}) copy-start(s32[16,32]{1,0:T(8,128)} %param.8) | copy-start | bytes 6148
  21.9 4.8 %collective-permute-start.6 = (bf16[3,16,1152]{2,1,0:T(8,128)(2,1)S(1)}, bf16[3,16,1152]{2,1,0:T(8,128)(2,1)S(1)}, u32[]{:S(2)}, u32[]{:S(2)}) collective-permute-start(bf16[3,16,1152]{2,1,0:T(8,128)(2,1)S(1)} %get-tuple-element.21._), channel_id=1, source_target_pairs={{0,4},{4,0},{8,12},{12,8},{16,20},{20,16},{24,28},{28,24},{1,5},{5... | collective-permute-start | bytes 331784 | tf_op jit(solution)/shard_map/ppermute | solution.py:18
  23.1 7.6 %collective-permute-start.4 = (bf16[16,1152]{1,0:T(8,128)(2,1)S(1)}, bf16[16,1152]{1,0:T(8,128)(2,1)S(1)}, u32[]{:S(2)}, u32[]{:S(2)}) collective-permute-start(bf16[16,1152]{1,0:T(8,128)(2,1)S(1)} %get-tuple-element.18), channel_id=1, source_target_pairs={{0,4},{4,0},{8,12},{12,8},{16,20},{20,16},{24,28},{28,24},{1,5},{5... | collective-permute-start | bytes 110600 | tf_op jit(solution)/shard_map/ppermute | solution.py:18
  27.0 8.3 %collective-permute-start.7 = (bf16[16,1152]{1,0:T(8,128)(2,1)S(1)}, bf16[16,1152]{1,0:T(8,128)(2,1)S(1)}, u32[]{:S(2)}, u32[]{:S(2)}) collective-permute-start(bf16[16,1152]{1,0:T(8,128)(2,1)S(1)} %get-tuple-element.22._), channel_id=1, source_target_pairs={{0,16},{4,20},{8,24},{12,28},{16,0},{20,4},{24,8},{28,12},{1,17},{... | collective-permute-start | bytes 110600 | tf_op jit(solution)/shard_map/ppermute | solution.py:18
  27.2 8.1 %collective-permute-start.8 = (bf16[16,1152]{1,0:T(8,128)(2,1)S(1)}, bf16[16,1152]{1,0:T(8,128)(2,1)S(1)}, u32[]{:S(2)}, u32[]{:S(2)}) collective-permute-start(bf16[16,1152]{1,0:T(8,128)(2,1)S(1)} %get-tuple-element.23), channel_id=1, source_target_pairs={{0,24},{4,28},{8,16},{12,20},{16,8},{20,12},{24,0},{28,4},{1,25},{... | collective-permute-start | bytes 110600 | tf_op jit(solution)/shard_map/ppermute | solution.py:18
  29.8 5.6 %collective-permute-start.9 = (bf16[16,1152]{1,0:T(8,128)(2,1)S(1)}, bf16[16,1152]{1,0:T(8,128)(2,1)S(1)}, u32[]{:S(2)}, u32[]{:S(2)}) collective-permute-start(bf16[16,1152]{1,0:T(8,128)(2,1)S(1)} %get-tuple-element.24), channel_id=1, source_target_pairs={{0,8},{4,12},{8,0},{12,4},{16,24},{20,28},{24,16},{28,20},{1,9},{5... | collective-permute-start | bytes 110600 | tf_op jit(solution)/shard_map/ppermute | solution.py:18
  36.3 3.6 %collective-permute-start.12 = (bf16[16,1024]{1,0:T(8,128)(2,1)S(1)}, bf16[16,1024]{1,0:T(8,128)(2,1)S(1)}, u32[]{:S(2)}, u32[]{:S(2)}) collective-permute-start(bf16[16,1024]{1,0:T(8,128)(2,1)S(1)} %get-tuple-element.29), channel_id=1, source_target_pairs={{0,3},{1,2},{2,1},{3,0},{4,7},{5,6},{6,5},{7,4},{8,11},{9,10},{10,... | collective-permute-start | bytes 98312 | tf_op jit(solution)/shard_map/ppermute | solution.py:18
  36.3 4.0 %collective-permute-start.11 = (bf16[16,1024]{1,0:T(8,128)(2,1)S(1)}, bf16[16,1024]{1,0:T(8,128)(2,1)S(1)}, u32[]{:S(2)}, u32[]{:S(2)}) collective-permute-start(bf16[16,1024]{1,0:T(8,128)(2,1)S(1)} %get-tuple-element.28), channel_id=1, source_target_pairs={{0,2},{1,3},{2,0},{3,1},{4,6},{5,7},{6,4},{7,5},{8,10},{9,11},{10,... | collective-permute-start | bytes 98312 | tf_op jit(solution)/shard_map/ppermute | solution.py:18
  38.5 1.8 %collective-permute-start.10 = (bf16[16,1024]{1,0:T(8,128)(2,1)S(1)}, bf16[16,1024]{1,0:T(8,128)(2,1)S(1)}, u32[]{:S(2)}, u32[]{:S(2)}) collective-permute-start(bf16[16,1024]{1,0:T(8,128)(2,1)S(1)} %get-tuple-element.27), channel_id=1, source_target_pairs={{0,1},{1,0},{2,3},{3,2},{4,5},{5,4},{6,7},{7,6},{8,9},{9,8},{10,11... | collective-permute-start | bytes 98312 | tf_op jit(solution)/shard_map/ppermute | solution.py:18
